TPU v7x, 128 devices: a whole 4x4x4 slice. The times are simulated.
128 devices in a mesh: gx: 4 (over y), gy: 8 (over z, x_lo), gz: 4 (over x_hi, core).
Axes of the slice: x: 4 (x_hi: 2, x_lo: 2; x = x_hi * 2 + x_lo), y: 4, z: 4, core: 2. Of those that a mesh axis runs over, the one named last changes fastest.
Arguments:
- node_latent: bfloat16 [64, 256, 16, 128], P('gx', 'gy', 'gz'), may hold values from -6 to 6
- edge_latent: bfloat16 [4, 8, 4, 12288, 128], P('gx', 'gy', 'gz'), may hold values from -6 to 6
- senders: int32 [4, 8, 4, 12288], P('gx', 'gy', 'gz'), may hold values from 7 to 3664, as said below
- receivers: int32 [4, 8, 4, 12288], P('gx', 'gy', 'gz'), may hold values from 0 to 2047, as said below
- w1_edge: bfloat16 [384, 128], replicated, may hold values from -0.3125 to 0.3125
- b1_edge: float32 [128], replicated, may hold values from -3 to 3
- w2_edge: bfloat16 [128, 128], replicated, may hold values from -0.5 to 0.5
- b2_edge: float32 [128], replicated, may hold values from -3 to 3
- w1_node: bfloat16 [256, 128], replicated, may hold values from -0.375 to 0.375
- b1_node: float32 [128], replicated, may hold values from -3 to 3
- w2_node: bfloat16 [128, 128], replicated, may hold values from -0.5 to 0.5
- cot_node: bfloat16 [64, 256, 16, 128], P('gx', 'gy', 'gz'), may hold values from -6 to 6
- cot_edge: bfloat16 [4, 8, 4, 12288, 128], P('gx', 'gy', 'gz'), may hold values from -8 to 8
Outputs:
- grad_node: bfloat16 [64, 256, 16, 128], P('gx', 'gy', 'gz')
- grad_edge: bfloat16 [4, 8, 4, 12288, 128], P('gx', 'gy', 'gz')
- grad_w1_edge: float32 [384, 128], replicated
- grad_w2_edge: float32 [128, 128], replicated
- grad_w1_node: float32 [256, 128], replicated
- grad_w2_node: float32 [128, 128], replicated
- grad_biases: float32 [4, 128], replicated
Inputs may be any that keep to these rules, and one draw needn't show every extreme that they name: `receivers`: in every block the list is nondecreasing; entry (i * 32 + j) * 4 + l names the block's cell at local coordinates (i, j, l). `senders`: entry (p * 34 + q) * 6 + r names the cell at local coordinates (p - 1, q - 1, r - 1) of the block extended by one cell on every side, the extension being cells of the adjacent blocks around the periodic box; it is always one of the six face neighbours of the same slot's receiver.
All inputs are finite; a program needn't handle non-finite values.
Results may differ from a plain program's by a relative error of at most 0.01.
Values may be sent and summed in bfloat16 or wider, within the bound.
A program may use at most 128 MiB of HBM per device.

v0:
```python
import jax
import jax.numpy as jnp
from jax import lax
from jax.sharding import PartitionSpec as P


def with_halo(shard, sides, width):
    edges = {}
    for axis, dim in sides:
        peers, length = (lax.axis_size(axis), shard.shape[dim])
        up = [(i, (i + 1) % peers) for i in range(peers)]
        last = lax.slice_in_dim(shard, length - width, length, axis=dim)
        leading = lax.slice_in_dim(shard, 0, width, axis=dim)
        edges[dim] = (
            lax.ppermute(last, axis, up),
            lax.ppermute(leading, axis, [(b, a) for a, b in up]),
        )
    done = []
    for _, dim in sides:
        low, high = edges[dim]
        around = [(width, width) if d in done else (0, 0) for d in range(shard.ndim)]
        shard = jnp.concatenate([jnp.pad(low, around), shard, jnp.pad(high, around)], axis=dim)
        done.append(dim)
    return shard


def transposed_dot(left, right):
    return lax.dot_general(
        left, right, (((0,), (0,)), ((), ())), preferred_element_type=jnp.float32
    )


def column_sums(values):
    return jnp.sum(values.astype(jnp.float32), axis=0)


def silu_slope(values):
    sigma = jax.nn.sigmoid(values)
    return sigma * (1.0 + values * (1.0 - sigma))


def reduce_flat(flat_grads):
    return lax.psum(flat_grads, ("gx", "gy", "gz"))


def on_device(
    node_latent,
    edge_latent,
    senders,
    receivers,
    w1_edge,
    b1_edge,
    w2_edge,
    b2_edge,
    w1_node,
    b1_node,
    w2_node,
    cot_node,
    cot_edge,
):
    side_x, side_y, side_z, latent = node_latent.shape
    cell_count = side_x * side_y * side_z
    edge_count = edge_latent.shape[3]
    padded = with_halo(node_latent, (("gx", 0), ("gy", 1), ("gz", 2)), 1)
    flat_pad = padded.reshape(-1, latent)
    own_rows = node_latent.reshape(cell_count, latent)
    edge_rows = edge_latent.reshape(edge_count, latent)
    cot_rows = cot_edge.reshape(edge_count, latent)
    cot_cells = cot_node.reshape(cell_count, latent)
    sender_ids = senders.reshape(edge_count)
    receiver_ids = receivers.reshape(edge_count)
    sender_rows = jnp.take(flat_pad, sender_ids, axis=0)
    receiver_rows = jnp.take(own_rows, receiver_ids, axis=0)
    x_edge = jnp.concatenate([edge_rows, sender_rows, receiver_rows], axis=1)
    z_edge = jnp.dot(x_edge, w1_edge, preferred_element_type=jnp.float32) + b1_edge
    u_edge = jax.nn.silu(z_edge).astype(jnp.bfloat16)
    edge_new = (
        edge_rows.astype(jnp.float32)
        + jnp.dot(u_edge, w2_edge, preferred_element_type=jnp.float32)
        + b2_edge
    ).astype(jnp.bfloat16)
    aggregate = jax.ops.segment_sum(
        edge_new.astype(jnp.float32), receiver_ids, cell_count, indices_are_sorted=True
    ).astype(jnp.bfloat16)
    x_node = jnp.concatenate([own_rows, aggregate], axis=1)
    z_node = jnp.dot(x_node, w1_node, preferred_element_type=jnp.float32) + b1_node
    u_node = jax.nn.silu(z_node).astype(jnp.bfloat16)
    dz_node = (
        jnp.dot(cot_cells, w2_node.T, preferred_element_type=jnp.float32) * silu_slope(z_node)
    ).astype(jnp.bfloat16)
    dx_node = jnp.dot(dz_node, w1_node.T, preferred_element_type=jnp.float32)
    node_flat = jnp.concatenate(
        [
            transposed_dot(x_node, dz_node).reshape(-1),
            column_sums(dz_node),
            transposed_dot(u_node, cot_cells).reshape(-1),
            column_sums(cot_cells),
        ]
    )
    d_edge = (
        cot_rows.astype(jnp.float32) + jnp.take(dx_node[:, latent:], receiver_ids, axis=0)
    ).astype(jnp.bfloat16)
    dz_edge = (
        jnp.dot(d_edge, w2_edge.T, preferred_element_type=jnp.float32) * silu_slope(z_edge)
    ).astype(jnp.bfloat16)
    d_self = jnp.dot(dz_edge, w1_edge[:latent].T, preferred_element_type=jnp.float32)
    d_sender = jnp.dot(dz_edge, w1_edge[latent : 2 * latent].T, preferred_element_type=jnp.float32)
    d_receiver = jnp.dot(dz_edge, w1_edge[2 * latent :].T, preferred_element_type=jnp.float32)
    grad_edge = (
        (d_edge.astype(jnp.float32) + d_self).astype(jnp.bfloat16).reshape(edge_latent.shape)
    )
    edge_flat = jnp.concatenate(
        [
            transposed_dot(x_edge, dz_edge).reshape(-1),
            column_sums(dz_edge),
            transposed_dot(u_edge, d_edge).reshape(-1),
            column_sums(d_edge),
        ]
    )
    summed = (reduce_flat(jnp.concatenate([node_flat, edge_flat])),)
    send_grid = jax.ops.segment_sum(d_sender, sender_ids, flat_pad.shape[0]).reshape(
        side_x + 2, side_y + 2, side_z + 2, latent
    )
    receiver_sum = jax.ops.segment_sum(
        d_receiver, receiver_ids, cell_count, indices_are_sorted=True
    )
    own_terms = cot_cells.astype(jnp.float32) + dx_node[:, :latent] + receiver_sum
    interior = send_grid[1:-1, 1:-1, 1:-1] + own_terms.reshape(side_x, side_y, side_z, latent)
    extended = with_halo(
        send_grid.astype(jnp.bfloat16), (("gx", 0), ("gy", 1), ("gz", 2)), 1
    ).astype(send_grid.dtype)
    interior = interior.at[0].add(extended[0, 2:-2, 2:-2]).at[-1].add(extended[-1, 2:-2, 2:-2])
    interior = (
        interior.at[:, 0].add(extended[2:-2, 0, 2:-2]).at[:, -1].add(extended[2:-2, -1, 2:-2])
    )
    interior = (
        interior.at[:, :, 0].add(extended[2:-2, 2:-2, 0]).at[:, :, -1].add(extended[2:-2, 2:-2, -1])
    )
    grad_node = interior.astype(jnp.bfloat16)
    param_count = 7 * latent * latent + 4 * latent
    partial_value = sum((jnp.sum(portion * portion) for portion in summed))
    factor = 1.0 / jnp.maximum(1.0, jnp.sqrt(partial_value / param_count))
    scaled = [portion * factor for portion in summed]
    full_grads = scaled[0]
    square = latent * latent
    cut_a = 2 * square
    cut_b = cut_a + latent
    cut_c = cut_b + square
    cut_d = cut_c + latent
    cut_e = cut_d + 3 * square
    cut_f = cut_e + latent
    cut_g = cut_f + square
    grad_w1_node = full_grads[:cut_a].reshape(2 * latent, latent)
    bias_one_node = full_grads[cut_a:cut_b]
    grad_w2_node = full_grads[cut_b:cut_c].reshape(latent, latent)
    bias_two_node = full_grads[cut_c:cut_d]
    grad_w1_edge = full_grads[cut_d:cut_e].reshape(3 * latent, latent)
    bias_one_edge = full_grads[cut_e:cut_f]
    grad_w2_edge = full_grads[cut_f:cut_g].reshape(latent, latent)
    bias_two_edge = full_grads[cut_g:]
    grad_biases = jnp.stack([bias_one_edge, bias_two_edge, bias_one_node, bias_two_node])
    return (
        grad_node,
        grad_edge,
        grad_w1_edge,
        grad_w2_edge,
        grad_w1_node,
        grad_w2_node,
        grad_biases,
    )


def solution(mesh):
    placed = (
        P("gx", "gy", "gz", None),
        P("gx", "gy", "gz", None, None),
        P("gx", "gy", "gz", None),
        P("gx", "gy", "gz", None),
        P(),
        P(),
        P(),
        P(),
        P(),
        P(),
        P(),
        P("gx", "gy", "gz", None),
        P("gx", "gy", "gz", None, None),
    )
    return jax.shard_map(
        on_device,
        mesh=mesh,
        in_specs=placed,
        out_specs=(
            P("gx", "gy", "gz", None),
            P("gx", "gy", "gz", None, None),
            P(),
            P(),
            P(),
            P(),
            P(),
        ),
        check_vma=False,
    )
```

profile of v0, /device:TPU:1, one launch (start us, length us, event | category | flops | bytes accessed | tf_op | source)
XLA Modules:
  0.0 521.9 jit_solution(16961521660698633385)
XLA Ops:
  10.2 3.6 collective-permute-start.4
  19.2 3.8 collective-permute-start
  28.0 43.3 %gather_fusion.1 = bf16[12288,128]{1,0:T(8,128)(2,1)} fusion(bf16[2048,128]{1,0:T(8,128)(2,1)S(1)} %bitcast.62, s32[12288]{0:T(1024)S(1)} %broadcast_clamp_fusion), kind=kCustom, calls=%fused_computation.1 | custom fusion | bytes 6340608 | tf_op jit(solution)/shard_map/jit(_take)/gather | solution.py:73
  73.8 43.7 %gather_fusion = bf16[12288,128]{1,0:T(8,128)(2,1)} fusion(bf16[3672,128]{1,0:T(8,128)(2,1)S(1)} %reshape.366, s32[12288]{0:T(1024)S(1)} %broadcast_clamp_fusion.1), kind=kCustom, calls=%fused_computation | custom fusion | bytes 6340608 | tf_op jit(solution)/shard_map/jit(_take)/gather | solution.py:72
  117.5 9.2 %broadcast_select_fusion = (bf16[12288,128]{1,0:T(8,128)(2,1)S(1)}, bf16[12288,128]{1,0:T(8,128)(2,1)S(1)}) fusion(bf16[12288,128]{1,0:T(8,128)(2,1)} %gather_fusion, pred[12288]{0:T(1024)(128)(4,1)S(1)} %compare_and_fusion, bf16[12288,128]{1,0:T(8,128)(2,1)} %gather_fusion.1, pred[12288]{0:T(1024)(128)(4,1)S(1)} %compare_and_fusion.1), kind=kLoop, calls=%fused_computation.38 | loop fusion | flops 3145728 | bytes 12607488 | tf_op jit(solution)/shard_map/jit(_take)/select_n | solution.py:72
  126.8 3.0 convolution_add_fusion.2
  132.5 3.8 fusion.4
  136.3 76.1 %scatter_custom_fusion = f32[2048,128]{1,0:T(8,128)S(1)} fusion(s32[12288]{0:T(1024)S(1)} %bitcast.69, f32[12288,128]{1,0:T(8,128)} %fusion.4, f32[]{:T(128)} %constant.207.clone.1), kind=kCustom, calls=%fused_computation.83 | custom fusion | flops 1572864 | bytes 1049088 | tf_op jit(solution)/shard_map/scatter-add | solution.py:82
  215.6 41.2 %gather_fusion.2 = f32[12288,128]{1,0:T(8,128)} fusion(f32[2048,128]{1,0:T(8,128)S(1)} %get-tuple-element.81, s32[12288]{0:T(1024)S(1)} %broadcast_clamp_fusion), kind=kCustom, calls=%fused_computation.2 | custom fusion | bytes 12632064 | tf_op jit(solution)/shard_map/jit(_take)/gather | solution.py:101
  256.8 9.3 %convert_reduce_fusion = (f32[128]{0:T(128)S(1)}, bf16[12288,128]{1,0:T(8,128)(2,1)S(1)}) fusion(f32[12288,128]{1,0:T(8,128)} %gather_fusion.2, pred[12288]{0:T(1024)(128)(4,1)S(1)} %compare_and_fusion.1, bf16[1,1,1,12288,128]{4,3,2,1,0:T(8,128)(2,1)} %param.37), kind=kLoop, calls=%fused_computation.17 | loop fusion | flops 9437056 | bytes 12595712 | tf_op jit(solution)/shard_map/reduce_sum | solution.py:34
  266.1 5.4 %convolution_bitcast_fusion.2 = f32[16384]{0:T(1024)} fusion(bf16[12288,128]{1,0:T(8,128)(2,1)S(1)} %get-tuple-element.80, f32[12288,128]{1,0:T(8,128)} %copy-done.25), kind=kOutput, calls=%fused_computation.63 | convolution fusion | flops 410517504 | bytes 9502720 | tf_op jit(solution)/shard_map/dot_general | solution.py:28
  271.6 3.2 convert_reduce_fusion.1
  275.3 3.3 convolution_bitcast_fusion
  281.3 3.6 fusion.47
  284.9 3.6 fusion.49
  288.5 66.6 %scatter_custom_fusion.1 = f32[3672,128]{1,0:T(8,128)S(1)} fusion(s32[12288]{0:T(1024)} %bitcast.74, f32[12288,128]{1,0:T(8,128)} %fusion.49, f32[]{:T(128)} %constant.207.clone.1), kind=kCustom, calls=%fused_computation.81 | custom fusion | flops 1572864 | bytes 1880576 | tf_op jit(solution)/shard_map/scatter-add | solution.py:121
  361.8 3.6 collective-permute-start.10
  368.1 4.4 collective-permute-start.6
  372.5 76.2 %scatter_fusion = f32[2048,128]{1,0:T(8,128)S(1)} fusion(f32[2048,128]{1,0:T(8,128)S(1)} %get-tuple-element.82, s32[12288]{0:T(1024)S(1)} %bitcast.70, f32[12288,128]{1,0:T(8,128)} %fusion.47), kind=kCustom, calls=%fused_computation.5 | custom fusion | flops 1572864 | bytes 18923520 | tf_op jit(solution)/shard_map/scatter-add | solution.py:124
  451.4 5.5 %collective-permute-done.11 = bf16[18,34,1,128]{3,2,1,0:T(2,128)(2,1)S(1)} collective-permute-done((bf16[18,34,1,128]{3,2,1,0:T(2,128)(2,1)}, bf16[18,34,1,128]{3,2,1,0:T(2,128)(2,1)S(1)}, u32[]{:S(2)}, u32[]{:S(2)}) %collective-permute-start.11) | collective-permute-done | bytes 156704 | tf_op jit(solution)/shard_map/ppermute | solution.py:16
  456.8 3.4 fusion.30
  462.2 5.3 %scatter-add.58 = f32[16,32,4,128]{3,2,1,0:T(4,128)S(1)} dynamic-update-slice(f32[16,32,4,128]{3,2,1,0:T(4,128)S(1)} %fusion.44, f32[16,32,1,128]{3,2,1,0:T(1,128)S(1)} %slice_add_fusion.3, s32[]{:T(128)} %constant.208.clone.1, s32[]{:T(128)} %constant.208.clone.1, s32[]{:T(128)} %constant.208.clone.1, s32[]{:T(128)} %constant.208.clone.1) | dynamic-update-slice | bytes 524292 | tf_op jit(solution)/shard_map/scatter-add | solution.py:137
  469.5 5.3 %scatter-add.59 = f32[16,32,4,128]{3,2,1,0:T(4,128)S(1)} dynamic-update-slice(f32[16,32,4,128]{3,2,1,0:T(4,128)S(1)} %scatter-add.58, f32[16,32,1,128]{3,2,1,0:T(1,128)S(1)} %slice_add_fusion.2, s32[]{:T(128)} %constant.208.clone.1, s32[]{:T(128)} %constant.208.clone.1, s32[]{:T(128)} %constant.219.clone.1, s32[]{:T(128)} %constant.208.clone.1) | dynamic-update-slice | bytes 524292 | tf_op jit(solution)/shard_map/scatter-add | solution.py:137
  475.8 33.1 %all-reduce.10.cloned.1.call-done = f32[115200]{0:T(1024)} async-done(((f32[115200]{0:T(1024)}), f32[115200]{0:T(1024)}) %all-reduce.10.cloned.1.call-update) | async-done | bytes 460816 | tf_op jit(solution)/shard_map/psum | solution.py:43
  (125 shorter events, 47.1 us)
Async XLA Ops:
  7.2 205.3 %copy-start = (bf16[256,128]{1,0:T(8,128)(2,1)S(1)}, bf16[256,128]{1,0:T(8,128)(2,1)}, u32[]{:S(2)}) copy-start(bf16[256,128]{1,0:T(8,128)(2,1)} %param.33) | copy-start | bytes 196612
  7.2 20.8 %copy-start.2 = (bf16[16,32,4,128]{3,2,1,0:T(4,128)(2,1)S(1)}, bf16[16,32,4,128]{3,2,1,0:T(4,128)(2,1)}, u32[]{:S(2)}) copy-start(bf16[16,32,4,128]{3,2,1,0:T(4,128)(2,1)} %param.25) | copy-start | bytes 1572868
  7.2 501.7 %all-reduce.10.cloned.1.call-start = ((), (), s32[]{:S(2)}) async-start(), calls=%async_computation | async-start | bytes 925696 | tf_op jit(solution)/shard_map/psum | solution.py:43
  8.1 18.3 %collective-permute-start.1 = (bf16[16,1,4,128]{3,2,1,0:T(4,128)(2,1)S(1)}, bf16[16,1,4,128]{3,2,1,0:T(4,128)(2,1)S(1)}, u32[]{:S(2)}, u32[]{:S(2)}) collective-permute-start(bf16[16,1,4,128]{3,2,1,0:T(4,128)(2,1)S(1)} %get-tuple-element.93), channel_id=1, source_target_pairs={{0,4},{4,8},{8,12},{12,16},{16,20},{20,24},{24,28},{28,0},{1,5},{5... | collective-permute-start | bytes 49160 | tf_op jit(solution)/shard_map/ppermute | solution.py:15
  10.2 61.2 %collective-permute-start.4 = (bf16[16,1,4,128]{3,2,1,0:T(4,128)(2,1)S(1)}, bf16[16,1,4,128]{3,2,1,0:T(4,128)(2,1)S(1)}, u32[]{:S(2)}, u32[]{:S(2)}) collective-permute-start(bf16[16,1,4,128]{3,2,1,0:T(4,128)(2,1)S(1)} %get-tuple-element.94), channel_id=1, source_target_pairs={{4,0},{8,4},{12,8},{16,12},{20,16},{24,20},{28,24},{0,28},{5,1},{9... | collective-permute-start | bytes 49160 | tf_op jit(solution)/shard_map/ppermute | solution.py:16
  14.5 56.8 %collective-permute-start.2 = (bf16[1,32,4,128]{3,2,1,0:T(4,128)(2,1)S(1)}, bf16[1,32,4,128]{3,2,1,0:T(4,128)(2,1)S(1)}, u32[]{:S(2)}, u32[]{:S(2)}) collective-permute-start(bf16[1,32,4,128]{3,2,1,0:T(4,128)(2,1)S(1)} %get-tuple-element.89), channel_id=1, source_target_pairs={{0,32},{32,64},{64,96},{96,0},{1,33},{33,65},{65,97},{97,1},{2,34}... | collective-permute-start | bytes 98312 | tf_op jit(solution)/shard_map/ppermute | solution.py:15
  15.9 55.5 %collective-permute-start.3 = (bf16[1,32,4,128]{3,2,1,0:T(4,128)(2,1)S(1)}, bf16[1,32,4,128]{3,2,1,0:T(4,128)(2,1)S(1)}, u32[]{:S(2)}, u32[]{:S(2)}) collective-permute-start(bf16[1,32,4,128]{3,2,1,0:T(4,128)(2,1)S(1)} %get-tuple-element.90), channel_id=1, source_target_pairs={{32,0},{64,32},{96,64},{0,96},{33,1},{65,33},{97,65},{1,97},{34,2}... | collective-permute-start | bytes 98312 | tf_op jit(solution)/shard_map/ppermute | solution.py:16
  19.2 52.2 %collective-permute-start = (bf16[16,32,1,128]{3,2,1,0:T(2,128)(2,1)S(1)}, bf16[16,32,1,128]{3,2,1,0:T(2,128)(2,1)S(1)}, u32[]{:S(2)}, u32[]{:S(2)}) collective-permute-start(bf16[16,32,1,128]{3,2,1,0:T(2,128)(2,1)S(1)} %get-tuple-element.91), channel_id=1, source_target_pairs={{0,1},{1,2},{2,3},{3,0},{4,5},{5,6},{6,7},{7,4},{8,9},{9,10},{10,1... | collective-permute-start | bytes 393224 | tf_op jit(solution)/shard_map/ppermute | solution.py:15
  26.3 45.0 %collective-permute-start.5 = (bf16[16,32,1,128]{3,2,1,0:T(2,128)(2,1)S(1)}, bf16[16,32,1,128]{3,2,1,0:T(2,128)(2,1)S(1)}, u32[]{:S(2)}, u32[]{:S(2)}) collective-permute-start(bf16[16,32,1,128]{3,2,1,0:T(2,128)(2,1)S(1)} %get-tuple-element.92), channel_id=1, source_target_pairs={{1,0},{2,1},{3,2},{0,3},{5,4},{6,5},{7,6},{4,7},{9,8},{10,9},{11,1... | collective-permute-start | bytes 393224 | tf_op jit(solution)/shard_map/ppermute | solution.py:16
  117.5 9.3 %copy-start.12 = (bf16[384,128]{1,0:T(8,128)(2,1)S(1)}, bf16[384,128]{1,0:T(8,128)(2,1)}, u32[]{:S(2)}) copy-start(bf16[384,128]{1,0:T(8,128)(2,1)} %param.29) | copy-start | bytes 294916
  117.5 9.3 %copy-start.17 = (bf16[1,1,1,12288,128]{4,3,2,1,0:T(8,128)(2,1)S(1)}, bf16[1,1,1,12288,128]{4,3,2,1,0:T(8,128)(2,1)}, u32[]{:S(2)}) copy-start(bf16[1,1,1,12288,128]{4,3,2,1,0:T(8,128)(2,1)} %param.26) | copy-start | bytes 9437188
  117.5 9.3 %copy-start.21 = (f32[128]{0:T(128)S(1)}, f32[128]{0:T(128)}, u32[]{:S(2)}) copy-start(f32[128]{0:T(128)} %param.30) | copy-start | bytes 1540
  126.8 5.7 %copy-start.20 = (bf16[128,128]{1,0:T(8,128)(2,1)S(1)}, bf16[128,128]{1,0:T(8,128)(2,1)}, u32[]{:S(2)}) copy-start(bf16[128,128]{1,0:T(8,128)(2,1)} %param.31) | copy-start | bytes 98308
  132.5 80.0 %copy-start.23 = (f32[128]{0:T(128)S(1)}, f32[128]{0:T(128)}, u32[]{:S(2)}) copy-start(f32[128]{0:T(128)} %param.34) | copy-start | bytes 1540
  136.3 76.6 %copy-start.8 = (bf16[16,32,4,128]{3,2,1,0:T(4,128)(2,1)S(1)}, bf16[16,32,4,128]{3,2,1,0:T(4,128)(2,1)}, u32[]{:S(2)}) copy-start(bf16[16,32,4,128]{3,2,1,0:T(4,128)(2,1)} %param.36) | copy-start | bytes 1572868
  256.8 14.7 %slice-start = ((s8[6291456]{0:T(1024)(128)(4,1)}), s8[4194304]{0:T(1024)(128)(4,1)S(1)}, s32[]{:S(2)}) async-start(s8[6291456]{0:T(1024)(128)(4,1)} %bitcast.77), calls=%async_computation.1 | async-start | bytes 8388608
  360.8 87.9 %collective-permute-start.7 = (bf16[18,1,6,128]{3,2,1,0:T(8,128)(2,1)S(1)}, bf16[18,1,6,128]{3,2,1,0:T(8,128)(2,1)S(1)}, u32[]{:S(2)}, u32[]{:S(2)}) collective-permute-start(bf16[18,1,6,128]{3,2,1,0:T(8,128)(2,1)S(1)} %get-tuple-element.87), channel_id=1, source_target_pairs={{0,4},{4,8},{8,12},{12,16},{16,20},{20,24},{24,28},{28,0},{1,5},{5... | collective-permute-start | bytes 82952 | tf_op jit(solution)/shard_map/ppermute | solution.py:15
  361.8 89.5 %collective-permute-start.10 = (bf16[18,1,6,128]{3,2,1,0:T(8,128)(2,1)S(1)}, bf16[18,1,6,128]{3,2,1,0:T(8,128)(2,1)S(1)}, u32[]{:S(2)}, u32[]{:S(2)}) collective-permute-start(bf16[18,1,6,128]{3,2,1,0:T(8,128)(2,1)S(1)} %get-tuple-element.88), channel_id=1, source_target_pairs={{4,0},{8,4},{12,8},{16,12},{20,16},{24,20},{28,24},{0,28},{5,1},{9... | collective-permute-start | bytes 82952 | tf_op jit(solution)/shard_map/ppermute | solution.py:16
  365.4 85.9 %collective-permute-start.8 = (bf16[1,34,6,128]{3,2,1,0:T(8,128)(2,1)}, bf16[1,34,6,128]{3,2,1,0:T(8,128)(2,1)}, u32[]{:S(2)}, u32[]{:S(2)}) collective-permute-start(bf16[1,34,6,128]{3,2,1,0:T(8,128)(2,1)} %get-tuple-element.83), channel_id=1, source_target_pairs={{0,32},{32,64},{64,96},{96,0},{1,33},{33,65},{65,97},{97,1},{2,34}... | collective-permute-start | bytes 156680 | tf_op jit(solution)/shard_map/ppermute | solution.py:15
  365.5 85.8 %collective-permute-start.9 = (bf16[1,34,6,128]{3,2,1,0:T(8,128)(2,1)}, bf16[1,34,6,128]{3,2,1,0:T(8,128)(2,1)}, u32[]{:S(2)}, u32[]{:S(2)}) collective-permute-start(bf16[1,34,6,128]{3,2,1,0:T(8,128)(2,1)} %get-tuple-element.84), channel_id=1, source_target_pairs={{32,0},{64,32},{96,64},{0,96},{33,1},{65,33},{97,65},{1,97},{34,2}... | collective-permute-start | bytes 156680 | tf_op jit(solution)/shard_map/ppermute | solution.py:16
  368.1 83.2 %collective-permute-start.6 = (bf16[18,34,1,128]{3,2,1,0:T(2,128)(2,1)}, bf16[18,34,1,128]{3,2,1,0:T(2,128)(2,1)}, u32[]{:S(2)}, u32[]{:S(2)}) collective-permute-start(bf16[18,34,1,128]{3,2,1,0:T(2,128)(2,1)} %get-tuple-element.85), channel_id=1, source_target_pairs={{0,1},{1,2},{2,3},{3,0},{4,5},{5,6},{6,7},{7,4},{8,9},{9,10},{10,1... | collective-permute-start | bytes 470024 | tf_op jit(solution)/shard_map/ppermute | solution.py:15
  448.7 8.1 %collective-permute-start.11 = (bf16[18,34,1,128]{3,2,1,0:T(2,128)(2,1)}, bf16[18,34,1,128]{3,2,1,0:T(2,128)(2,1)S(1)}, u32[]{:S(2)}, u32[]{:S(2)}) collective-permute-start(bf16[18,34,1,128]{3,2,1,0:T(2,128)(2,1)} %get-tuple-element.86), channel_id=1, source_target_pairs={{1,0},{2,1},{3,2},{0,3},{5,4},{6,5},{7,6},{4,7},{9,8},{10,9},{11,1... | collective-permute-start | bytes 470024 | tf_op jit(solution)/shard_map/ppermute | solution.py:16
  449.3 7.5 %copy-start.16 = (bf16[18,1,6,128]{3,2,1,0:T(8,128)(2,1)S(1)}, bf16[18,1,6,128]{3,2,1,0:T(8,128)(2,1)}, u32[]{:S(2)}) copy-start(bf16[18,1,6,128]{3,2,1,0:T(8,128)(2,1)} %copy-done.15) | copy-start | bytes 82948
  460.3 54.7 %copy-start.1 = (bf16[256,128]{1,0:T(8,128)(2,1)S(1)}, bf16[256,128]{1,0:T(8,128)(2,1)}, u32[]{:S(2)}) copy-start(bf16[256,128]{1,0:T(8,128)(2,1)} %param.33) | copy-start | bytes 196612
  (17 other events, 54.6 us)
Sparse Core Ops, SparseCore 0:
  361.9 146.9 all-reduce.9
where the time goes:
time: 523 us; the launch traced here: 522 us
  other arithmetic  259 us (50%)
  local copies, waits for them, and re-layouts  154 us (29%)
  waiting for transfers between devices  38.6 us (7%)
  matrix products  31.6 us (6%)
  starting transfers between devices  23.2 us (4%)
  between operations  15.3 us (3%)
    scatter-add x1, other arithmetic, on_device(): jax.ops.segment_sum(d_receiver, receiver_ids, cell_count, indices_are_sor...  76.2 us
    scatter-add x1, other arithmetic, on_device(): jax.ops.segment_sum(edge_new.astype(jnp.float32), receiver_ids, cell_coun...  76.1 us
    scatter-add x1, other arithmetic, on_device(): jax.ops.segment_sum(d_sender, sender_ids, flat_pad.shape[0])  66.6 us
    gather x1, local copies, waits for them, and re-layouts, on_device(): sender_rows = jnp.take(flat_pad, sender_ids, axis=0)  43.7 us
    gather x1, local copies, waits for them, and re-layouts, on_device(): receiver_rows = jnp.take(own_rows, receiver_ids, axis=0)  43.3 us
    gather x1, local copies, waits for them, and re-layouts, on_device(): jnp.take(dx_node[:, latent:], receiver_ids, axis=0)  41.2 us
    psum x1, waiting for transfers between devices, reduce_flat(): return lax.psum(flat_grads, ('gx', 'gy', 'gz'))  33.1 us
    ppermute x6, starting transfers between devices, with_halo(): lax.ppermute(last, axis, up)  11.7 us
  transfers between devices with their start and end apart: 13, of which 2 were waited for; matrix products, arithmetic and copies ran while one was open for 28% of the time, Pallas kernels for 0%

commit v1 on v0

v1 whole, which is shorter than its diff:
```python
import functools

import jax
import jax.numpy as jnp
from jax import lax
from jax.experimental import pallas as pl
from jax.experimental.pallas import tpu as pltpu
from jax.sharding import PartitionSpec as P

H = 128
PLANES = 16
ROWS = 128
CELLS = PLANES * ROWS
EDGES = 12288
TILE = 896
PADDED = EDGES + TILE
CHUNK = 512
RAW_ROWS = 904

F32 = jnp.float32
BF16 = jnp.bfloat16


def dot(a, b):
    return jnp.dot(a, b, preferred_element_type=F32)


def dot_tn(a, b):
    return lax.dot_general(a, b, (((0,), (0,)), ((), ())), preferred_element_type=F32)


def pair_dot(rows, diagonal):
    half = rows.shape[0] // 2
    both = dot(jnp.concatenate([rows[:half], rows[half:]], axis=1), diagonal)
    return jnp.concatenate([both[:, :H], both[:, H:]], axis=0)


def block_diagonal(w):
    zero = jnp.zeros_like(w)
    return jnp.concatenate(
        [jnp.concatenate([w, zero], axis=1), jnp.concatenate([zero, w], axis=1)], axis=0
    )


def slope_and_value(z):
    sigma = 0.5 * jnp.tanh(0.5 * z) + 0.5
    value = z * sigma
    return value, sigma * (1.0 + (z - value))


def local_kernel(
    bounds,
    send_ref,
    recv_ref,
    edge_hbm,
    cot_edge_hbm,
    node_ref,
    cot_node_ref,
    face_x_ref,
    face_y_ref,
    face_z_ref,
    w1e_ref,
    b1e_ref,
    w2e_ref,
    b2e_ref,
    w1n_ref,
    b1n_ref,
    w2n_ref,
    grad_edge_hbm,
    base_ref,
    out_x_ref,
    out_y_ref,
    out_z_ref,
    raw_ref,
    edge,
    cot,
    value,
    slope,
    grad,
    code_col,
    code_row,
    proj,
    proj_own,
    gathered,
    degree,
    table,
    sums,
    diag_w1,
    diag_w2t,
    diag_w1t,
    sems,
):
    copies = [
        pltpu.make_async_copy(edge_hbm, edge.at[pl.ds(0, EDGES), :], sems.at[0]),
        pltpu.make_async_copy(cot_edge_hbm, cot.at[pl.ds(0, EDGES), :], sems.at[1]),
    ]
    for item in copies:
        item.start()

    tail = jnp.zeros((TILE, H), BF16)
    edge[EDGES:, :] = tail
    cot[EDGES:, :] = tail

    recv = recv_ref[...]
    step = send_ref[...] - (
        ((recv >> 7) + 1) * 204 + (((recv >> 2) & 31) + 1) * 6 + (recv & 3) + 1
    )
    size = jnp.abs(step)
    axis = jnp.where(size == 204, 0, jnp.where(size == 6, 1, 2))
    key = (recv >> 7) * 256 + jnp.where(step < 0, 128, 0) + (recv & 127)
    code = key * 4 + axis
    code_row[0:96, :] = code
    code_row[96:, :] = jnp.full((code_row.shape[0] - 96, 128), -4, jnp.int32)
    turned = jnp.concatenate([code.astype(F32), jnp.zeros((32, 128), F32)], axis=0).T.astype(
        jnp.int32
    )
    for k in range(96):
        code_col[k * 128 : (k + 1) * 128, :] = jnp.broadcast_to(turned[:, k : k + 1], (128, 128))
    code_col[EDGES:, :] = jnp.full((TILE, 128), -4, jnp.int32)

    w1a = w1e_ref[0:H, :]
    w1b = w1e_ref[H : 2 * H, :]
    w1c = w1e_ref[2 * H :, :]
    diag_w1[...] = block_diagonal(w1a)
    diag_w2t[...] = block_diagonal(w2e_ref[...].T)
    diag_w1t[...] = block_diagonal(w1a.T)
    b1e = b1e_ref[...]

    proj[0:ROWS, :] = dot(face_x_ref[0], w1b)
    proj[ROWS * (PLANES + 1) :, :] = dot(face_x_ref[1], w1b)
    w1bc = jnp.concatenate([w1b, w1c], axis=1)

    def project(k, carry):
        rows = pl.ds(pl.multiple_of(k * CHUNK, CHUNK), CHUNK)
        both = dot(node_ref[rows, :], w1bc)
        proj[pl.ds(pl.multiple_of(k * CHUNK + ROWS, ROWS), CHUNK), :] = both[:, :H]
        proj_own[rows, :] = both[:, H:] + b1e
        return carry

    lax.fori_loop(0, CELLS // CHUNK, project, 0)

    row_id = lax.broadcasted_iota(jnp.int32, (ROWS, H), 0)
    low_z = (row_id & 3) == 0
    high_z = (row_id & 3) == 3
    low_y = row_id < 4
    high_y = row_id >= 124

    def first_row(i):
        return (bounds[i] >> 4) << 4

    def tiles_of(i):
        lo, hi = bounds[i], bounds[i + 1]
        count = (hi - first_row(i) + (TILE - 1)) // TILE
        return jnp.where(hi > lo, count, 0)

    def column_codes(start, i):
        codes = code_col[pl.ds(start, TILE), :]
        return codes & 3, (codes >> 2) - 256 * i

    def one_hot(keys):
        lane = lax.broadcasted_iota(jnp.int32, (TILE, 128), 1)
        low = jnp.where(keys == lane, 1.0, 0.0)
        high = jnp.where(keys == lane + 128, 1.0, 0.0)
        return jnp.concatenate([low, high], axis=1).astype(BF16)

    def one_hot_turned(start, i):
        q = start >> 7
        off = start & 127
        turn = (128 - off) & 127
        here = pltpu.roll(code_row[pl.ds(q, 8), :], turn, 1)
        there = pltpu.roll(code_row[pl.ds(q + 1, 8), :], turn, 1)
        lane = lax.broadcasted_iota(jnp.int32, (8, 128), 1)
        keys = (jnp.where(lane < 128 - off, here, there) >> 2) - 256 * i
        slot = lax.broadcasted_iota(jnp.int32, (256, 128), 0)
        pieces = [
            jnp.where(jnp.broadcast_to(keys[k : k + 1, :], (256, 128)) == slot, 1.0, 0.0)
            for k in range(TILE // 128)
        ]
        return pieces

    def keep_head(ref, start, new, inside):
        old = ref[pl.ds(start, 16), :].astype(F32)
        return jnp.concatenate([jnp.where(inside[:16], new[:16], old), new[16:]], axis=0)

    copies[0].wait()

    def forward_plane(i, carry):
        rows = pl.ds(pl.multiple_of(i * ROWS, ROWS), ROWS)
        own = proj_own[rows, :]
        mine = proj[pl.ds(pl.multiple_of((i + 1) * ROWS, ROWS), ROWS), :]
        above = proj[pl.ds(pl.multiple_of((i + 2) * ROWS, ROWS), ROWS), :]
        below = proj[rows, :]
        side_y = dot(face_y_ref[rows, :], w1e_ref[H : 2 * H, :])
        side_z = dot(face_z_ref[rows, :], w1e_ref[H : 2 * H, :])
        up_y = jnp.where(high_y, side_y, pltpu.roll(mine, 124, 0))
        down_y = jnp.where(low_y, side_y, pltpu.roll(mine, 4, 0))
        up_z = jnp.where(high_z, side_z, pltpu.roll(mine, 127, 0))
        down_z = jnp.where(low_z, side_z, pltpu.roll(mine, 1, 0))
        table[0:ROWS, :] = jnp.concatenate([above + own, up_y + own, up_z + own], axis=1).astype(
            BF16
        )
        table[ROWS:, :] = jnp.concatenate(
            [below + own, down_y + own, down_z + own], axis=1
        ).astype(BF16)
        gathered[rows, :] = jnp.zeros((ROWS, 2 * H), F32)
        degree[rows, :] = jnp.zeros((ROWS, H), F32)

        def tile(t, inner):
            start = pl.multiple_of(first_row(i) + t * TILE, 16)
            span = pl.ds(start, TILE)
            axis, keys = column_codes(start, i)
            picked = dot(one_hot(keys), table[...])
            latent = edge[span, :]
            z = pair_dot(latent, diag_w1[...]) + jnp.where(
                axis == 0,
                picked[:, :H],
                jnp.where(axis == 1, picked[:, H : 2 * H], picked[:, 2 * H :]),
            )
            u, sp = slope_and_value(z)
            inside = (keys >= 0) & (keys < 256)
            value[span, :] = keep_head(value, start, u, inside).astype(BF16)
            slope[span, :] = keep_head(slope, start, sp, inside).astype(BF16)
            pieces = one_hot_turned(start, i)
            spread = jnp.concatenate(pieces, axis=1)
            spread = (spread[:ROWS] + spread[ROWS:]).astype(BF16)
            gathered[rows, :] += dot(spread, jnp.concatenate([latent, u.astype(BF16)], axis=1))
            count = pieces[0]
            for piece in pieces[1:]:
                count = count + piece
            count = count[:ROWS] + count[ROWS:]
            degree[rows, :] += jnp.broadcast_to(
                jnp.sum(count, axis=1, keepdims=True), (ROWS, H)
            )
            return inner

        return lax.fori_loop(0, tiles_of(i), tile, carry)

    value[EDGES:, :] = tail
    slope[EDGES:, :] = tail
    lax.fori_loop(0, PLANES, forward_plane, 0)

    raw_ref[...] = jnp.zeros((RAW_ROWS, H), F32)
    w2nt = w2n_ref[...].T
    w1nt = w1n_ref[...].T

    def nodes(k, carry):
        rows = pl.ds(pl.multiple_of(k * CHUNK, CHUNK), CHUNK)
        packed = gathered[rows, :]
        aggregate = (
            packed[:, :H]
            + dot(packed[:, H:].astype(BF16), w2e_ref[...])
            + degree[rows, :] * b2e_ref[...]
        ).astype(BF16)
        x_node = jnp.concatenate([node_ref[rows, :], aggregate], axis=1)
        z_node = dot(x_node, w1n_ref[...]) + b1n_ref[...]
        u_node, sp_node = slope_and_value(z_node)
        cot_cells = cot_node_ref[rows, :]
        dz_node = (dot(cot_cells, w2nt) * sp_node).astype(BF16)
        dx_node = dot(dz_node, w1nt)
        base_ref[rows, :] = cot_cells.astype(F32) + dx_node[:, :H]
        gathered[rows, 0:H] = dx_node[:, H:]
        raw_ref[512:768, :] += dot_tn(x_node, dz_node)
        raw_ref[768:896, :] += dot_tn(u_node.astype(BF16), cot_cells)
        raw_ref[898:899, :] += jnp.sum(dz_node.astype(F32), axis=0, keepdims=True)
        raw_ref[899:900, :] += jnp.sum(cot_cells.astype(F32), axis=0, keepdims=True)
        return carry

    lax.fori_loop(0, CELLS // CHUNK, nodes, 0)
    copies[1].wait()

    def backward_plane(i, carry):
        rows = pl.ds(pl.multiple_of(i * ROWS, ROWS), ROWS)
        drow = gathered[rows, 0:H].astype(BF16)
        twice = jnp.concatenate([drow, drow], axis=0)
        sums[i + 1] = jnp.zeros((256, 3 * H), F32)

        def tile(t, inner):
            start = pl.multiple_of(first_row(i) + t * TILE, 16)
            span = pl.ds(start, TILE)
            axis, keys = column_codes(start, i)
            inside = (keys >= 0) & (keys < 256)
            added = dot(one_hot(keys), twice)
            d_wide = jnp.where(inside, cot[span, :].astype(F32) + added, 0.0)
            d_edge = d_wide.astype(BF16)
            dz = pair_dot(d_edge, diag_w2t[...]) * slope[span, :].astype(F32)
            dz_edge = dz.astype(BF16)
            new = d_edge.astype(F32) + pair_dot(dz_edge, diag_w1t[...])
            grad[span, :] = keep_head(grad, start, new, inside).astype(BF16)
            both = dot_tn(
                jnp.concatenate([edge[span, :], value[span, :]], axis=1),
                jnp.concatenate([dz_edge, d_edge], axis=1),
            )
            raw_ref[0:H, :] += both[:H, :H]
            raw_ref[384:512, :] += both[H:, H:]
            raw_ref[897:898, :] += jnp.sum(d_edge.astype(F32), axis=0, keepdims=True)
            spread = jnp.concatenate(one_hot_turned(start, i), axis=1).astype(BF16)
            parted = jnp.concatenate(
                [jnp.where(axis == a, dz, 0.0).astype(BF16) for a in range(3)], axis=1
            )
            sums[i + 1] += dot(spread, parted)
            return inner

        return lax.fori_loop(0, tiles_of(i), tile, carry)

    lax.fori_loop(0, PLANES, backward_plane, 0)
    grad_copy = pltpu.make_async_copy(grad.at[pl.ds(0, EDGES), :], grad_edge_hbm, sems.at[2])
    grad_copy.start()

    sums[0] = jnp.zeros((256, 3 * H), F32)
    sums[PLANES + 1] = jnp.zeros((256, 3 * H), F32)
    w1bt = w1e_ref[H : 2 * H, :].T
    w1ct = w1e_ref[2 * H :, :].T
    diag_w1[...] = block_diagonal(w1bt)
    diag_w2t[:, 0:H] = jnp.concatenate([w1bt, w1ct], axis=0)

    def cells(i, carry):
        rows = pl.ds(pl.multiple_of(i * ROWS, ROWS), ROWS)
        here = sums[i + 1]
        plus, minus = here[:ROWS], here[ROWS:]
        everything = plus + minus
        arrived = everything[:, :H] + everything[:, H : 2 * H] + everything[:, 2 * H :]
        yp, ym = plus[:, H : 2 * H], minus[:, H : 2 * H]
        zp, zm = plus[:, 2 * H :], minus[:, 2 * H :]
        left = (
            sums[i, 0:ROWS, 0:H]
            + sums[i + 2, ROWS : 2 * ROWS, 0:H]
            + jnp.where(low_y, 0.0, pltpu.roll(yp, 4, 0))
            + jnp.where(high_y, 0.0, pltpu.roll(ym, 124, 0))
            + jnp.where(low_z, 0.0, pltpu.roll(zp, 1, 0))
            + jnp.where(high_z, 0.0, pltpu.roll(zm, 127, 0))
        ).astype(BF16)
        arrived_low = arrived.astype(BF16)
        edge_y = jnp.where(high_y, yp, jnp.where(low_y, ym, 0.0)).astype(BF16)
        edge_z = jnp.where(high_z, zp, jnp.where(low_z, zm, 0.0)).astype(BF16)
        base_ref[rows, :] += dot(
            jnp.concatenate([left, arrived_low], axis=1), diag_w2t[:, 0:H]
        )
        outs = dot(jnp.concatenate([edge_y, edge_z], axis=1), diag_w1[...]).astype(BF16)
        out_y_ref[rows, :] = outs[:, :H]
        out_z_ref[rows, :] = outs[:, H:]
        cells_here = node_ref[rows, :]
        raw_ref[H : 2 * H, :] += dot_tn(
            jnp.concatenate([cells_here, face_y_ref[rows, :], face_z_ref[rows, :]], axis=0),
            jnp.concatenate([left, edge_y, edge_z], axis=0),
        )
        raw_ref[2 * H : 3 * H, :] += dot_tn(cells_here, arrived_low)
        raw_ref[896:897, :] += jnp.sum(arrived, axis=0, keepdims=True)
        return carry

    lax.fori_loop(0, PLANES, cells, 0)
    low_x = sums[1, ROWS : 2 * ROWS, 0:H].astype(BF16)
    high_x = sums[PLANES, 0:ROWS, 0:H].astype(BF16)
    out_x_ref[0] = dot(low_x, w1bt).astype(BF16)
    out_x_ref[1] = dot(high_x, w1bt).astype(BF16)
    raw_ref[H : 2 * H, :] += dot_tn(
        jnp.concatenate([face_x_ref[0], face_x_ref[1]], axis=0),
        jnp.concatenate([low_x, high_x], axis=0),
    )
    grad_copy.wait()


def local_terms(bounds, *operands):
    vmem = pl.BlockSpec(memory_space=pltpu.VMEM)
    anywhere = pl.BlockSpec(memory_space=pl.ANY)
    return pl.pallas_call(
        local_kernel,
        out_shape=(
            jax.ShapeDtypeStruct((EDGES, H), BF16),
            jax.ShapeDtypeStruct((CELLS, H), F32),
            jax.ShapeDtypeStruct((2, ROWS, H), BF16),
            jax.ShapeDtypeStruct((CELLS, H), BF16),
            jax.ShapeDtypeStruct((CELLS, H), BF16),
            jax.ShapeDtypeStruct((RAW_ROWS, H), F32),
        ),
        in_specs=[pl.BlockSpec(memory_space=pltpu.SMEM), vmem, vmem, anywhere, anywhere]
        + [vmem] * 12,
        out_specs=(anywhere, vmem, vmem, vmem, vmem, vmem),
        scratch_shapes=[
            pltpu.VMEM((PADDED, H), BF16),
            pltpu.VMEM((PADDED, H), BF16),
            pltpu.VMEM((PADDED, H), BF16),
            pltpu.VMEM((PADDED, H), BF16),
            pltpu.VMEM((PADDED, H), BF16),
            pltpu.VMEM((PADDED, 128), jnp.int32),
            pltpu.VMEM((112, 128), jnp.int32),
            pltpu.VMEM((CELLS + 2 * ROWS, H), F32),
            pltpu.VMEM((CELLS, H), F32),
            pltpu.VMEM((CELLS, 2 * H), F32),
            pltpu.VMEM((CELLS, H), F32),
            pltpu.VMEM((256, 3 * H), BF16),
            pltpu.VMEM((PLANES + 2, 256, 3 * H), F32),
            pltpu.VMEM((256, 256), BF16),
            pltpu.VMEM((256, 256), BF16),
            pltpu.VMEM((256, 256), BF16),
            pltpu.SemaphoreType.DMA((3,)),
        ],
        compiler_params=pltpu.CompilerParams(vmem_limit_bytes=62 * 1024 * 1024),
        cost_estimate=pl.CostEstimate(
            flops=10_000_000_000, bytes_accessed=20_000_000, transcendentals=2_000_000
        ),
    )(bounds, *operands)


def neighbours(axis, low, high):
    peers = lax.axis_size(axis)
    up = [(i, (i + 1) % peers) for i in range(peers)]
    down = [(b, a) for a, b in up]
    return lax.ppermute(high, axis, up), lax.ppermute(low, axis, down)


def on_device(
    node_latent,
    edge_latent,
    senders,
    receivers,
    w1_edge,
    b1_edge,
    w2_edge,
    b2_edge,
    w1_node,
    b1_node,
    w2_node,
    cot_node,
    cot_edge,
):
    side_x, side_y, side_z, latent = node_latent.shape
    x_low, x_high = neighbours("gx", node_latent[:1], node_latent[-1:])
    y_low, y_high = neighbours("gy", node_latent[:, :1], node_latent[:, -1:])
    z_low, z_high = neighbours("gz", node_latent[:, :, :1], node_latent[:, :, -1:])
    face_x = jnp.concatenate([x_low, x_high], axis=0).reshape(2, ROWS, latent)
    face_y = jnp.concatenate(
        [y_low, jnp.zeros((side_x, side_y - 2, side_z, latent), BF16), y_high], axis=1
    ).reshape(CELLS, latent)
    face_z = jnp.concatenate(
        [z_low, jnp.zeros((side_x, side_y, side_z - 2, latent), BF16), z_high], axis=2
    ).reshape(CELLS, latent)
    receiver_ids = receivers.reshape(96, 128)
    marks = jnp.arange(PLANES + 1, dtype=jnp.int32) * ROWS
    bounds = jnp.sum(
        (receivers.reshape(1, EDGES) < marks[:, None]).astype(jnp.int32), axis=1
    )
    grad_edge, base, out_x, out_y, out_z, raw = local_terms(
        bounds,
        senders.reshape(96, 128),
        receiver_ids,
        edge_latent.reshape(EDGES, latent),
        cot_edge.reshape(EDGES, latent),
        node_latent.reshape(CELLS, latent),
        cot_node.reshape(CELLS, latent),
        face_x,
        face_y,
        face_z,
        w1_edge,
        b1_edge.reshape(1, latent),
        w2_edge,
        b2_edge.reshape(1, latent),
        w1_node,
        b1_node.reshape(1, latent),
        w2_node,
    )
    total = lax.psum(raw, ("gx", "gy", "gz"))
    out_x = out_x.reshape(2, side_y, side_z, latent)
    out_y = out_y.reshape(side_x, side_y, side_z, latent)
    out_z = out_z.reshape(side_x, side_y, side_z, latent)
    from_low_x, from_high_x = neighbours("gx", out_x[:1], out_x[1:])
    from_low_y, from_high_y = neighbours("gy", out_y[:, :1], out_y[:, -1:])
    from_low_z, from_high_z = neighbours("gz", out_z[:, :, :1], out_z[:, :, -1:])
    interior = base.reshape(side_x, side_y, side_z, latent)
    interior = interior.at[:1].add(from_low_x.astype(F32)).at[-1:].add(from_high_x.astype(F32))
    interior = (
        interior.at[:, :1].add(from_low_y.astype(F32)).at[:, -1:].add(from_high_y.astype(F32))
    )
    interior = (
        interior.at[:, :, :1]
        .add(from_low_z.astype(F32))
        .at[:, :, -1:]
        .add(from_high_z.astype(F32))
    )
    grad_node = interior.astype(BF16)
    squares = jnp.sum(total * total)
    factor = 1.0 / jnp.maximum(1.0, jnp.sqrt(squares / (7 * latent * latent + 4 * latent)))
    scaled = total * factor
    return (
        grad_node,
        grad_edge.reshape(edge_latent.shape),
        scaled[:384],
        scaled[384:512],
        scaled[512:768],
        scaled[768:896],
        scaled[896:900],
    )


def solution(mesh):
    cell = P("gx", "gy", "gz", None)
    slots = P("gx", "gy", "gz", None, None)
    placed = (cell, slots, cell, cell, P(), P(), P(), P(), P(), P(), P(), cell, slots)
    return jax.shard_map(
        on_device,
        mesh=mesh,
        in_specs=placed,
        out_specs=(cell, slots, P(), P(), P(), P(), P()),
        check_vma=False,
    )
```

time: 523 us -> 241 us (0.46)
  other arithmetic: 259 us -> 17.9 us
  local copies, waits for them, and re-layouts: 154 us -> 25.4 us
  waiting for transfers between devices: 38.6 us -> 115 us
  Pallas kernels: 0 us -> 46.4 us
  matrix products: 31.6 us -> 0 us
    scatter-add x7 -> x4, other arithmetic: 219 us -> 4.89 us  [the longest x2 2.76 us: on_device(): interior.at[:, :1].add(from_low_y.astype(F32)).at[:, -1:]]
    gather x3 -> x0, local copies, waits for them, and re-layouts: 128 us -> none  [the longest x1 43.7 us: on_device(): sender_rows = jnp.take(flat_pad, sender_ids, axis=0)]
    psum x1, waiting for transfers between devices: 33.1 us -> 109 us  [on_device(): total = lax.psum(raw, ('gx', 'gy', 'gz'))]
    pallas_call x0 -> x1, Pallas kernels: none -> 46.4 us  [local_terms(): pl.pallas_call(local_kernel, out_shape=(jax.ShapeDtypeStruct((EDGES, H),...]
    dot_general x13 -> x0, matrix products: 31.6 us -> none  [the longest x4 10.3 us: transposed_dot(): lax.dot_general(left, right, (((0,), (0,)), ((), ())), preferred_element_...]
    select_n x3 -> x0, other arithmetic: 10.9 us -> none  [the longest x2 10.1 us: on_device(): sender_rows = jnp.take(flat_pad, sender_ids, axis=0)]
    reduce_sum x3 -> x2, other arithmetic: 12.6 us -> 3.36 us  [the longest x1 1.74 us: on_device(): squares = jnp.sum(total * total)]
    unnamed x62 -> x0, local copies, waits for them, and re-layouts: 6.06 us -> none
  transfers between devices with their start and end apart: 13 -> 13, of which waited for: 2 -> 3; matrix products, arithmetic and copies ran while one was open for 28% -> 14% of each run, Pallas kernels for 0% -> 0%
where the time goes in v1:
time: 241 us; the launch traced here: 240 us
  waiting for transfers between devices  115 us (48%)
  Pallas kernels  46.4 us (19%)
  local copies, waits for them, and re-layouts  25.4 us (11%)
  starting transfers between devices  19.8 us (8%)
  other arithmetic  17.9 us (7%)
  between operations  14.8 us (6%)
    psum x1, waiting for transfers between devices, on_device(): total = lax.psum(raw, ('gx', 'gy', 'gz'))  109 us
    pallas_call x1, Pallas kernels, local_terms(): pl.pallas_call(local_kernel, out_shape=(jax.ShapeDtypeStruct((EDGES, H),...  46.4 us
    ppermute x12, starting transfers between devices, neighbours(): return (lax.ppermute(high, axis, up), lax.ppermute(low, axis, down))  19.8 us
    scatter-add x2, local copies, waits for them, and re-layouts, on_device(): interior = interior.at[:, :, :1].add(from_low_z.astype(F32)).at[:, :, -1:...  15.1 us
    ppermute x12, waiting for transfers between devices, neighbours(): return (lax.ppermute(high, axis, up), lax.ppermute(low, axis, down))  5.71 us
  transfers between devices with their start and end apart: 13, of which 3 were waited for; matrix products, arithmetic and copies ran while one was open for 14% of the time, Pallas kernels for 0%

profile of v1, /device:TPU:1, one launch (start us, length us, event | category | flops | bytes accessed | tf_op | source)
XLA Modules:
  0.0 239.5 jit_solution(2144737016026204435)
XLA Ops:
  8.0 2.1 collective-permute-start.2
  10.1 3.6 %collective-permute-start.3 = (bf16[16,1,4,128]{3,2,1,0:T(4,128)(2,1)S(1)}, bf16[16,1,4,128]{3,2,1,0:T(4,128)(2,1)S(1)}, u32[]{:S(2)}, u32[]{:S(2)}) collective-permute-start(bf16[16,1,4,128]{3,2,1,0:T(4,128)(2,1)S(1)} %get-tuple-element.98), channel_id=1, source_target_pairs={{4,0},{8,4},{12,8},{16,12},{20,16},{24,20},{28,24},{0,28},{5,1},{9... | collective-permute-start | bytes 49160 | tf_op jit(solution)/shard_map/ppermute | solution.py:408
  14.4 1.4 collective-permute-start
  15.8 1.5 collective-permute-start.1
  17.3 1.9 fusion.5
  19.2 3.8 %collective-permute-start.4 = (bf16[16,32,1,128]{3,2,1,0:T(2,128)(2,1)S(1)}, bf16[16,32,1,128]{3,2,1,0:T(2,128)(2,1)S(1)}, u32[]{:S(2)}, u32[]{:S(2)}) collective-permute-start(bf16[16,32,1,128]{3,2,1,0:T(2,128)(2,1)S(1)} %get-tuple-element.95), channel_id=1, source_target_pairs={{0,1},{1,2},{2,3},{3,0},{4,5},{5,6},{6,7},{7,4},{8,9},{9,10},{10,1... | collective-permute-start | bytes 393224 | tf_op jit(solution)/shard_map/ppermute | solution.py:408
  23.0 1.6 convert_reduce_fusion.bounds
  26.5 5.6 %collective-permute-done.5 = bf16[16,32,1,128]{3,2,1,0:T(2,128)(2,1)S(1)} collective-permute-done((bf16[16,32,1,128]{3,2,1,0:T(2,128)(2,1)S(1)}, bf16[16,32,1,128]{3,2,1,0:T(2,128)(2,1)S(1)}, u32[]{:S(2)}, u32[]{:S(2)}) %collective-permute-start.5) | collective-permute-done | bytes 131104 | tf_op jit(solution)/shard_map/ppermute | solution.py:408
  32.1 1.4 pad_maximum_fusion.1
  33.5 46.4 %shard_map.180 = (bf16[12288,128]{1,0:T(8,128)(2,1)}, f32[2048,128]{1,0:T(8,128)}, bf16[2,128,128]{2,1,0:T(8,128)(2,1)}, bf16[2048,128]{1,0:T(8,128)(2,1)}, bf16...) custom-call(s32[17]{0:T(128)} %convert_reduce_fusion.bounds, s32[96,128]{1,0:T(8,128)} %bitcast.35, s32[96,128]{1,0:T(8,128)} %bitcast.28, ...), custom_call_target="tpu_custom_call" | custom-call | flops 10000000000 | bytes 20000000 | tf_op jit(solution)/shard_map/pallas_call | solution.py:365
  81.5 1.2 collective-permute-start.9
  83.1 2.6 %collective-permute-start.7 = (bf16[1,32,4,128]{3,2,1,0:T(4,128)(2,1)S(1)}, bf16[1,32,4,128]{3,2,1,0:T(4,128)(2,1)S(1)}, u32[]{:S(2)}, u32[]{:S(2)}) collective-permute-start(bf16[1,32,4,128]{3,2,1,0:T(4,128)(2,1)S(1)} %bitcast.29), channel_id=1, source_target_pairs={{32,0},{64,32},{96,64},{0,96},{33,1},{65,33},{97,65},{1,97},{34,2}... | collective-permute-start | bytes 98312 | tf_op jit(solution)/shard_map/ppermute | solution.py:408
  85.7 1.8 fusion.3
  88.4 3.2 %collective-permute-start.10 = (bf16[16,32,1,128]{3,2,1,0:T(2,128)(2,1)S(1)}, bf16[16,32,1,128]{3,2,1,0:T(2,128)(2,1)S(1)}, u32[]{:S(2)}, u32[]{:S(2)}) collective-permute-start(bf16[16,32,1,128]{3,2,1,0:T(2,128)(2,1)S(1)} %get-tuple-element.92), channel_id=1, source_target_pairs={{0,1},{1,2},{2,3},{3,0},{4,5},{5,6},{6,7},{7,4},{8,9},{9,10},{10,1... | collective-permute-start | bytes 393224 | tf_op jit(solution)/shard_map/ppermute | solution.py:408
  92.2 1.5 fusion
  93.7 1.4 fusion.2
  95.1 1.4 fusion.1
  96.6 1.6 slice_add_fusion.1
  98.2 7.5 %scatter-add.26 = f32[16,32,4,128]{3,2,1,0:T(4,128)} dynamic-update-slice(f32[16,32,4,128]{3,2,1,0:T(4,128)} %fusion.1, f32[16,32,1,128]{3,2,1,0:T(1,128)S(1)} %slice_add_fusion.1, s32[]{:T(128)} %constant.166.clone.1, s32[]{:T(128)} %constant.166.clone.1, s32[]{:T(128)} %constant.166.clone.1, s32[]{:T(128)} %constant.166.clone.1) | dynamic-update-slice | bytes 524292 | tf_op jit(solution)/shard_map/scatter-add | solution.py:475
  105.7 1.7 slice_add_fusion
  107.4 7.5 %scatter-add.29 = f32[16,32,4,128]{3,2,1,0:T(4,128)} dynamic-update-slice(f32[16,32,4,128]{3,2,1,0:T(4,128)} %scatter-add.26, f32[16,32,1,128]{3,2,1,0:T(1,128)S(1)} %slice_add_fusion, s32[]{:T(128)} %constant.166.clone.1, s32[]{:T(128)} %constant.166.clone.1, s32[]{:T(128)} %constant.170.clone.1, s32[]{:T(128)} %constant.166.clone.1) | dynamic-update-slice | bytes 524292 | tf_op jit(solution)/shard_map/scatter-add | solution.py:477
  115.0 2.2 convert_element_type.31
  117.2 109.4 %all-reduce.2.cloned.1.call-done = f32[904,128]{1,0:T(8,128)} async-done(((f32[904,128]{1,0:T(8,128)}), f32[904,128]{1,0:T(8,128)}) %all-reduce.2.cloned.1.call-update) | async-done | bytes 462864 | tf_op jit(solution)/shard_map/psum | solution.py:461
  226.6 1.7 multiply_reduce_fusion
  (35 shorter events, 10.8 us)
Async XLA Ops:
  7.2 219.4 %all-reduce.2.cloned.1.call-start = ((), (), s32[]{:S(2)}) async-start(), calls=%async_computation | async-start | bytes 925696 | tf_op jit(solution)/shard_map/psum | solution.py:461
  8.0 16.8 %collective-permute-start.2 = (bf16[16,1,4,128]{3,2,1,0:T(4,128)(2,1)S(1)}, bf16[16,1,4,128]{3,2,1,0:T(4,128)(2,1)S(1)}, u32[]{:S(2)}, u32[]{:S(2)}) collective-permute-start(bf16[16,1,4,128]{3,2,1,0:T(4,128)(2,1)S(1)} %get-tuple-element.97), channel_id=1, source_target_pairs={{0,4},{4,8},{8,12},{12,16},{16,20},{20,24},{24,28},{28,0},{1,5},{5... | collective-permute-start | bytes 49160 | tf_op jit(solution)/shard_map/ppermute | solution.py:408
  10.1 14.7 %collective-permute-start.3 = (bf16[16,1,4,128]{3,2,1,0:T(4,128)(2,1)S(1)}, bf16[16,1,4,128]{3,2,1,0:T(4,128)(2,1)S(1)}, u32[]{:S(2)}, u32[]{:S(2)}) collective-permute-start(bf16[16,1,4,128]{3,2,1,0:T(4,128)(2,1)S(1)} %get-tuple-element.98), channel_id=1, source_target_pairs={{4,0},{8,4},{12,8},{16,12},{20,16},{24,20},{28,24},{0,28},{5,1},{9... | collective-permute-start | bytes 49160 | tf_op jit(solution)/shard_map/ppermute | solution.py:408
  14.4 11.4 %collective-permute-start = (bf16[1,32,4,128]{3,2,1,0:T(4,128)(2,1)S(1)}, bf16[1,32,4,128]{3,2,1,0:T(4,128)(2,1)S(1)}, u32[]{:S(2)}, u32[]{:S(2)}) collective-permute-start(bf16[1,32,4,128]{3,2,1,0:T(4,128)(2,1)S(1)} %get-tuple-element.99), channel_id=1, source_target_pairs={{0,32},{32,64},{64,96},{96,0},{1,33},{33,65},{65,97},{97,1},{2,34}... | collective-permute-start | bytes 98312 | tf_op jit(solution)/shard_map/ppermute | solution.py:408
  15.8 10.0 %collective-permute-start.1 = (bf16[1,32,4,128]{3,2,1,0:T(4,128)(2,1)S(1)}, bf16[1,32,4,128]{3,2,1,0:T(4,128)(2,1)S(1)}, u32[]{:S(2)}, u32[]{:S(2)}) collective-permute-start(bf16[1,32,4,128]{3,2,1,0:T(4,128)(2,1)S(1)} %get-tuple-element.100), channel_id=1, source_target_pairs={{32,0},{64,32},{96,64},{0,96},{33,1},{65,33},{97,65},{1,97},{34,2}... | collective-permute-start | bytes 98312 | tf_op jit(solution)/shard_map/ppermute | solution.py:408
  19.2 7.3 %collective-permute-start.4 = (bf16[16,32,1,128]{3,2,1,0:T(2,128)(2,1)S(1)}, bf16[16,32,1,128]{3,2,1,0:T(2,128)(2,1)S(1)}, u32[]{:S(2)}, u32[]{:S(2)}) collective-permute-start(bf16[16,32,1,128]{3,2,1,0:T(2,128)(2,1)S(1)} %get-tuple-element.95), channel_id=1, source_target_pairs={{0,1},{1,2},{2,3},{3,0},{4,5},{5,6},{6,7},{7,4},{8,9},{9,10},{10,1... | collective-permute-start | bytes 393224 | tf_op jit(solution)/shard_map/ppermute | solution.py:408
  24.7 7.3 %collective-permute-start.5 = (bf16[16,32,1,128]{3,2,1,0:T(2,128)(2,1)S(1)}, bf16[16,32,1,128]{3,2,1,0:T(2,128)(2,1)S(1)}, u32[]{:S(2)}, u32[]{:S(2)}) collective-permute-start(bf16[16,32,1,128]{3,2,1,0:T(2,128)(2,1)S(1)} %get-tuple-element.96), channel_id=1, source_target_pairs={{1,0},{2,1},{3,2},{0,3},{5,4},{6,5},{7,6},{4,7},{9,8},{10,9},{11,1... | collective-permute-start | bytes 393224 | tf_op jit(solution)/shard_map/ppermute | solution.py:408
  81.5 13.6 %collective-permute-start.9 = (bf16[16,1,4,128]{3,2,1,0:T(4,128)(2,1)S(1)}, bf16[16,1,4,128]{3,2,1,0:T(4,128)(2,1)S(1)}, u32[]{:S(2)}, u32[]{:S(2)}) collective-permute-start(bf16[16,1,4,128]{3,2,1,0:T(4,128)(2,1)S(1)} %get-tuple-element.93), channel_id=1, source_target_pairs={{4,0},{8,4},{12,8},{16,12},{20,16},{24,20},{28,24},{0,28},{5,1},{9... | collective-permute-start | bytes 49160 | tf_op jit(solution)/shard_map/ppermute | solution.py:408
  82.7 11.1 %collective-permute-start.8 = (bf16[16,1,4,128]{3,2,1,0:T(4,128)(2,1)S(1)}, bf16[16,1,4,128]{3,2,1,0:T(4,128)(2,1)S(1)}, u32[]{:S(2)}, u32[]{:S(2)}) collective-permute-start(bf16[16,1,4,128]{3,2,1,0:T(4,128)(2,1)S(1)} %get-tuple-element.94), channel_id=1, source_target_pairs={{0,4},{4,8},{8,12},{12,16},{16,20},{20,24},{24,28},{28,0},{1,5},{5... | collective-permute-start | bytes 49160 | tf_op jit(solution)/shard_map/ppermute | solution.py:408
  83.0 5.3 %collective-permute-start.6 = (bf16[1,32,4,128]{3,2,1,0:T(4,128)(2,1)S(1)}, bf16[1,32,4,128]{3,2,1,0:T(4,128)(2,1)S(1)}, u32[]{:S(2)}, u32[]{:S(2)}) collective-permute-start(bf16[1,32,4,128]{3,2,1,0:T(4,128)(2,1)S(1)} %bitcast.30), channel_id=1, source_target_pairs={{0,32},{32,64},{64,96},{96,0},{1,33},{33,65},{65,97},{97,1},{2,34}... | collective-permute-start | bytes 98312 | tf_op jit(solution)/shard_map/ppermute | solution.py:408
  83.1 9.1 %collective-permute-start.7 = (bf16[1,32,4,128]{3,2,1,0:T(4,128)(2,1)S(1)}, bf16[1,32,4,128]{3,2,1,0:T(4,128)(2,1)S(1)}, u32[]{:S(2)}, u32[]{:S(2)}) collective-permute-start(bf16[1,32,4,128]{3,2,1,0:T(4,128)(2,1)S(1)} %bitcast.29), channel_id=1, source_target_pairs={{32,0},{64,32},{96,64},{0,96},{33,1},{65,33},{97,65},{1,97},{34,2}... | collective-permute-start | bytes 98312 | tf_op jit(solution)/shard_map/ppermute | solution.py:408
  88.3 17.4 %collective-permute-start.11 = (bf16[16,32,1,128]{3,2,1,0:T(2,128)(2,1)S(1)}, bf16[16,32,1,128]{3,2,1,0:T(2,128)(2,1)S(1)}, u32[]{:S(2)}, u32[]{:S(2)}) collective-permute-start(bf16[16,32,1,128]{3,2,1,0:T(2,128)(2,1)S(1)} %get-tuple-element.91), channel_id=1, source_target_pairs={{1,0},{2,1},{3,2},{0,3},{5,4},{6,5},{7,6},{4,7},{9,8},{10,9},{11,1... | collective-permute-start | bytes 393224 | tf_op jit(solution)/shard_map/ppermute | solution.py:408
  88.4 8.2 %collective-permute-start.10 = (bf16[16,32,1,128]{3,2,1,0:T(2,128)(2,1)S(1)}, bf16[16,32,1,128]{3,2,1,0:T(2,128)(2,1)S(1)}, u32[]{:S(2)}, u32[]{:S(2)}) collective-permute-start(bf16[16,32,1,128]{3,2,1,0:T(2,128)(2,1)S(1)} %get-tuple-element.92), channel_id=1, source_target_pairs={{0,1},{1,2},{2,3},{3,0},{4,5},{5,6},{6,7},{7,4},{8,9},{9,10},{10,1... | collective-permute-start | bytes 393224 | tf_op jit(solution)/shard_map/ppermute | solution.py:408
Sparse Core Ops, SparseCore 0:
  81.6 144.8 all-reduce.1

commit v2 on v1

--- a/solution.py
+++ b/solution.py
@@ -15,7 +15,10 @@
 TILE = 896
 PADDED = EDGES + TILE
 CHUNK = 512
-RAW_ROWS = 904
+RAW_ROWS = 1024
+X_LOW, X_HIGH, Y_LOW, Y_HIGH, Z_LOW, Z_HIGH, FACES = 0, 128, 256, 320, 384, 896, 1408
+SPANS = ((X_LOW, 128), (X_HIGH, 128), (Y_LOW, 64), (Y_HIGH, 64), (Z_LOW, 512), (Z_HIGH, 512))
+MESH = pl.DeviceIdType.MESH
 
 F32 = jnp.float32
 BF16 = jnp.bfloat16
@@ -56,9 +59,7 @@
     cot_edge_hbm,
     node_ref,
     cot_node_ref,
-    face_x_ref,
-    face_y_ref,
-    face_z_ref,
+    face_ref,
     w1e_ref,
     b1e_ref,
     w2e_ref,
@@ -68,9 +69,7 @@
     w2n_ref,
     grad_edge_hbm,
     base_ref,
-    out_x_ref,
-    out_y_ref,
-    out_z_ref,
+    out_ref,
     raw_ref,
     edge,
     cot,
@@ -81,6 +80,9 @@
     code_row,
     proj,
     proj_own,
+    proj_face,
+    wide,
+    leaving,
     gathered,
     degree,
     table,
@@ -126,8 +128,10 @@
     diag_w1t[...] = block_diagonal(w1a.T)
     b1e = b1e_ref[...]
 
-    proj[0:ROWS, :] = dot(face_x_ref[0], w1b)
-    proj[ROWS * (PLANES + 1) :, :] = dot(face_x_ref[1], w1b)
+    proj_face[...] = dot(face_ref[...], w1b)
+    proj[0:ROWS, :] = proj_face[X_LOW : X_LOW + ROWS, :]
+    proj[ROWS * (PLANES + 1) :, :] = proj_face[X_HIGH : X_HIGH + ROWS, :]
+    wide[...] = jnp.zeros((2 * ROWS, H), F32)
     w1bc = jnp.concatenate([w1b, w1c], axis=1)
 
     def project(k, carry):
@@ -190,8 +194,12 @@
         mine = proj[pl.ds(pl.multiple_of((i + 1) * ROWS, ROWS), ROWS), :]
         above = proj[pl.ds(pl.multiple_of((i + 2) * ROWS, ROWS), ROWS), :]
         below = proj[rows, :]
-        side_y = dot(face_y_ref[rows, :], w1e_ref[H : 2 * H, :])
-        side_z = dot(face_z_ref[rows, :], w1e_ref[H : 2 * H, :])
+        wide[0:4, :] = proj_face[pl.ds(Y_LOW + 4 * i, 4), :]
+        wide[124:128, :] = proj_face[pl.ds(Y_HIGH + 4 * i, 4), :]
+        wide[pl.ds(ROWS, 32, stride=4), :] = proj_face[pl.ds(Z_LOW + 32 * i, 32), :]
+        wide[pl.ds(ROWS + 3, 32, stride=4), :] = proj_face[pl.ds(Z_HIGH + 32 * i, 32), :]
+        side_y = wide[:ROWS, :]
+        side_z = wide[ROWS:, :]
         up_y = jnp.where(high_y, side_y, pltpu.roll(mine, 124, 0))
         down_y = jnp.where(low_y, side_y, pltpu.roll(mine, 4, 0))
         up_z = jnp.where(high_z, side_z, pltpu.roll(mine, 127, 0))
@@ -310,7 +318,6 @@
     sums[PLANES + 1] = jnp.zeros((256, 3 * H), F32)
     w1bt = w1e_ref[H : 2 * H, :].T
     w1ct = w1e_ref[2 * H :, :].T
-    diag_w1[...] = block_diagonal(w1bt)
     diag_w2t[:, 0:H] = jnp.concatenate([w1bt, w1ct], axis=0)
 
     def cells(i, carry):
@@ -330,32 +337,27 @@
             + jnp.where(high_z, 0.0, pltpu.roll(zm, 127, 0))
         ).astype(BF16)
         arrived_low = arrived.astype(BF16)
-        edge_y = jnp.where(high_y, yp, jnp.where(low_y, ym, 0.0)).astype(BF16)
-        edge_z = jnp.where(high_z, zp, jnp.where(low_z, zm, 0.0)).astype(BF16)
+        leaving[pl.ds(Y_LOW + 4 * i, 4), :] = ym[:4]
+        leaving[pl.ds(Y_HIGH + 4 * i, 4), :] = yp[124:]
+        wide[0:ROWS, :] = zm
+        wide[ROWS:, :] = zp
+        leaving[pl.ds(Z_LOW + 32 * i, 32), :] = wide[pl.ds(0, 32, stride=4), :]
+        leaving[pl.ds(Z_HIGH + 32 * i, 32), :] = wide[pl.ds(ROWS + 3, 32, stride=4), :]
         base_ref[rows, :] += dot(
             jnp.concatenate([left, arrived_low], axis=1), diag_w2t[:, 0:H]
         )
-        outs = dot(jnp.concatenate([edge_y, edge_z], axis=1), diag_w1[...]).astype(BF16)
-        out_y_ref[rows, :] = outs[:, :H]
-        out_z_ref[rows, :] = outs[:, H:]
         cells_here = node_ref[rows, :]
-        raw_ref[H : 2 * H, :] += dot_tn(
-            jnp.concatenate([cells_here, face_y_ref[rows, :], face_z_ref[rows, :]], axis=0),
-            jnp.concatenate([left, edge_y, edge_z], axis=0),
-        )
+        raw_ref[H : 2 * H, :] += dot_tn(cells_here, left)
         raw_ref[2 * H : 3 * H, :] += dot_tn(cells_here, arrived_low)
         raw_ref[896:897, :] += jnp.sum(arrived, axis=0, keepdims=True)
         return carry
 
     lax.fori_loop(0, PLANES, cells, 0)
-    low_x = sums[1, ROWS : 2 * ROWS, 0:H].astype(BF16)
-    high_x = sums[PLANES, 0:ROWS, 0:H].astype(BF16)
-    out_x_ref[0] = dot(low_x, w1bt).astype(BF16)
-    out_x_ref[1] = dot(high_x, w1bt).astype(BF16)
-    raw_ref[H : 2 * H, :] += dot_tn(
-        jnp.concatenate([face_x_ref[0], face_x_ref[1]], axis=0),
-        jnp.concatenate([low_x, high_x], axis=0),
-    )
+    leaving[X_LOW : X_LOW + ROWS, :] = sums[1, ROWS : 2 * ROWS, 0:H]
+    leaving[X_HIGH : X_HIGH + ROWS, :] = sums[PLANES, 0:ROWS, 0:H]
+    gone = leaving[...].astype(BF16)
+    out_ref[...] = dot(gone, w1bt).astype(BF16)
+    raw_ref[H : 2 * H, :] += dot_tn(face_ref[...], gone)
     grad_copy.wait()
 
 
@@ -367,14 +369,12 @@
         out_shape=(
             jax.ShapeDtypeStruct((EDGES, H), BF16),
             jax.ShapeDtypeStruct((CELLS, H), F32),
-            jax.ShapeDtypeStruct((2, ROWS, H), BF16),
-            jax.ShapeDtypeStruct((CELLS, H), BF16),
-            jax.ShapeDtypeStruct((CELLS, H), BF16),
+            jax.ShapeDtypeStruct((FACES, H), BF16),
             jax.ShapeDtypeStruct((RAW_ROWS, H), F32),
         ),
         in_specs=[pl.BlockSpec(memory_space=pltpu.SMEM), vmem, vmem, anywhere, anywhere]
-        + [vmem] * 12,
-        out_specs=(anywhere, vmem, vmem, vmem, vmem, vmem),
+        + [vmem] * 10,
+        out_specs=(anywhere, vmem, vmem, vmem),
         scratch_shapes=[
             pltpu.VMEM((PADDED, H), BF16),
             pltpu.VMEM((PADDED, H), BF16),
@@ -385,6 +385,9 @@
             pltpu.VMEM((112, 128), jnp.int32),
             pltpu.VMEM((CELLS + 2 * ROWS, H), F32),
             pltpu.VMEM((CELLS, H), F32),
+            pltpu.VMEM((FACES, H), F32),
+            pltpu.VMEM((2 * ROWS, H), F32),
+            pltpu.VMEM((FACES, H), F32),
             pltpu.VMEM((CELLS, 2 * H), F32),
             pltpu.VMEM((CELLS, H), F32),
             pltpu.VMEM((256, 3 * H), BF16),
@@ -401,11 +404,257 @@
     )(bounds, *operands)
 
 
-def neighbours(axis, low, high):
-    peers = lax.axis_size(axis)
-    up = [(i, (i + 1) % peers) for i in range(peers)]
-    down = [(b, a) for a, b in up]
-    return lax.ppermute(high, axis, up), lax.ppermute(low, axis, down)
+def place():
+    return tuple(lax.axis_index(name) for name in ("gx", "gy", "gz"))
+
+
+def sizes():
+    return tuple(lax.axis_size(name) for name in ("gx", "gy", "gz"))
+
+
+def across(side):
+    dim, up = side // 2, side % 2
+    here, count = place(), sizes()
+    beyond = list(here)
+    beyond[dim] = lax.rem(here[dim] + (1 if up else count[dim] - 1), count[dim])
+    return tuple(beyond)
+
+
+def face_copies(source, target, send_sems, recv_sems):
+    copies = []
+    for side, (first, rows) in enumerate(SPANS):
+        opposite = SPANS[side ^ 1][0]
+        copies.append(
+            pltpu.make_async_remote_copy(
+                src_ref=source.at[pl.ds(first, rows), :],
+                dst_ref=target.at[pl.ds(opposite, rows), :],
+                send_sem=send_sems.at[side],
+                recv_sem=recv_sems.at[side],
+                device_id=across(side),
+                device_id_type=MESH,
+            )
+        )
+    return copies
+
+
+def halo_kernel(node_ref, recv_ref, face_ref, bounds_ref, cells, packed, send_sems, recv_sems):
+    barrier = pltpu.get_barrier_semaphore()
+    for side in range(6):
+        pl.semaphore_signal(barrier, inc=1, device_id=across(side), device_id_type=MESH)
+    cells[...] = node_ref[...].astype(F32)
+    packed[X_LOW : X_LOW + ROWS, :] = node_ref[0:ROWS, :]
+    packed[X_HIGH : X_HIGH + ROWS, :] = node_ref[CELLS - ROWS :, :]
+    for first, at in ((Y_LOW, 0), (Y_HIGH, 124)):
+        strips = [cells[ROWS * i + at : ROWS * i + at + 4, :] for i in range(PLANES)]
+        packed[first : first + 64, :] = jnp.concatenate(strips, axis=0).astype(BF16)
+    packed[Z_LOW : Z_LOW + 512, :] = cells[pl.ds(0, 512, stride=4), :].astype(BF16)
+    packed[Z_HIGH : Z_HIGH + 512, :] = cells[pl.ds(3, 512, stride=4), :].astype(BF16)
+    pl.semaphore_wait(barrier, 6)
+    copies = face_copies(packed, face_ref, send_sems, recv_sems)
+    for side in (5, 4, 1, 0, 3, 2):
+        copies[side].start()
+    recv = recv_ref[...]
+    for i in range(PLANES + 1):
+        below = jnp.where(recv < ROWS * i, 1.0, 0.0)
+        bounds_ref[i] = jnp.sum(below).astype(jnp.int32)
+    for item in copies:
+        item.wait()
+
+
+def halo(node, recv):
+    vmem = pl.BlockSpec(memory_space=pltpu.VMEM)
+    return pl.pallas_call(
+        halo_kernel,
+        out_shape=(
+            jax.ShapeDtypeStruct((FACES, H), BF16),
+            jax.ShapeDtypeStruct((PLANES + 1,), jnp.int32),
+        ),
+        in_specs=[vmem, vmem],
+        out_specs=(vmem, pl.BlockSpec(memory_space=pltpu.SMEM)),
+        scratch_shapes=[
+            pltpu.VMEM((CELLS, H), F32),
+            pltpu.VMEM((FACES, H), BF16),
+            pltpu.SemaphoreType.DMA((6,)),
+            pltpu.SemaphoreType.DMA((6,)),
+        ],
+        compiler_params=pltpu.CompilerParams(
+            collective_id=0, has_side_effects=True, vmem_limit_bytes=16 * 1024 * 1024
+        ),
+    )(node, recv)
+
+
+def finish_kernel(
+    base_ref,
+    out_ref,
+    raw_ref,
+    grad_ref,
+    w1e_ref,
+    w2e_ref,
+    w1n_ref,
+    w2n_ref,
+    bias_ref,
+    faces,
+    cells,
+    partner_part,
+    half,
+    parts,
+    mine,
+    full,
+    send_sems,
+    recv_sems,
+    pair_send,
+    pair_recv,
+    all_send,
+    all_recv,
+):
+    (ga, gb, gc), (na, nb, nc) = place(), sizes()
+    nz = nc // 2
+    chips = na * nb * nz
+    chip_z, core = lax.div(gc, 2), lax.rem(gc, 2)
+    chip = (ga * nb + gb) * nz + chip_z
+    partner = (ga, gb, 2 * chip_z + 1 - core)
+
+    def peer(d):
+        da, rest = lax.div(d, nb * nz), lax.rem(d, nb * nz)
+        db, dz = lax.div(rest, nz), lax.rem(rest, nz)
+        pa, pb = lax.rem(ga + da, na), lax.rem(gb + db, nb)
+        pz = lax.rem(chip_z + dz, nz)
+        return (pa, pb, 2 * pz + core), (pa * nb + pb) * nz + pz
+
+    barrier = pltpu.get_barrier_semaphore()
+
+    def greet(d, carry):
+        pl.semaphore_signal(barrier, inc=1, device_id=peer(d)[0], device_id_type=MESH)
+        return carry
+
+    pl.semaphore_signal(barrier, inc=1, device_id=partner, device_id_type=MESH)
+    lax.fori_loop(1, chips, greet, 0)
+    for side in (4, 5):
+        pl.semaphore_signal(barrier, inc=1, device_id=across(side), device_id_type=MESH)
+    pl.semaphore_wait(barrier, chips + 2)
+
+    def to_partner(source, target, k):
+        return pltpu.make_async_remote_copy(
+            src_ref=source,
+            dst_ref=target,
+            send_sem=pair_send.at[k],
+            recv_sem=pair_recv.at[k],
+            device_id=partner,
+            device_id_type=MESH,
+        )
+
+    first = to_partner(raw_ref.at[pl.ds((1 - core) * chips, chips)], partner_part, 0)
+    first.start()
+    halos = face_copies(out_ref, faces, send_sems, recv_sems)
+    for side in (0, 1, 2, 3):
+        halos[side].start()
+    first.wait()
+    half[...] = raw_ref[pl.ds(core * chips, chips)] + partner_part[...]
+
+    def scatter(d, carry):
+        where, other = peer(d)
+        pltpu.make_async_remote_copy(
+            src_ref=half.at[other],
+            dst_ref=parts.at[chip],
+            send_sem=all_send.at[0],
+            recv_sem=all_recv.at[0],
+            device_id=where,
+            device_id_type=MESH,
+        ).start()
+        return carry
+
+    lax.fori_loop(1, chips, scatter, 0)
+    for side in (4, 5):
+        halos[side].start()
+    parts[chip] = half[chip]
+
+    def settle(buffer, sem):
+        span = buffer.at[pl.ds(0, chips - 1)]
+        pltpu.make_async_copy(span, span, sem).wait()
+
+    settle(parts, all_recv.at[0])
+    mine[...] = jnp.sum(parts[...], axis=0)
+
+    def gather(d, carry):
+        where, _ = peer(d)
+        pltpu.make_async_remote_copy(
+            src_ref=mine,
+            dst_ref=full.at[core * chips + chip],
+            send_sem=all_send.at[1],
+            recv_sem=all_recv.at[1],
+            device_id=where,
+            device_id_type=MESH,
+        ).start()
+        return carry
+
+    lax.fori_loop(1, chips, gather, 0)
+    full[core * chips + chip] = mine[...]
+    for item in halos:
+        item.wait()
+    cells[...] = base_ref[...]
+    cells[0:ROWS, :] += faces[X_LOW : X_LOW + ROWS, :].astype(F32)
+    cells[CELLS - ROWS :, :] += faces[X_HIGH : X_HIGH + ROWS, :].astype(F32)
+    for start, at in ((Y_LOW, 0), (Y_HIGH, 124)):
+        strip = faces[start : start + 64, :].astype(F32)
+        for i in range(PLANES):
+            cells[ROWS * i + at : ROWS * i + at + 4, :] += strip[4 * i : 4 * i + 4]
+    cells[pl.ds(0, 512, stride=4), :] += faces[Z_LOW : Z_LOW + 512, :].astype(F32)
+    cells[pl.ds(3, 512, stride=4), :] += faces[Z_HIGH : Z_HIGH + 512, :].astype(F32)
+    grad_ref[...] = cells[...].astype(BF16)
+    settle(full, all_recv.at[1])
+    held = pl.ds(core * chips, chips)
+    last = to_partner(full.at[held], full.at[held], 1)
+    last.start()
+    settle(half, all_send.at[0])
+    settle(half, all_send.at[1])
+    last.wait()
+    total = full[...].reshape(RAW_ROWS, H)
+    squares = jnp.sum(total * total, axis=0, keepdims=True)
+    squares = jnp.sum(squares, axis=1, keepdims=True)
+    factor = 1.0 / jnp.maximum(1.0, jnp.sqrt(squares / (7 * H * H + 4 * H)))
+    scaled = total * factor
+    w1e_ref[...] = scaled[:384]
+    w2e_ref[...] = scaled[384:512]
+    w1n_ref[...] = scaled[512:768]
+    w2n_ref[...] = scaled[768:896]
+    bias_ref[...] = scaled[896:900]
+
+
+def finish(base, out, raw):
+    chips = lax.axis_size("gx") * lax.axis_size("gy") * lax.axis_size("gz") // 2
+    block = RAW_ROWS // (2 * chips)
+    vmem = pl.BlockSpec(memory_space=pltpu.VMEM)
+    return pl.pallas_call(
+        finish_kernel,
+        out_shape=(
+            jax.ShapeDtypeStruct((CELLS, H), BF16),
+            jax.ShapeDtypeStruct((384, H), F32),
+            jax.ShapeDtypeStruct((128, H), F32),
+            jax.ShapeDtypeStruct((256, H), F32),
+            jax.ShapeDtypeStruct((128, H), F32),
+            jax.ShapeDtypeStruct((4, H), F32),
+        ),
+        in_specs=[vmem] * 3,
+        out_specs=(vmem,) * 6,
+        scratch_shapes=[
+            pltpu.VMEM((FACES, H), BF16),
+            pltpu.VMEM((CELLS, H), F32),
+            pltpu.VMEM((chips, block, H), F32),
+            pltpu.VMEM((chips, block, H), F32),
+            pltpu.VMEM((chips, block, H), F32),
+            pltpu.VMEM((block, H), F32),
+            pltpu.VMEM((2 * chips, block, H), F32),
+            pltpu.SemaphoreType.DMA((6,)),
+            pltpu.SemaphoreType.DMA((6,)),
+            pltpu.SemaphoreType.DMA((2,)),
+            pltpu.SemaphoreType.DMA((2,)),
+            pltpu.SemaphoreType.DMA((2,)),
+            pltpu.SemaphoreType.DMA((2,)),
+        ],
+        compiler_params=pltpu.CompilerParams(
+            collective_id=1, has_side_effects=True, vmem_limit_bytes=24 * 1024 * 1024
+        ),
+    )(base, out, raw.reshape(2 * chips, block, H))
 
 
 def on_device(
@@ -423,72 +672,28 @@
     cot_node,
     cot_edge,
 ):
-    side_x, side_y, side_z, latent = node_latent.shape
-    x_low, x_high = neighbours("gx", node_latent[:1], node_latent[-1:])
-    y_low, y_high = neighbours("gy", node_latent[:, :1], node_latent[:, -1:])
-    z_low, z_high = neighbours("gz", node_latent[:, :, :1], node_latent[:, :, -1:])
-    face_x = jnp.concatenate([x_low, x_high], axis=0).reshape(2, ROWS, latent)
-    face_y = jnp.concatenate(
-        [y_low, jnp.zeros((side_x, side_y - 2, side_z, latent), BF16), y_high], axis=1
-    ).reshape(CELLS, latent)
-    face_z = jnp.concatenate(
-        [z_low, jnp.zeros((side_x, side_y, side_z - 2, latent), BF16), z_high], axis=2
-    ).reshape(CELLS, latent)
+    cells = node_latent.reshape(CELLS, H)
     receiver_ids = receivers.reshape(96, 128)
-    marks = jnp.arange(PLANES + 1, dtype=jnp.int32) * ROWS
-    bounds = jnp.sum(
-        (receivers.reshape(1, EDGES) < marks[:, None]).astype(jnp.int32), axis=1
-    )
-    grad_edge, base, out_x, out_y, out_z, raw = local_terms(
+    faces, bounds = halo(cells, receiver_ids)
+    grad_edge, base, out, raw = local_terms(
         bounds,
         senders.reshape(96, 128),
         receiver_ids,
-        edge_latent.reshape(EDGES, latent),
-        cot_edge.reshape(EDGES, latent),
-        node_latent.reshape(CELLS, latent),
-        cot_node.reshape(CELLS, latent),
-        face_x,
-        face_y,
-        face_z,
+        edge_latent.reshape(EDGES, H),
+        cot_edge.reshape(EDGES, H),
+        cells,
+        cot_node.reshape(CELLS, H),
+        faces,
         w1_edge,
-        b1_edge.reshape(1, latent),
+        b1_edge.reshape(1, H),
         w2_edge,
-        b2_edge.reshape(1, latent),
+        b2_edge.reshape(1, H),
         w1_node,
-        b1_node.reshape(1, latent),
+        b1_node.reshape(1, H),
         w2_node,
     )
-    total = lax.psum(raw, ("gx", "gy", "gz"))
-    out_x = out_x.reshape(2, side_y, side_z, latent)
-    out_y = out_y.reshape(side_x, side_y, side_z, latent)
-    out_z = out_z.reshape(side_x, side_y, side_z, latent)
-    from_low_x, from_high_x = neighbours("gx", out_x[:1], out_x[1:])
-    from_low_y, from_high_y = neighbours("gy", out_y[:, :1], out_y[:, -1:])
-    from_low_z, from_high_z = neighbours("gz", out_z[:, :, :1], out_z[:, :, -1:])
-    interior = base.reshape(side_x, side_y, side_z, latent)
-    interior = interior.at[:1].add(from_low_x.astype(F32)).at[-1:].add(from_high_x.astype(F32))
-    interior = (
-        interior.at[:, :1].add(from_low_y.astype(F32)).at[:, -1:].add(from_high_y.astype(F32))
-    )
-    interior = (
-        interior.at[:, :, :1]
-        .add(from_low_z.astype(F32))
-        .at[:, :, -1:]
-        .add(from_high_z.astype(F32))
-    )
-    grad_node = interior.astype(BF16)
-    squares = jnp.sum(total * total)
-    factor = 1.0 / jnp.maximum(1.0, jnp.sqrt(squares / (7 * latent * latent + 4 * latent)))
-    scaled = total * factor
-    return (
-        grad_node,
-        grad_edge.reshape(edge_latent.shape),
-        scaled[:384],
-        scaled[384:512],
-        scaled[512:768],
-        scaled[768:896],
-        scaled[896:900],
-    )
+    grad_node, *grads = finish(base, out, raw)
+    return (grad_node.reshape(node_latent.shape), grad_edge.reshape(edge_latent.shape), *grads)
 
 
 def solution(mesh):

time: 241 us -> 94.9 us (0.39)
  waiting for transfers between devices: 115 us -> 0 us
  Pallas kernels: 46.4 us -> 83.6 us
  starting transfers between devices: 19.8 us -> 0 us
  other arithmetic: 17.9 us -> 0 us
  local copies, waits for them, and re-layouts: 25.4 us -> 10.3 us
  between operations: 14.8 us -> 0.69 us
    psum x1 -> x0, waiting for transfers between devices: 109 us -> none  [on_device(): total = lax.psum(raw, ('gx', 'gy', 'gz'))]
    pallas_call x0 -> x2, Pallas kernels: none -> 39.4 us  [the longest x1 26.7 us: finish(): pl.pallas_call(finish_kernel, out_shape=(jax.ShapeDtypeStruct((CELLS, H),...]
    ppermute x12 -> x0, starting transfers between devices: 19.8 us -> none  [neighbours(): return (lax.ppermute(high, axis, up), lax.ppermute(low, axis, down))]
    scatter-add x2 -> x0, local copies, waits for them, and re-layouts: 15.1 us -> none  [on_device(): interior = interior.at[:, :, :1].add(from_low_z.astype(F32)).at[:, :, -1:...]
    unnamed x0 -> x20, local copies, waits for them, and re-layouts: none -> 10.3 us
    slice x10 -> x0, local copies, waits for them, and re-layouts: 9.33 us -> none  [the longest x1 1.86 us: on_device(): node_latent[:, :, -1:]]
    ppermute x12 -> x0, waiting for transfers between devices: 5.71 us -> none  [neighbours(): return (lax.ppermute(high, axis, up), lax.ppermute(low, axis, down))]
    scatter-add x4 -> x0, other arithmetic: 4.89 us -> none  [the longest x2 2.76 us: on_device(): interior.at[:, :1].add(from_low_y.astype(F32)).at[:, -1:]]
  transfers between devices with their start and end apart: 13 -> 0, of which waited for: 3 -> 0; matrix products, arithmetic and copies ran while one was open for 14% -> 0% of each run, Pallas kernels for 0% -> 0%
where the time goes in v2:
time: 94.9 us; the launch traced here: 94.6 us
  Pallas kernels  83.6 us (88%)
  local copies, waits for them, and re-layouts  10.3 us (11%)
    pallas_call x1, Pallas kernels, local_terms(): pl.pallas_call(local_kernel, out_shape=(jax.ShapeDtypeStruct((EDGES, H),...  44.2 us
    pallas_call x1, Pallas kernels, finish(): pl.pallas_call(finish_kernel, out_shape=(jax.ShapeDtypeStruct((CELLS, H),...  26.7 us
    pallas_call x1, Pallas kernels, halo(): pl.pallas_call(halo_kernel, out_shape=(jax.ShapeDtypeStruct((FACES, H), B...  12.8 us
    unnamed x20, local copies, waits for them, and re-layouts  10.3 us

profile of v2, /device:TPU:1, one launch (start us, length us, event | category | flops | bytes accessed | tf_op | source)
XLA Modules:
  0.0 94.6 jit_solution(12753801756402222721)
XLA Ops:
  0.6 0.0 copy-start.1
  0.6 1.0 %copy-done.1 = bf16[16,32,4,128]{3,2,1,0:T(4,128)(2,1)S(1)} copy-done((bf16[16,32,4,128]{3,2,1,0:T(4,128)(2,1)S(1)}, bf16[16,32,4,128]{3,2,1,0:T(4,128)(2,1)}, u32[]{:S(2)}) %copy-start.1) | copy-done | bytes 524312
  1.7 0.0 copy-start.4
  1.7 0.8 copy-done.4
  2.5 12.8 %shard_map.180 = (bf16[1408,128]{1,0:T(8,128)(2,1)S(1)}, s32[17]{0:T(128)S(1)}) custom-call(bf16[2048,128]{1,0:T(8,128)(2,1)S(1)} %bitcast.13, s32[96,128]{1,0:T(8,128)S(1)} %bitcast.17), custom_call_target="tpu_custom_call" | custom-call | tf_op jit(solution)/shard_map/pallas_call | solution.py:466
  15.2 0.0 copy-start.5
  15.3 0.8 copy-done.5
  16.0 0.0 copy-start.6
  16.0 0.5 copy-done.6
  16.5 44.2 %shard_map.181 = (bf16[12288,128]{1,0:T(8,128)(2,1)}, f32[2048,128]{1,0:T(8,128)}, bf16[1408,128]{1,0:T(8,128)(2,1)}, f32[1024,128]{1,0:T(8,128)}) custom-call(s32[17]{0:T(128)} %copy-done.6, s32[96,128]{1,0:T(8,128)} %bitcast.21, s32[96,128]{1,0:T(8,128)} %bitcast.16, bf16[12288,128]{1,0:T(8,128)(2,1)} %bitcast.18, bf16[12288,128]{1,0:T(8,128)(2,1)} %bitcast.19, ...), custom_call_target="tpu_custom_call" | custom-call | flops 10000000000 | bytes 20000000 | tf_op jit(solution)/shard_map/pallas_call | solution.py:367
  60.7 0.0 copy-start
  60.7 1.2 %copy-done = f32[2048,128]{1,0:T(8,128)S(1)} copy-done((f32[2048,128]{1,0:T(8,128)S(1)}, f32[2048,128]{1,0:T(8,128)}, u32[]{:S(2)}) %copy-start) | copy-done | bytes 1048600
  61.9 0.0 copy-start.2
  61.9 1.0 %copy-done.2 = f32[1024,128]{1,0:T(8,128)S(1)} copy-done((f32[1024,128]{1,0:T(8,128)S(1)}, f32[1024,128]{1,0:T(8,128)}, u32[]{:S(2)}) %copy-start.2) | copy-done | bytes 524312
  63.0 0.0 copy-start.3
  63.0 1.0 %copy-done.3 = bf16[1408,128]{1,0:T(8,128)(2,1)S(1)} copy-done((bf16[1408,128]{1,0:T(8,128)(2,1)S(1)}, bf16[1408,128]{1,0:T(8,128)(2,1)}, u32[]{:S(2)}) %copy-start.3) | copy-done | bytes 360472
  64.0 26.7 %shard_map.182 = (bf16[2048,128]{1,0:T(8,128)(2,1)S(1)}, f32[384,128]{1,0:T(8,128)S(1)}, f32[128,128]{1,0:T(8,128)S(1)}, f32[256,128]{1,0:T(8,128)S(1)}, f32[128,128]{1,0:T(8,128)S(1)}, /*index=5*/f32[4,128]{1,0:T(4,128)S(1)}) custom-call(f32[2048,128]{1,0:T(8,128)S(1)} %copy-done, bf16[1408,128]{1,0:T(8,128)(2,1)S(1)} %copy-done.3, f32[128,8,128]{2,1,0:T(8,128)S(1)} %bitcast.15), custom_call_target="tpu_custom_call" | custom-call | tf_op jit(solution)/shard_map/pallas_call | solution.py:627
  90.6 0.8 copy.26
  91.4 0.7 copy.27
  92.1 0.6 copy.28
  92.8 0.7 copy.29
  93.4 0.6 copy.30
  94.0 0.6 copy.31
Async XLA Ops:
  0.6 1.0 %copy-start.1 = (bf16[16,32,4,128]{3,2,1,0:T(4,128)(2,1)S(1)}, bf16[16,32,4,128]{3,2,1,0:T(4,128)(2,1)}, u32[]{:S(2)}) copy-start(bf16[16,32,4,128]{3,2,1,0:T(4,128)(2,1)} %param.13) | copy-start | bytes 1572868
  1.7 0.8 copy-start.4
  15.2 0.8 copy-start.5
  16.0 0.5 copy-start.6
  60.7 1.2 %copy-start = (f32[2048,128]{1,0:T(8,128)S(1)}, f32[2048,128]{1,0:T(8,128)}, u32[]{:S(2)}) copy-start(f32[2048,128]{1,0:T(8,128)} %get-tuple-element.21.base_ref) | copy-start | bytes 3145732
  61.9 1.0 %copy-start.2 = (f32[1024,128]{1,0:T(8,128)S(1)}, f32[1024,128]{1,0:T(8,128)}, u32[]{:S(2)}) copy-start(f32[1024,128]{1,0:T(8,128)} %get-tuple-element.23) | copy-start | bytes 1572868
  63.0 1.0 %copy-start.3 = (bf16[1408,128]{1,0:T(8,128)(2,1)S(1)}, bf16[1408,128]{1,0:T(8,128)(2,1)}, u32[]{:S(2)}) copy-start(bf16[1408,128]{1,0:T(8,128)(2,1)} %get-tuple-element.22.out_ref) | copy-start | bytes 1081348

commit v3 on v2

--- a/solution.py
+++ b/solution.py
@@ -13,6 +13,7 @@
 CELLS = PLANES * ROWS
 EDGES = 12288
 TILE = 896
+LOCAL_VMEM = 42 * 1024 * 1024
 PADDED = EDGES + TILE
 CHUNK = 512
 RAW_ROWS = 1024
@@ -49,6 +50,12 @@
     sigma = 0.5 * jnp.tanh(0.5 * z) + 0.5
     value = z * sigma
     return value, sigma * (1.0 + (z - value))
+
+
+def steps_of(send, recv):
+    step = send - (((recv >> 7) + 1) * 204 + (((recv >> 2) & 31) + 1) * 6 + (recv & 3) + 1)
+    size = jnp.abs(step)
+    return step, jnp.where(size == 204, 0, jnp.where(size == 6, 1, 2))
 
 
 def local_kernel(
@@ -60,6 +67,8 @@
     node_ref,
     cot_node_ref,
     face_ref,
+    key_col,
+    kind_col,
     w1e_ref,
     b1e_ref,
     w2e_ref,
@@ -76,7 +85,6 @@
     value,
     slope,
     grad,
-    code_col,
     code_row,
     proj,
     proj_own,
@@ -85,11 +93,17 @@
     leaving,
     gathered,
     degree,
-    table,
+    tables,
     sums,
     diag_w1,
     diag_w2t,
     diag_w1t,
+    z_a,
+    z_b,
+    d_a,
+    d_b,
+    starts,
+    planes,
     sems,
 ):
     copies = [
@@ -100,26 +114,32 @@
         item.start()
 
     tail = jnp.zeros((TILE, H), BF16)
-    edge[EDGES:, :] = tail
-    cot[EDGES:, :] = tail
-
-    recv = recv_ref[...]
-    step = send_ref[...] - (
-        ((recv >> 7) + 1) * 204 + (((recv >> 2) & 31) + 1) * 6 + (recv & 3) + 1
-    )
-    size = jnp.abs(step)
-    axis = jnp.where(size == 204, 0, jnp.where(size == 6, 1, 2))
-    key = (recv >> 7) * 256 + jnp.where(step < 0, 128, 0) + (recv & 127)
-    code = key * 4 + axis
+    for ref in (edge, cot, value, slope):
+        ref[EDGES:, :] = tail
+
+    def list_plane(i, n):
+        lo, hi = bounds[i], bounds[i + 1]
+        first = (lo >> 4) << 4
+        count = jnp.where(hi > lo, (hi - first + (TILE - 1)) // TILE, 0)
+
+        def put(t, n):
+            starts[n] = first + t * TILE
+            planes[n] = i
+            return n + 1
+
+        return lax.fori_loop(0, count, put, n)
+
+    starts[0] = EDGES
+    planes[0] = 0
+    last = lax.fori_loop(0, PLANES, list_plane, 1)
+    rounds = last // 2
+    starts[last] = EDGES
+    planes[last] = 0
+
+    recv, step, axis = recv_ref[...], *steps_of(send_ref[...], recv_ref[...])
+    code = recv * 8 + jnp.where(step < 0, 4, 0) + axis
     code_row[0:96, :] = code
-    code_row[96:, :] = jnp.full((code_row.shape[0] - 96, 128), -4, jnp.int32)
-    turned = jnp.concatenate([code.astype(F32), jnp.zeros((32, 128), F32)], axis=0).T.astype(
-        jnp.int32
-    )
-    for k in range(96):
-        code_col[k * 128 : (k + 1) * 128, :] = jnp.broadcast_to(turned[:, k : k + 1], (128, 128))
-    code_col[EDGES:, :] = jnp.full((TILE, 128), -4, jnp.int32)
-
+    code_row[96:, :] = jnp.full((code_row.shape[0] - 96, 128), -8, jnp.int32)
     w1a = w1e_ref[0:H, :]
     w1b = w1e_ref[H : 2 * H, :]
     w1c = w1e_ref[2 * H :, :]
@@ -139,6 +159,8 @@
         both = dot(node_ref[rows, :], w1bc)
         proj[pl.ds(pl.multiple_of(k * CHUNK + ROWS, ROWS), CHUNK), :] = both[:, :H]
         proj_own[rows, :] = both[:, H:] + b1e
+        gathered[rows, :] = jnp.zeros((CHUNK, 2 * H), F32)
+        degree[rows, :] = jnp.zeros((CHUNK, H), F32)
         return carry
 
     lax.fori_loop(0, CELLS // CHUNK, project, 0)
@@ -149,51 +171,14 @@
     low_y = row_id < 4
     high_y = row_id >= 124
 
-    def first_row(i):
-        return (bounds[i] >> 4) << 4
-
-    def tiles_of(i):
-        lo, hi = bounds[i], bounds[i + 1]
-        count = (hi - first_row(i) + (TILE - 1)) // TILE
-        return jnp.where(hi > lo, count, 0)
-
-    def column_codes(start, i):
-        codes = code_col[pl.ds(start, TILE), :]
-        return codes & 3, (codes >> 2) - 256 * i
-
-    def one_hot(keys):
-        lane = lax.broadcasted_iota(jnp.int32, (TILE, 128), 1)
-        low = jnp.where(keys == lane, 1.0, 0.0)
-        high = jnp.where(keys == lane + 128, 1.0, 0.0)
-        return jnp.concatenate([low, high], axis=1).astype(BF16)
-
-    def one_hot_turned(start, i):
-        q = start >> 7
-        off = start & 127
-        turn = (128 - off) & 127
-        here = pltpu.roll(code_row[pl.ds(q, 8), :], turn, 1)
-        there = pltpu.roll(code_row[pl.ds(q + 1, 8), :], turn, 1)
-        lane = lax.broadcasted_iota(jnp.int32, (8, 128), 1)
-        keys = (jnp.where(lane < 128 - off, here, there) >> 2) - 256 * i
-        slot = lax.broadcasted_iota(jnp.int32, (256, 128), 0)
-        pieces = [
-            jnp.where(jnp.broadcast_to(keys[k : k + 1, :], (256, 128)) == slot, 1.0, 0.0)
-            for k in range(TILE // 128)
-        ]
-        return pieces
-
-    def keep_head(ref, start, new, inside):
-        old = ref[pl.ds(start, 16), :].astype(F32)
-        return jnp.concatenate([jnp.where(inside[:16], new[:16], old), new[16:]], axis=0)
-
-    copies[0].wait()
-
-    def forward_plane(i, carry):
-        rows = pl.ds(pl.multiple_of(i * ROWS, ROWS), ROWS)
-        own = proj_own[rows, :]
-        mine = proj[pl.ds(pl.multiple_of((i + 1) * ROWS, ROWS), ROWS), :]
-        above = proj[pl.ds(pl.multiple_of((i + 2) * ROWS, ROWS), ROWS), :]
-        below = proj[rows, :]
+    def plane_rows(i):
+        return pl.ds(pl.multiple_of(i * ROWS, ROWS), ROWS)
+
+    def build_table(i, carry):
+        own = proj_own[plane_rows(i), :]
+        mine = proj[plane_rows(i + 1), :]
+        above = proj[plane_rows(i + 2), :]
+        below = proj[plane_rows(i), :]
         wide[0:4, :] = proj_face[pl.ds(Y_LOW + 4 * i, 4), :]
         wide[124:128, :] = proj_face[pl.ds(Y_HIGH + 4 * i, 4), :]
         wide[pl.ds(ROWS, 32, stride=4), :] = proj_face[pl.ds(Z_LOW + 32 * i, 32), :]
@@ -204,48 +189,97 @@
         down_y = jnp.where(low_y, side_y, pltpu.roll(mine, 4, 0))
         up_z = jnp.where(high_z, side_z, pltpu.roll(mine, 127, 0))
         down_z = jnp.where(low_z, side_z, pltpu.roll(mine, 1, 0))
-        table[0:ROWS, :] = jnp.concatenate([above + own, up_y + own, up_z + own], axis=1).astype(
-            BF16
-        )
-        table[ROWS:, :] = jnp.concatenate(
+        tables[i, 0:ROWS, :] = jnp.concatenate(
+            [above + own, up_y + own, up_z + own], axis=1
+        ).astype(BF16)
+        tables[i, ROWS : 2 * ROWS, :] = jnp.concatenate(
             [below + own, down_y + own, down_z + own], axis=1
         ).astype(BF16)
-        gathered[rows, :] = jnp.zeros((ROWS, 2 * H), F32)
-        degree[rows, :] = jnp.zeros((ROWS, H), F32)
-
-        def tile(t, inner):
-            start = pl.multiple_of(first_row(i) + t * TILE, 16)
-            span = pl.ds(start, TILE)
-            axis, keys = column_codes(start, i)
-            picked = dot(one_hot(keys), table[...])
-            latent = edge[span, :]
-            z = pair_dot(latent, diag_w1[...]) + jnp.where(
-                axis == 0,
-                picked[:, :H],
-                jnp.where(axis == 1, picked[:, H : 2 * H], picked[:, 2 * H :]),
-            )
-            u, sp = slope_and_value(z)
-            inside = (keys >= 0) & (keys < 256)
-            value[span, :] = keep_head(value, start, u, inside).astype(BF16)
-            slope[span, :] = keep_head(slope, start, sp, inside).astype(BF16)
-            pieces = one_hot_turned(start, i)
-            spread = jnp.concatenate(pieces, axis=1)
-            spread = (spread[:ROWS] + spread[ROWS:]).astype(BF16)
-            gathered[rows, :] += dot(spread, jnp.concatenate([latent, u.astype(BF16)], axis=1))
-            count = pieces[0]
-            for piece in pieces[1:]:
-                count = count + piece
-            count = count[:ROWS] + count[ROWS:]
-            degree[rows, :] += jnp.broadcast_to(
-                jnp.sum(count, axis=1, keepdims=True), (ROWS, H)
-            )
-            return inner
-
-        return lax.fori_loop(0, tiles_of(i), tile, carry)
-
-    value[EDGES:, :] = tail
-    slope[EDGES:, :] = tail
-    lax.fori_loop(0, PLANES, forward_plane, 0)
+        return carry
+
+    lax.fori_loop(0, PLANES, build_table, 0)
+
+    def tile_at(j):
+        start = pl.multiple_of(starts[j], 16)
+        return start, pl.ds(start, TILE), planes[j]
+
+    lane = lax.broadcasted_iota(jnp.int32, (1, 128), 1).astype(F32)
+    lane_low, lane_high = lane.astype(BF16), (lane + 128.0).astype(BF16)
+
+    one, zero = jnp.ones((TILE, 128), BF16), jnp.zeros((TILE, 128), BF16)
+
+    def kinds(i, count):
+        first = jnp.full((1, 128), 4 * i, jnp.int32).astype(F32)
+        return [first + float(k) for k in range(count)]
+
+    def head_inside(start, i):
+        kind = kind_col[pl.ds(start, 16), :].astype(F32)
+        low, _, high = kinds(i, 3)
+        return (kind >= low) & (kind <= high)
+
+    def row_codes(start):
+        q = start >> 7
+        off = start & 127
+        turn = (128 - off) & 127
+        here = pltpu.roll(code_row[pl.ds(q, 8), :], turn, 1)
+        there = pltpu.roll(code_row[pl.ds(q + 1, 8), :], turn, 1)
+        spot = lax.broadcasted_iota(jnp.int32, (8, 128), 1)
+        return jnp.where(spot < 128 - off, here, there)
+
+    def one_hot_turned(keys, slots):
+        slot = lax.broadcasted_iota(jnp.int32, (slots, 128), 0)
+        return [
+            jnp.where(jnp.broadcast_to(keys[k : k + 1, :], (slots, 128)) == slot, 1.0, 0.0)
+            for k in range(TILE // 128)
+        ]
+
+    def keep_head(ref, start, new, inside):
+        old = ref[pl.ds(start, 16), :].astype(F32)
+        return jnp.concatenate([jnp.where(inside, new[:16], old), new[16:]], axis=0)
+
+    copies[0].wait()
+
+    def forward_sums(j, z_buffer):
+        start, span, i = tile_at(j)
+        u, sp = slope_and_value(z_buffer[...])
+        inside = head_inside(start, i)
+        u = keep_head(value, start, u, inside).astype(BF16)
+        value[span, :] = u
+        slope[span, :] = keep_head(slope, start, sp, inside).astype(BF16)
+        pieces = one_hot_turned((row_codes(start) >> 3) - 128 * i, ROWS)
+        count = pieces[0]
+        for piece in pieces[1:]:
+            count = count + piece
+        degree[plane_rows(i), :] += count
+        spread = jnp.concatenate(pieces, axis=1).astype(BF16)
+        gathered[plane_rows(i), :] += dot(spread, jnp.concatenate([edge[span, :], u], axis=1))
+
+    def forward_values(j, z_buffer):
+        start, span, i = tile_at(j)
+        keys = key_col[span, :]
+        hot = jnp.concatenate(
+            [jnp.where(keys == lane_low, one, zero), jnp.where(keys == lane_high, one, zero)],
+            axis=1,
+        )
+        picked = dot(hot, tables[i])
+        kind = kind_col[span, :].astype(F32)
+        first, second = kinds(i, 2)
+        z_buffer[...] = pair_dot(edge[span, :], diag_w1[...]) + jnp.where(
+            kind == first,
+            picked[:, :H],
+            jnp.where(kind == second, picked[:, H : 2 * H], picked[:, 2 * H :]),
+        )
+
+    def forward(m, carry):
+        forward_values(2 * m + 1, z_a)
+        forward_sums(2 * m, z_b)
+        forward_values(2 * m + 2, z_b)
+        forward_sums(2 * m + 1, z_a)
+        return carry
+
+    z_b[...] = jnp.zeros((TILE, H), F32)
+    lax.fori_loop(0, rounds, forward, 0)
+    forward_sums(2 * rounds, z_b)
 
     raw_ref[...] = jnp.zeros((RAW_ROWS, H), F32)
     w2nt = w2n_ref[...].T
@@ -254,10 +288,11 @@
     def nodes(k, carry):
         rows = pl.ds(pl.multiple_of(k * CHUNK, CHUNK), CHUNK)
         packed = gathered[rows, :]
+        count = jnp.sum(degree[rows, :], axis=1, keepdims=True)
         aggregate = (
             packed[:, :H]
             + dot(packed[:, H:].astype(BF16), w2e_ref[...])
-            + degree[rows, :] * b2e_ref[...]
+            + count * b2e_ref[...]
         ).astype(BF16)
         x_node = jnp.concatenate([node_ref[rows, :], aggregate], axis=1)
         z_node = dot(x_node, w1n_ref[...]) + b1n_ref[...]
@@ -276,58 +311,75 @@
     lax.fori_loop(0, CELLS // CHUNK, nodes, 0)
     copies[1].wait()
 
-    def backward_plane(i, carry):
-        rows = pl.ds(pl.multiple_of(i * ROWS, ROWS), ROWS)
-        drow = gathered[rows, 0:H].astype(BF16)
-        twice = jnp.concatenate([drow, drow], axis=0)
-        sums[i + 1] = jnp.zeros((256, 3 * H), F32)
-
-        def tile(t, inner):
-            start = pl.multiple_of(first_row(i) + t * TILE, 16)
-            span = pl.ds(start, TILE)
-            axis, keys = column_codes(start, i)
-            inside = (keys >= 0) & (keys < 256)
-            added = dot(one_hot(keys), twice)
-            d_wide = jnp.where(inside, cot[span, :].astype(F32) + added, 0.0)
-            d_edge = d_wide.astype(BF16)
-            dz = pair_dot(d_edge, diag_w2t[...]) * slope[span, :].astype(F32)
-            dz_edge = dz.astype(BF16)
-            new = d_edge.astype(F32) + pair_dot(dz_edge, diag_w1t[...])
-            grad[span, :] = keep_head(grad, start, new, inside).astype(BF16)
-            both = dot_tn(
-                jnp.concatenate([edge[span, :], value[span, :]], axis=1),
-                jnp.concatenate([dz_edge, d_edge], axis=1),
-            )
-            raw_ref[0:H, :] += both[:H, :H]
-            raw_ref[384:512, :] += both[H:, H:]
-            raw_ref[897:898, :] += jnp.sum(d_edge.astype(F32), axis=0, keepdims=True)
-            spread = jnp.concatenate(one_hot_turned(start, i), axis=1).astype(BF16)
-            parted = jnp.concatenate(
-                [jnp.where(axis == a, dz, 0.0).astype(BF16) for a in range(3)], axis=1
-            )
-            sums[i + 1] += dot(spread, parted)
-            return inner
-
-        return lax.fori_loop(0, tiles_of(i), tile, carry)
-
-    lax.fori_loop(0, PLANES, backward_plane, 0)
+    def clear(i, carry):
+        sums[i] = jnp.zeros((256, 3 * H), F32)
+        return carry
+
+    lax.fori_loop(0, PLANES + 2, clear, 0)
+    ones = jnp.ones((16, TILE), BF16)
+
+    def backward_sums(j, d_buffer):
+        start, span, i = tile_at(j)
+        dz_edge = d_buffer[:, :H]
+        both = dot(
+            jnp.concatenate([edge[span, :].T, value[span, :].T, ones], axis=0), d_buffer[...]
+        )
+        raw_ref[0:H, :] += both[:H, :H]
+        raw_ref[384:512, :] += both[H : 2 * H, H:]
+        raw_ref[897:898, :] += both[2 * H : 2 * H + 1, H:]
+        codes = row_codes(start)
+        keys = (codes >> 3) - 128 * i + ((codes >> 2) & 1) * 128
+        keys = jnp.where((codes >> 10) == i, keys, -1)
+        spread = jnp.concatenate(one_hot_turned(keys, 2 * ROWS), axis=1).astype(BF16)
+        kind = kind_col[span, :]
+        first, second = (number.astype(BF16) for number in kinds(i, 2))
+        parted = jnp.concatenate(
+            [
+                jnp.where(kind == first, dz_edge, zero),
+                jnp.where(kind == second, dz_edge, zero),
+                dz_edge,
+            ],
+            axis=1,
+        )
+        sums[i + 1] += dot(spread, parted)
+
+    def backward_values(j, d_buffer):
+        start, span, i = tile_at(j)
+        keys, kind = key_col[span, :], kind_col[span, :]
+        hot = jnp.where((keys == lane_low) | (keys == lane_high), one, zero)
+        added = pair_dot(hot, block_diagonal(gathered[plane_rows(i), 0:H].astype(BF16)))
+        d_wide = cot[span, :].astype(F32) + added
+        low, _, high = (number.astype(BF16) for number in kinds(i, 3))
+        d_edge = jnp.where((kind >= low) & (kind <= high), d_wide.astype(BF16), zero)
+        dz_edge = (pair_dot(d_edge, diag_w2t[...]) * slope[span, :].astype(F32)).astype(BF16)
+        d_buffer[...] = jnp.concatenate([dz_edge, d_edge], axis=1)
+        new = d_wide + pair_dot(dz_edge, diag_w1t[...])
+        grad[span, :] = keep_head(grad, start, new, head_inside(start, i)).astype(BF16)
+
+    def backward(m, carry):
+        backward_values(2 * m + 1, d_a)
+        backward_sums(2 * m, d_b)
+        backward_values(2 * m + 2, d_b)
+        backward_sums(2 * m + 1, d_a)
+        return carry
+
+    d_b[...] = jnp.zeros((TILE, 2 * H), BF16)
+    lax.fori_loop(0, rounds, backward, 0)
+    backward_sums(2 * rounds, d_b)
     grad_copy = pltpu.make_async_copy(grad.at[pl.ds(0, EDGES), :], grad_edge_hbm, sems.at[2])
     grad_copy.start()
 
-    sums[0] = jnp.zeros((256, 3 * H), F32)
-    sums[PLANES + 1] = jnp.zeros((256, 3 * H), F32)
     w1bt = w1e_ref[H : 2 * H, :].T
     w1ct = w1e_ref[2 * H :, :].T
     diag_w2t[:, 0:H] = jnp.concatenate([w1bt, w1ct], axis=0)
 
     def cells(i, carry):
-        rows = pl.ds(pl.multiple_of(i * ROWS, ROWS), ROWS)
+        rows = plane_rows(i)
         here = sums[i + 1]
-        plus, minus = here[:ROWS], here[ROWS:]
-        everything = plus + minus
-        arrived = everything[:, :H] + everything[:, H : 2 * H] + everything[:, 2 * H :]
-        yp, ym = plus[:, H : 2 * H], minus[:, H : 2 * H]
-        zp, zm = plus[:, 2 * H :], minus[:, 2 * H :]
+        third = here[:, 2 * H :] - here[:, :H] - here[:, H : 2 * H]
+        arrived = here[:ROWS, 2 * H :] + here[ROWS:, 2 * H :]
+        yp, ym = here[:ROWS, H : 2 * H], here[ROWS:, H : 2 * H]
+        zp, zm = third[:ROWS], third[ROWS:]
         left = (
             sums[i, 0:ROWS, 0:H]
             + sums[i + 2, ROWS : 2 * ROWS, 0:H]
@@ -343,12 +395,10 @@
         wide[ROWS:, :] = zp
         leaving[pl.ds(Z_LOW + 32 * i, 32), :] = wide[pl.ds(0, 32, stride=4), :]
         leaving[pl.ds(Z_HIGH + 32 * i, 32), :] = wide[pl.ds(ROWS + 3, 32, stride=4), :]
-        base_ref[rows, :] += dot(
-            jnp.concatenate([left, arrived_low], axis=1), diag_w2t[:, 0:H]
-        )
-        cells_here = node_ref[rows, :]
-        raw_ref[H : 2 * H, :] += dot_tn(cells_here, left)
-        raw_ref[2 * H : 3 * H, :] += dot_tn(cells_here, arrived_low)
+        base_ref[rows, :] += dot(jnp.concatenate([left, arrived_low], axis=1), diag_w2t[:, 0:H])
+        both = dot_tn(node_ref[rows, :], jnp.concatenate([left, arrived_low], axis=1))
+        raw_ref[H : 2 * H, :] += both[:, :H]
+        raw_ref[2 * H : 3 * H, :] += both[:, H:]
         raw_ref[896:897, :] += jnp.sum(arrived, axis=0, keepdims=True)
         return carry
 
@@ -363,7 +413,7 @@
 
 def local_terms(bounds, *operands):
     vmem = pl.BlockSpec(memory_space=pltpu.VMEM)
-    anywhere = pl.BlockSpec(memory_space=pl.ANY)
+    anywhere = pl.BlockSpec(memory_space=pltpu.MemorySpace.HBM)
     return pl.pallas_call(
         local_kernel,
         out_shape=(
@@ -373,15 +423,10 @@
             jax.ShapeDtypeStruct((RAW_ROWS, H), F32),
         ),
         in_specs=[pl.BlockSpec(memory_space=pltpu.SMEM), vmem, vmem, anywhere, anywhere]
-        + [vmem] * 10,
+        + [vmem] * 12,
         out_specs=(anywhere, vmem, vmem, vmem),
-        scratch_shapes=[
-            pltpu.VMEM((PADDED, H), BF16),
-            pltpu.VMEM((PADDED, H), BF16),
-            pltpu.VMEM((PADDED, H), BF16),
-            pltpu.VMEM((PADDED, H), BF16),
-            pltpu.VMEM((PADDED, H), BF16),
-            pltpu.VMEM((PADDED, 128), jnp.int32),
+        scratch_shapes=[pltpu.VMEM((PADDED, H), BF16)] * 5
+        + [
             pltpu.VMEM((112, 128), jnp.int32),
             pltpu.VMEM((CELLS + 2 * ROWS, H), F32),
             pltpu.VMEM((CELLS, H), F32),
@@ -390,14 +435,20 @@
             pltpu.VMEM((FACES, H), F32),
             pltpu.VMEM((CELLS, 2 * H), F32),
             pltpu.VMEM((CELLS, H), F32),
-            pltpu.VMEM((256, 3 * H), BF16),
+            pltpu.VMEM((PLANES, 256, 3 * H), BF16),
             pltpu.VMEM((PLANES + 2, 256, 3 * H), F32),
             pltpu.VMEM((256, 256), BF16),
             pltpu.VMEM((256, 256), BF16),
             pltpu.VMEM((256, 256), BF16),
+            pltpu.VMEM((TILE, H), F32),
+            pltpu.VMEM((TILE, H), F32),
+            pltpu.VMEM((TILE, 2 * H), BF16),
+            pltpu.VMEM((TILE, 2 * H), BF16),
+            pltpu.SMEM((48,), jnp.int32),
+            pltpu.SMEM((48,), jnp.int32),
             pltpu.SemaphoreType.DMA((3,)),
         ],
-        compiler_params=pltpu.CompilerParams(vmem_limit_bytes=62 * 1024 * 1024),
+        compiler_params=pltpu.CompilerParams(vmem_limit_bytes=LOCAL_VMEM),
         cost_estimate=pl.CostEstimate(
             flops=10_000_000_000, bytes_accessed=20_000_000, transcendentals=2_000_000
         ),
@@ -437,7 +488,19 @@
     return copies
 
 
-def halo_kernel(node_ref, recv_ref, face_ref, bounds_ref, cells, packed, send_sems, recv_sems):
+def halo_kernel(
+    node_ref,
+    send_ref,
+    recv_ref,
+    face_ref,
+    bounds_ref,
+    key_col,
+    kind_col,
+    cells,
+    packed,
+    send_sems,
+    recv_sems,
+):
     barrier = pltpu.get_barrier_semaphore()
     for side in range(6):
         pl.semaphore_signal(barrier, inc=1, device_id=across(side), device_id_type=MESH)
@@ -457,20 +520,42 @@
     for i in range(PLANES + 1):
         below = jnp.where(recv < ROWS * i, 1.0, 0.0)
         bounds_ref[i] = jnp.sum(below).astype(jnp.int32)
+    step, axis = steps_of(send_ref[...], recv)
+    columns = (key_col, kind_col)
+    zero = jnp.zeros((32, 128), F32)
+    turned = jnp.concatenate(
+        [
+            jnp.concatenate([numbers.astype(F32), zero], axis=0).T
+            for numbers in ((recv & 127) + jnp.where(step < 0, 128, 0), (recv >> 7) * 4 + axis)
+        ],
+        axis=0,
+    ).astype(BF16)
+    row = lax.broadcasted_iota(jnp.int32, (128, 256), 0)
+    lane = lax.broadcasted_iota(jnp.int32, (128, 256), 1)
+    for k in range(0, 96, 2):
+        pick = jnp.where(row - (lane >> 7) == k, 1.0, 0.0).astype(BF16)
+        both = dot(turned, pick).astype(BF16)
+        for c, column in enumerate(columns):
+            block = both[128 * c : 128 * c + 128]
+            column[k * 128 : (k + 1) * 128, :] = block[:, :128]
+            column[(k + 1) * 128 : (k + 2) * 128, :] = block[:, 128:]
+    for column in columns:
+        column[EDGES:, :] = jnp.full((TILE, 128), -4.0, BF16)
     for item in copies:
         item.wait()
 
 
-def halo(node, recv):
+def halo(node, send, recv):
     vmem = pl.BlockSpec(memory_space=pltpu.VMEM)
     return pl.pallas_call(
         halo_kernel,
         out_shape=(
             jax.ShapeDtypeStruct((FACES, H), BF16),
             jax.ShapeDtypeStruct((PLANES + 1,), jnp.int32),
-        ),
-        in_specs=[vmem, vmem],
-        out_specs=(vmem, pl.BlockSpec(memory_space=pltpu.SMEM)),
+        )
+        + (pltpu.VMEM((PADDED, 128), BF16),) * 2,
+        in_specs=[vmem] * 3,
+        out_specs=(vmem, pl.BlockSpec(memory_space=pltpu.SMEM)) + (vmem,) * 2,
         scratch_shapes=[
             pltpu.VMEM((CELLS, H), F32),
             pltpu.VMEM((FACES, H), BF16),
@@ -478,9 +563,9 @@
             pltpu.SemaphoreType.DMA((6,)),
         ],
         compiler_params=pltpu.CompilerParams(
-            collective_id=0, has_side_effects=True, vmem_limit_bytes=16 * 1024 * 1024
+            collective_id=0, has_side_effects=True, vmem_limit_bytes=12 * 1024 * 1024
         ),
-    )(node, recv)
+    )(node, send, recv)
 
 
 def finish_kernel(
@@ -488,11 +573,7 @@
     out_ref,
     raw_ref,
     grad_ref,
-    w1e_ref,
-    w2e_ref,
-    w1n_ref,
-    w2n_ref,
-    bias_ref,
+    total_ref,
     faces,
     cells,
     partner_part,
@@ -608,34 +689,55 @@
     settle(half, all_send.at[0])
     settle(half, all_send.at[1])
     last.wait()
-    total = full[...].reshape(RAW_ROWS, H)
+    total_ref[...] = full[...]
+
+
+def write_kernel(grad_ref, total_ref, *refs):
+    outs, scaled, sems = refs[:6], refs[6], refs[7]
+    first = pltpu.make_async_copy(grad_ref, outs[0], sems.at[0])
+    first.start()
+    total = total_ref[...]
     squares = jnp.sum(total * total, axis=0, keepdims=True)
     squares = jnp.sum(squares, axis=1, keepdims=True)
     factor = 1.0 / jnp.maximum(1.0, jnp.sqrt(squares / (7 * H * H + 4 * H)))
-    scaled = total * factor
-    w1e_ref[...] = scaled[:384]
-    w2e_ref[...] = scaled[384:512]
-    w1n_ref[...] = scaled[512:768]
-    w2n_ref[...] = scaled[768:896]
-    bias_ref[...] = scaled[896:900]
+    scaled[...] = total * factor
+    copies = [first]
+    at = 0
+    for k, rows in enumerate((384, 128, 256, 128, 4)):
+        copies.append(
+            pltpu.make_async_copy(scaled.at[pl.ds(at, rows), :], outs[k + 1], sems.at[k + 1])
+        )
+        copies[-1].start()
+        at += rows
+    for item in copies:
+        item.wait()
+
+
+def write(grad, total):
+    vmem = pl.BlockSpec(memory_space=pltpu.VMEM)
+    return pl.pallas_call(
+        write_kernel,
+        out_shape=(jax.ShapeDtypeStruct((CELLS, H), BF16),)
+        + tuple(jax.ShapeDtypeStruct((rows, H), F32) for rows in (384, 128, 256, 128, 4)),
+        in_specs=[vmem] * 2,
+        out_specs=(pl.BlockSpec(memory_space=pl.ANY),) * 6,
+        scratch_shapes=[pltpu.VMEM((RAW_ROWS, H), F32), pltpu.SemaphoreType.DMA((6,))],
+        compiler_params=pltpu.CompilerParams(vmem_limit_bytes=48 * 1024 * 1024),
+    )(grad, total)
 
 
 def finish(base, out, raw):
     chips = lax.axis_size("gx") * lax.axis_size("gy") * lax.axis_size("gz") // 2
     block = RAW_ROWS // (2 * chips)
     vmem = pl.BlockSpec(memory_space=pltpu.VMEM)
-    return pl.pallas_call(
+    grad, total = pl.pallas_call(
         finish_kernel,
         out_shape=(
             jax.ShapeDtypeStruct((CELLS, H), BF16),
-            jax.ShapeDtypeStruct((384, H), F32),
-            jax.ShapeDtypeStruct((128, H), F32),
-            jax.ShapeDtypeStruct((256, H), F32),
-            jax.ShapeDtypeStruct((128, H), F32),
-            jax.ShapeDtypeStruct((4, H), F32),
+            jax.ShapeDtypeStruct((2 * chips, block, H), F32),
         ),
         in_specs=[vmem] * 3,
-        out_specs=(vmem,) * 6,
+        out_specs=(vmem,) * 2,
         scratch_shapes=[
             pltpu.VMEM((FACES, H), BF16),
             pltpu.VMEM((CELLS, H), F32),
@@ -655,6 +757,7 @@
             collective_id=1, has_side_effects=True, vmem_limit_bytes=24 * 1024 * 1024
         ),
     )(base, out, raw.reshape(2 * chips, block, H))
+    return write(grad, total.reshape(RAW_ROWS, H))
 
 
 def on_device(
@@ -674,16 +777,18 @@
 ):
     cells = node_latent.reshape(CELLS, H)
     receiver_ids = receivers.reshape(96, 128)
-    faces, bounds = halo(cells, receiver_ids)
+    sender_ids = senders.reshape(96, 128)
+    faces, bounds, *columns = halo(cells, sender_ids, receiver_ids)
     grad_edge, base, out, raw = local_terms(
         bounds,
-        senders.reshape(96, 128),
+        sender_ids,
         receiver_ids,
-        edge_latent.reshape(EDGES, H),
-        cot_edge.reshape(EDGES, H),
+        pltpu.with_memory_space_constraint(edge_latent.reshape(EDGES, H), pltpu.MemorySpace.HBM),
+        pltpu.with_memory_space_constraint(cot_edge.reshape(EDGES, H), pltpu.MemorySpace.HBM),
         cells,
         cot_node.reshape(CELLS, H),
         faces,
+        *columns,
         w1_edge,
         b1_edge.reshape(1, H),
         w2_edge,

time: 94.9 us -> 87.7 us (0.924)
  Pallas kernels: 83.6 us -> 74.8 us
  local copies, waits for them, and re-layouts: 10.3 us -> 11.5 us
    pallas_call x1, Pallas kernels: 44.2 us -> 34.3 us  [local_terms(): pl.pallas_call(local_kernel, out_shape=(jax.ShapeDtypeStruct((EDGES, H),...]
    unnamed x20 -> x28, local copies, waits for them, and re-layouts: 10.3 us -> 11.5 us
    pallas_call x0 -> x1, Pallas kernels: none -> 1.08 us  [write(): pl.pallas_call(write_kernel, out_shape=(jax.ShapeDtypeStruct((CELLS, H),...]
where the time goes in v3:
time: 87.7 us; the launch traced here: 87 us
  Pallas kernels  74.8 us (85%)
  local copies, waits for them, and re-layouts  11.5 us (13%)
    pallas_call x1, Pallas kernels, local_terms(): pl.pallas_call(local_kernel, out_shape=(jax.ShapeDtypeStruct((EDGES, H),...  34.3 us
    pallas_call x1, Pallas kernels, finish(): pl.pallas_call(finish_kernel, out_shape=(jax.ShapeDtypeStruct((CELLS, H),...  26.7 us
    pallas_call x1, Pallas kernels, halo(): pl.pallas_call(halo_kernel, out_shape=(jax.ShapeDtypeStruct((FACES, H), B...  12.8 us
    unnamed x28, local copies, waits for them, and re-layouts  11.5 us

profile of v3, /device:TPU:1, one launch (start us, length us, event | category | flops | bytes accessed | tf_op | source)
XLA Modules:
  0.0 87.0 jit_solution(6500898909846364189)
XLA Ops:
  0.6 0.0 copy-start
  0.6 1.0 %copy-done = bf16[16,32,4,128]{3,2,1,0:T(4,128)(2,1)S(1)} copy-done((bf16[16,32,4,128]{3,2,1,0:T(4,128)(2,1)S(1)}, bf16[16,32,4,128]{3,2,1,0:T(4,128)(2,1)}, u32[]{:S(2)}) %copy-start) | copy-done | bytes 524312
  1.7 0.0 copy-start.2
  1.7 0.8 copy-done.2
  2.5 0.0 copy-start.4
  2.5 0.8 copy-done.4
  3.3 12.8 %shard_map.180 = (bf16[1408,128]{1,0:T(8,128)(2,1)S(1)}, s32[17]{0:T(128)S(1)}, bf16[13184,128]{1,0:T(8,128)(2,1)S(1)}, bf16[13184,128]{1,0:T(8,128)(2,1)S(1)}) custom-call(bf16[2048,128]{1,0:T(8,128)(2,1)S(1)} %bitcast.13, s32[96,128]{1,0:T(8,128)S(1)} %bitcast.17, s32[96,128]{1,0:T(8,128)S(1)} %bitcast.19), custom_call_target="tpu_custom_call" | custom-call | tf_op jit(solution)/shard_map/pallas_call | solution.py:550
  16.1 0.0 copy-start.1
  16.1 1.0 %copy-done.1 = bf16[16,32,4,128]{3,2,1,0:T(4,128)(2,1)S(1)} copy-done((bf16[16,32,4,128]{3,2,1,0:T(4,128)(2,1)S(1)}, bf16[16,32,4,128]{3,2,1,0:T(4,128)(2,1)}, u32[]{:S(2)}) %copy-start.1) | copy-done | bytes 524312
  17.1 0.0 copy-start.3
  17.1 0.8 copy-done.3
  17.9 0.0 copy-start.5
  17.9 0.8 copy-done.5
  18.7 1.0 %copy-done.6 = bf16[16,32,4,128]{3,2,1,0:T(4,128)(2,1)S(1)} copy-done((bf16[16,32,4,128]{3,2,1,0:T(4,128)(2,1)S(1)}, bf16[16,32,4,128]{3,2,1,0:T(4,128)(2,1)}, u32[]{:S(2)}) %copy-start.6) | copy-done | bytes 524312
  19.7 0.9 %copy-done.7 = bf16[384,128]{1,0:T(8,128)(2,1)S(1)} copy-done((bf16[384,128]{1,0:T(8,128)(2,1)S(1)}, bf16[384,128]{1,0:T(8,128)(2,1)}, u32[]{:S(2)}) %copy-start.7) | copy-done | bytes 98328
  20.6 0.8 copy-done.8
  21.5 0.8 copy-done.9
  22.2 0.8 copy-done.10
  23.0 0.7 copy-done.11
  23.6 0.7 copy-done.12
  24.3 0.7 copy-done.13
  25.0 34.3 %shard_map.181 = (bf16[12288,128]{1,0:T(8,128)(2,1)}, f32[2048,128]{1,0:T(8,128)S(1)}, bf16[1408,128]{1,0:T(8,128)(2,1)S(1)}, f32[1024,128]{1,0:T(8,128)S(1)}) custom-call(s32[17]{0:T(128)S(1)} %get-tuple-element.23.bounds, s32[96,128]{1,0:T(8,128)S(1)} %bitcast.18, s32[96,128]{1,0:T(8,128)S(1)} %bitcast.20, bf16[12288,128]{1,0:T(8,128)(2,1)} %bitcast.25, ...), custom_call_target="tpu_custom_call" | custom-call | flops 10000000000 | bytes 20000000 | tf_op jit(solution)/shard_map/pallas_call | solution.py:417
  59.3 26.7 %shard_map.182 = (bf16[2048,128]{1,0:T(8,128)(2,1)S(1)}, f32[128,8,128]{2,1,0:T(8,128)S(1)}) custom-call(f32[2048,128]{1,0:T(8,128)S(1)} %get-tuple-element.27.base_ref, bf16[1408,128]{1,0:T(8,128)(2,1)S(1)} %get-tuple-element.28.out_ref, f32[128,8,128]{2,1,0:T(8,128)S(1)} %bitcast.16), custom_call_target="tpu_custom_call" | custom-call | tf_op jit(solution)/shard_map/pallas_call | solution.py:733
  85.9 1.1 %shard_map.183 = (bf16[2048,128]{1,0:T(8,128)(2,1)}, f32[384,128]{1,0:T(8,128)}, f32[128,128]{1,0:T(8,128)}, f32[256,128]{1,0:T(8,128)}, f32[128,128]{1,0:T(8,128)}, /*index=5*/f32[4,128]{1,0:T(4,128)}) custom-call(bf16[2048,128]{1,0:T(8,128)(2,1)S(1)} %get-tuple-element.30.grad_ref, f32[1024,128]{1,0:T(8,128)S(1)} %bitcast.15), custom_call_target="tpu_custom_call" | custom-call | tf_op jit(solution)/shard_map/pallas_call | solution.py:718
  (8 shorter events, 0.0 us)
Async XLA Ops:
  0.6 1.0 %copy-start = (bf16[16,32,4,128]{3,2,1,0:T(4,128)(2,1)S(1)}, bf16[16,32,4,128]{3,2,1,0:T(4,128)(2,1)}, u32[]{:S(2)}) copy-start(bf16[16,32,4,128]{3,2,1,0:T(4,128)(2,1)} %param.13) | copy-start | bytes 1572868
  1.7 0.8 copy-start.2
  2.5 0.8 copy-start.4
  16.1 1.0 %copy-start.1 = (bf16[16,32,4,128]{3,2,1,0:T(4,128)(2,1)S(1)}, bf16[16,32,4,128]{3,2,1,0:T(4,128)(2,1)}, u32[]{:S(2)}) copy-start(bf16[16,32,4,128]{3,2,1,0:T(4,128)(2,1)} %param.13) | copy-start | bytes 1572868
  17.1 0.8 copy-start.3
  17.9 0.8 copy-start.5
  18.7 1.0 %copy-start.6 = (bf16[16,32,4,128]{3,2,1,0:T(4,128)(2,1)S(1)}, bf16[16,32,4,128]{3,2,1,0:T(4,128)(2,1)}, u32[]{:S(2)}) copy-start(bf16[16,32,4,128]{3,2,1,0:T(4,128)(2,1)} %param.24) | copy-start | bytes 1572868
  19.7 0.9 %copy-start.7 = (bf16[384,128]{1,0:T(8,128)(2,1)S(1)}, bf16[384,128]{1,0:T(8,128)(2,1)}, u32[]{:S(2)}) copy-start(bf16[384,128]{1,0:T(8,128)(2,1)} %w1e_ref.1) | copy-start | bytes 294916
  20.6 0.8 copy-start.8
  21.5 0.8 copy-start.9
  22.2 0.8 copy-start.10
  23.0 0.7 copy-start.11
  23.6 0.7 copy-start.12
  24.3 0.7 copy-start.13

commit v4 on v3

--- a/solution.py
+++ b/solution.py
@@ -13,7 +13,7 @@
 CELLS = PLANES * ROWS
 EDGES = 12288
 TILE = 896
-LOCAL_VMEM = 42 * 1024 * 1024
+LOCAL_VMEM = 37 * 1024 * 1024
 PADDED = EDGES + TILE
 CHUNK = 512
 RAW_ROWS = 1024
@@ -60,57 +60,67 @@
 
 def local_kernel(
     bounds,
-    send_ref,
-    recv_ref,
-    edge_hbm,
-    cot_edge_hbm,
-    node_ref,
-    cot_node_ref,
     face_ref,
     key_col,
     kind_col,
-    w1e_ref,
-    b1e_ref,
-    w2e_ref,
-    b2e_ref,
-    w1n_ref,
-    b1n_ref,
-    w2n_ref,
-    grad_edge_hbm,
-    base_ref,
-    out_ref,
-    raw_ref,
-    edge,
-    cot,
-    value,
-    slope,
-    grad,
-    code_row,
-    proj,
-    proj_own,
-    proj_face,
-    wide,
-    leaving,
-    gathered,
-    degree,
-    tables,
-    sums,
-    diag_w1,
-    diag_w2t,
-    diag_w1t,
-    z_a,
-    z_b,
-    d_a,
-    d_b,
-    starts,
-    planes,
-    sems,
+    edge_hbm,
+    cot_edge_hbm,
+    *refs,
 ):
+    small_hbm, refs = refs[:11], refs[11:]
+    (
+        grad_edge_hbm,
+        base_ref,
+        raw_ref,
+        sums,
+        edge,
+        cot,
+        value,
+        slope,
+        grad,
+        code_row,
+        proj,
+        proj_own,
+        proj_face,
+        wide,
+        gathered,
+        degree,
+        tables,
+        diag_w1,
+        diag_w2t,
+        diag_w1t,
+        z_a,
+        z_b,
+        d_a,
+        d_b,
+        starts,
+        planes,
+        sems,
+        small_sems,
+    ) = refs[:28]
+    small = refs[28:]
+    (
+        recv_ref,
+        send_ref,
+        w1e_ref,
+        b1e_ref,
+        w2e_ref,
+        node_ref,
+        cot_node_ref,
+        b2e_ref,
+        w1n_ref,
+        b1n_ref,
+        w2n_ref,
+    ) = small
+    small_copies = [
+        pltpu.make_async_copy(source, target, small_sems.at[k])
+        for k, (source, target) in enumerate(zip(small_hbm, small))
+    ]
     copies = [
         pltpu.make_async_copy(edge_hbm, edge.at[pl.ds(0, EDGES), :], sems.at[0]),
         pltpu.make_async_copy(cot_edge_hbm, cot.at[pl.ds(0, EDGES), :], sems.at[1]),
     ]
-    for item in copies:
+    for item in small_copies[:6] + copies[:1] + small_copies[6:] + copies[1:]:
         item.start()
 
     tail = jnp.zeros((TILE, H), BF16)
@@ -136,6 +146,8 @@
     starts[last] = EDGES
     planes[last] = 0
 
+    for item in small_copies[:6]:
+        item.wait()
     recv, step, axis = recv_ref[...], *steps_of(send_ref[...], recv_ref[...])
     code = recv * 8 + jnp.where(step < 0, 4, 0) + axis
     code_row[0:96, :] = code
@@ -281,6 +293,8 @@
     lax.fori_loop(0, rounds, forward, 0)
     forward_sums(2 * rounds, z_b)
 
+    for item in small_copies[6:]:
+        item.wait()
     raw_ref[...] = jnp.zeros((RAW_ROWS, H), F32)
     w2nt = w2n_ref[...].T
     w1nt = w1n_ref[...].T
@@ -369,62 +383,22 @@
     grad_copy = pltpu.make_async_copy(grad.at[pl.ds(0, EDGES), :], grad_edge_hbm, sems.at[2])
     grad_copy.start()
 
-    w1bt = w1e_ref[H : 2 * H, :].T
-    w1ct = w1e_ref[2 * H :, :].T
-    diag_w2t[:, 0:H] = jnp.concatenate([w1bt, w1ct], axis=0)
-
-    def cells(i, carry):
-        rows = plane_rows(i)
-        here = sums[i + 1]
-        third = here[:, 2 * H :] - here[:, :H] - here[:, H : 2 * H]
-        arrived = here[:ROWS, 2 * H :] + here[ROWS:, 2 * H :]
-        yp, ym = here[:ROWS, H : 2 * H], here[ROWS:, H : 2 * H]
-        zp, zm = third[:ROWS], third[ROWS:]
-        left = (
-            sums[i, 0:ROWS, 0:H]
-            + sums[i + 2, ROWS : 2 * ROWS, 0:H]
-            + jnp.where(low_y, 0.0, pltpu.roll(yp, 4, 0))
-            + jnp.where(high_y, 0.0, pltpu.roll(ym, 124, 0))
-            + jnp.where(low_z, 0.0, pltpu.roll(zp, 1, 0))
-            + jnp.where(high_z, 0.0, pltpu.roll(zm, 127, 0))
-        ).astype(BF16)
-        arrived_low = arrived.astype(BF16)
-        leaving[pl.ds(Y_LOW + 4 * i, 4), :] = ym[:4]
-        leaving[pl.ds(Y_HIGH + 4 * i, 4), :] = yp[124:]
-        wide[0:ROWS, :] = zm
-        wide[ROWS:, :] = zp
-        leaving[pl.ds(Z_LOW + 32 * i, 32), :] = wide[pl.ds(0, 32, stride=4), :]
-        leaving[pl.ds(Z_HIGH + 32 * i, 32), :] = wide[pl.ds(ROWS + 3, 32, stride=4), :]
-        base_ref[rows, :] += dot(jnp.concatenate([left, arrived_low], axis=1), diag_w2t[:, 0:H])
-        both = dot_tn(node_ref[rows, :], jnp.concatenate([left, arrived_low], axis=1))
-        raw_ref[H : 2 * H, :] += both[:, :H]
-        raw_ref[2 * H : 3 * H, :] += both[:, H:]
-        raw_ref[896:897, :] += jnp.sum(arrived, axis=0, keepdims=True)
-        return carry
-
-    lax.fori_loop(0, PLANES, cells, 0)
-    leaving[X_LOW : X_LOW + ROWS, :] = sums[1, ROWS : 2 * ROWS, 0:H]
-    leaving[X_HIGH : X_HIGH + ROWS, :] = sums[PLANES, 0:ROWS, 0:H]
-    gone = leaving[...].astype(BF16)
-    out_ref[...] = dot(gone, w1bt).astype(BF16)
-    raw_ref[H : 2 * H, :] += dot_tn(face_ref[...], gone)
     grad_copy.wait()
 
 
-def local_terms(bounds, *operands):
+def local_terms(bounds, faces, columns, edge_rows, cot_rows, small):
     vmem = pl.BlockSpec(memory_space=pltpu.VMEM)
-    anywhere = pl.BlockSpec(memory_space=pltpu.MemorySpace.HBM)
+    hbm = pl.BlockSpec(memory_space=pltpu.MemorySpace.HBM)
     return pl.pallas_call(
         local_kernel,
         out_shape=(
             jax.ShapeDtypeStruct((EDGES, H), BF16),
-            jax.ShapeDtypeStruct((CELLS, H), F32),
-            jax.ShapeDtypeStruct((FACES, H), BF16),
-            jax.ShapeDtypeStruct((RAW_ROWS, H), F32),
+            pltpu.VMEM((CELLS, H), F32),
+            pltpu.VMEM((RAW_ROWS, H), F32),
+            pltpu.VMEM((PLANES + 2, 256, 3 * H), F32),
         ),
-        in_specs=[pl.BlockSpec(memory_space=pltpu.SMEM), vmem, vmem, anywhere, anywhere]
-        + [vmem] * 12,
-        out_specs=(anywhere, vmem, vmem, vmem),
+        in_specs=[pl.BlockSpec(memory_space=pltpu.SMEM)] + [vmem] * 3 + [hbm] * 13,
+        out_specs=(hbm, vmem, vmem, vmem),
         scratch_shapes=[pltpu.VMEM((PADDED, H), BF16)] * 5
         + [
             pltpu.VMEM((112, 128), jnp.int32),
@@ -432,11 +406,9 @@
             pltpu.VMEM((CELLS, H), F32),
             pltpu.VMEM((FACES, H), F32),
             pltpu.VMEM((2 * ROWS, H), F32),
-            pltpu.VMEM((FACES, H), F32),
             pltpu.VMEM((CELLS, 2 * H), F32),
             pltpu.VMEM((CELLS, H), F32),
             pltpu.VMEM((PLANES, 256, 3 * H), BF16),
-            pltpu.VMEM((PLANES + 2, 256, 3 * H), F32),
             pltpu.VMEM((256, 256), BF16),
             pltpu.VMEM((256, 256), BF16),
             pltpu.VMEM((256, 256), BF16),
@@ -447,12 +419,14 @@
             pltpu.SMEM((48,), jnp.int32),
             pltpu.SMEM((48,), jnp.int32),
             pltpu.SemaphoreType.DMA((3,)),
-        ],
+            pltpu.SemaphoreType.DMA((11,)),
+        ]
+        + [pltpu.VMEM(item.shape, item.dtype) for item in small],
         compiler_params=pltpu.CompilerParams(vmem_limit_bytes=LOCAL_VMEM),
         cost_estimate=pl.CostEstimate(
             flops=10_000_000_000, bytes_accessed=20_000_000, transcendentals=2_000_000
         ),
-    )(bounds, *operands)
+    )(bounds, faces, *columns, edge_rows, cot_rows, *small)
 
 
 def place():
@@ -489,21 +463,35 @@
 
 
 def halo_kernel(
-    node_ref,
-    send_ref,
-    recv_ref,
+    node_hbm,
+    send_hbm,
+    recv_hbm,
     face_ref,
     bounds_ref,
     key_col,
     kind_col,
+    node_ref,
+    send_ref,
+    recv_ref,
     cells,
     packed,
+    load_sems,
     send_sems,
     recv_sems,
 ):
+    loads = [
+        pltpu.make_async_copy(source, target, load_sems.at[k])
+        for k, (source, target) in enumerate(
+            ((node_hbm, node_ref), (send_hbm, send_ref), (recv_hbm, recv_ref))
+        )
+    ]
+    for item in loads:
+        item.start()
     barrier = pltpu.get_barrier_semaphore()
     for side in range(6):
         pl.semaphore_signal(barrier, inc=1, device_id=across(side), device_id_type=MESH)
+    for item in loads:
+        item.wait()
     cells[...] = node_ref[...].astype(F32)
     packed[X_LOW : X_LOW + ROWS, :] = node_ref[0:ROWS, :]
     packed[X_HIGH : X_HIGH + ROWS, :] = node_ref[CELLS - ROWS :, :]
@@ -550,15 +538,19 @@
     return pl.pallas_call(
         halo_kernel,
         out_shape=(
-            jax.ShapeDtypeStruct((FACES, H), BF16),
+            pltpu.VMEM((FACES, H), BF16),
             jax.ShapeDtypeStruct((PLANES + 1,), jnp.int32),
         )
         + (pltpu.VMEM((PADDED, 128), BF16),) * 2,
-        in_specs=[vmem] * 3,
+        in_specs=[pl.BlockSpec(memory_space=pltpu.MemorySpace.HBM)] * 3,
         out_specs=(vmem, pl.BlockSpec(memory_space=pltpu.SMEM)) + (vmem,) * 2,
         scratch_shapes=[
+            pltpu.VMEM((CELLS, H), BF16),
+            pltpu.VMEM((96, 128), jnp.int32),
+            pltpu.VMEM((96, 128), jnp.int32),
             pltpu.VMEM((CELLS, H), F32),
             pltpu.VMEM((FACES, H), BF16),
+            pltpu.SemaphoreType.DMA((3,)),
             pltpu.SemaphoreType.DMA((6,)),
             pltpu.SemaphoreType.DMA((6,)),
         ],
@@ -570,10 +562,20 @@
 
 def finish_kernel(
     base_ref,
-    out_ref,
-    raw_ref,
+    raw_in,
+    sums,
+    face_ref,
+    node_hbm,
+    w1e_hbm,
     grad_ref,
     total_ref,
+    node_ref,
+    w1e_ref,
+    raw_ref,
+    edge_raw,
+    leaving,
+    wide,
+    out_ref,
     faces,
     cells,
     partner_part,
@@ -587,6 +589,7 @@
     pair_recv,
     all_send,
     all_recv,
+    load_sems,
 ):
     (ga, gb, gc), (na, nb, nc) = place(), sizes()
     nz = nc // 2
@@ -612,6 +615,64 @@
     lax.fori_loop(1, chips, greet, 0)
     for side in (4, 5):
         pl.semaphore_signal(barrier, inc=1, device_id=across(side), device_id_type=MESH)
+
+    loads = [
+        pltpu.make_async_copy(node_hbm, node_ref, load_sems.at[0]),
+        pltpu.make_async_copy(w1e_hbm, w1e_ref, load_sems.at[1]),
+    ]
+    for item in loads:
+        item.start()
+    raw_ref[...] = raw_in[...]
+    edge_raw[...] = jnp.zeros_like(edge_raw)
+    for item in loads:
+        item.wait()
+
+    w1bt = w1e_ref[H : 2 * H, :].T
+    w1bct = jnp.concatenate([w1bt, w1e_ref[2 * H :, :].T], axis=0)
+    row_id = lax.broadcasted_iota(jnp.int32, (ROWS, H), 0)
+    low_z = lax.rem(row_id, 4) == 0
+    high_z = lax.rem(row_id, 4) == 3
+    low_y = row_id < 4
+    high_y = row_id >= 124
+
+    def collect(i, carry):
+        rows = pl.ds(pl.multiple_of(i * ROWS, ROWS), ROWS)
+        here = sums[i + 1]
+        third = here[:, 2 * H :] - here[:, :H] - here[:, H : 2 * H]
+        arrived = here[:ROWS, 2 * H :] + here[ROWS:, 2 * H :]
+        yp, ym = here[:ROWS, H : 2 * H], here[ROWS:, H : 2 * H]
+        zp, zm = third[:ROWS], third[ROWS:]
+        left = (
+            sums[i, 0:ROWS, 0:H]
+            + sums[i + 2, ROWS : 2 * ROWS, 0:H]
+            + jnp.where(low_y, 0.0, pltpu.roll(yp, 4, 0))
+            + jnp.where(high_y, 0.0, pltpu.roll(ym, 124, 0))
+            + jnp.where(low_z, 0.0, pltpu.roll(zp, 1, 0))
+            + jnp.where(high_z, 0.0, pltpu.roll(zm, 127, 0))
+        )
+        moved = jnp.concatenate([left, arrived], axis=1).astype(BF16)
+        leaving[pl.ds(Y_LOW + 4 * i, 4), :] = ym[:4]
+        leaving[pl.ds(Y_HIGH + 4 * i, 4), :] = yp[124:]
+        wide[0:ROWS, :] = zm
+        wide[ROWS:, :] = zp
+        leaving[pl.ds(Z_LOW + 32 * i, 32), :] = wide[pl.ds(0, 32, stride=4), :]
+        leaving[pl.ds(Z_HIGH + 32 * i, 32), :] = wide[pl.ds(ROWS + 3, 32, stride=4), :]
+        cells[rows, :] = base_ref[rows, :] + dot(moved, w1bct)
+        both = dot_tn(node_ref[rows, :], moved)
+        edge_raw[0:H, :] += both[:, :H]
+        edge_raw[H : 2 * H, :] += both[:, H:]
+        edge_raw[2 * H : 2 * H + 1, :] += jnp.sum(arrived, axis=0, keepdims=True)
+        return carry
+
+    lax.fori_loop(0, PLANES, collect, 0)
+    leaving[X_LOW : X_LOW + ROWS, :] = sums[1, ROWS : 2 * ROWS, 0:H]
+    leaving[X_HIGH : X_HIGH + ROWS, :] = sums[PLANES, 0:ROWS, 0:H]
+    gone = leaving[...].astype(BF16)
+    out_ref[...] = dot(gone, w1bt).astype(BF16)
+    edge_raw[0:H, :] += dot_tn(face_ref[...], gone)
+    block = raw_ref.shape[1]
+    raw_ref[H // block : 3 * H // block] = edge_raw[0 : 2 * H, :].reshape(2 * H // block, block, H)
+    raw_ref[896 // block, 896 % block : 896 % block + 1, :] = edge_raw[2 * H : 2 * H + 1, :]
     pl.semaphore_wait(barrier, chips + 2)
 
     def to_partner(source, target, k):
@@ -672,7 +733,6 @@
     full[core * chips + chip] = mine[...]
     for item in halos:
         item.wait()
-    cells[...] = base_ref[...]
     cells[0:ROWS, :] += faces[X_LOW : X_LOW + ROWS, :].astype(F32)
     cells[CELLS - ROWS :, :] += faces[X_HIGH : X_HIGH + ROWS, :].astype(F32)
     for start, at in ((Y_LOW, 0), (Y_HIGH, 124)):
@@ -726,7 +786,7 @@
     )(grad, total)
 
 
-def finish(base, out, raw):
+def finish(base, raw, sums, faces, node, w1_edge):
     chips = lax.axis_size("gx") * lax.axis_size("gy") * lax.axis_size("gz") // 2
     block = RAW_ROWS // (2 * chips)
     vmem = pl.BlockSpec(memory_space=pltpu.VMEM)
@@ -736,9 +796,16 @@
             jax.ShapeDtypeStruct((CELLS, H), BF16),
             jax.ShapeDtypeStruct((2 * chips, block, H), F32),
         ),
-        in_specs=[vmem] * 3,
+        in_specs=[vmem] * 4 + [pl.BlockSpec(memory_space=pltpu.MemorySpace.HBM)] * 2,
         out_specs=(vmem,) * 2,
         scratch_shapes=[
+            pltpu.VMEM((CELLS, H), BF16),
+            pltpu.VMEM((3 * H, H), BF16),
+            pltpu.VMEM((2 * chips, block, H), F32),
+            pltpu.VMEM((2 * H + 8, H), F32),
+            pltpu.VMEM((FACES, H), F32),
+            pltpu.VMEM((2 * ROWS, H), F32),
+            pltpu.VMEM((FACES, H), BF16),
             pltpu.VMEM((FACES, H), BF16),
             pltpu.VMEM((CELLS, H), F32),
             pltpu.VMEM((chips, block, H), F32),
@@ -752,11 +819,12 @@
             pltpu.SemaphoreType.DMA((2,)),
             pltpu.SemaphoreType.DMA((2,)),
             pltpu.SemaphoreType.DMA((2,)),
+            pltpu.SemaphoreType.DMA((2,)),
         ],
         compiler_params=pltpu.CompilerParams(
             collective_id=1, has_side_effects=True, vmem_limit_bytes=24 * 1024 * 1024
         ),
-    )(base, out, raw.reshape(2 * chips, block, H))
+    )(base, raw.reshape(2 * chips, block, H), sums, faces, node, w1_edge)
     return write(grad, total.reshape(RAW_ROWS, H))
 
 
@@ -775,29 +843,35 @@
     cot_node,
     cot_edge,
 ):
-    cells = node_latent.reshape(CELLS, H)
-    receiver_ids = receivers.reshape(96, 128)
-    sender_ids = senders.reshape(96, 128)
+    keep = functools.partial(
+        pltpu.with_memory_space_constraint, memory_space=pltpu.MemorySpace.HBM
+    )
+    cells = keep(node_latent.reshape(CELLS, H))
+    sender_ids = keep(senders.reshape(96, 128))
+    receiver_ids = keep(receivers.reshape(96, 128))
+    w1_edge = keep(w1_edge)
     faces, bounds, *columns = halo(cells, sender_ids, receiver_ids)
-    grad_edge, base, out, raw = local_terms(
+    grad_edge, base, raw, sums = local_terms(
         bounds,
-        sender_ids,
-        receiver_ids,
-        pltpu.with_memory_space_constraint(edge_latent.reshape(EDGES, H), pltpu.MemorySpace.HBM),
-        pltpu.with_memory_space_constraint(cot_edge.reshape(EDGES, H), pltpu.MemorySpace.HBM),
-        cells,
-        cot_node.reshape(CELLS, H),
         faces,
-        *columns,
-        w1_edge,
-        b1_edge.reshape(1, H),
-        w2_edge,
-        b2_edge.reshape(1, H),
-        w1_node,
-        b1_node.reshape(1, H),
-        w2_node,
+        columns,
+        keep(edge_latent.reshape(EDGES, H)),
+        keep(cot_edge.reshape(EDGES, H)),
+        (
+            receiver_ids,
+            sender_ids,
+            w1_edge,
+            keep(b1_edge.reshape(1, H)),
+            keep(w2_edge),
+            cells,
+            keep(cot_node.reshape(CELLS, H)),
+            keep(b2_edge.reshape(1, H)),
+            keep(w1_node),
+            keep(b1_node.reshape(1, H)),
+            keep(w2_node),
+        ),
     )
-    grad_node, *grads = finish(base, out, raw)
+    grad_node, *grads = finish(base, raw, sums, faces, cells, w1_edge)
     return (grad_node.reshape(node_latent.shape), grad_edge.reshape(edge_latent.shape), *grads)
 
 

time: 87.7 us -> 75.6 us (0.86)
  local copies, waits for them, and re-layouts: 11.5 us -> 0 us
    unnamed x28 -> x0, local copies, waits for them, and re-layouts: 11.5 us -> none
    pallas_call x1, Pallas kernels: 34.3 us -> 32.8 us  [local_terms(): pl.pallas_call(local_kernel, out_shape=(jax.ShapeDtypeStruct((EDGES, H),...]
    pallas_call x1, Pallas kernels: 26.7 us -> 28 us  [finish(): pl.pallas_call(finish_kernel, out_shape=(jax.ShapeDtypeStruct((CELLS, H),...]
where the time goes in v4:
time: 75.6 us; the launch traced here: 75.4 us
  Pallas kernels  74.8 us (99%)
    pallas_call x1, Pallas kernels, local_terms(): pl.pallas_call(local_kernel, out_shape=(jax.ShapeDtypeStruct((EDGES, H),...  32.8 us
    pallas_call x1, Pallas kernels, finish(): pl.pallas_call(finish_kernel, out_shape=(jax.ShapeDtypeStruct((CELLS, H),...  28 us
    pallas_call x1, Pallas kernels, halo(): pl.pallas_call(halo_kernel, out_shape=(pltpu.VMEM((FACES, H), BF16), jax....  12.9 us

profile of v4, /device:TPU:1, one launch (start us, length us, event | category | flops | bytes accessed | tf_op | source)
XLA Modules:
  0.0 75.4 jit_solution(11340396851691535740)
XLA Ops:
  0.6 12.9 %shard_map.180 = (bf16[1408,128]{1,0:T(8,128)(2,1)S(1)}, s32[17]{0:T(128)S(1)}, bf16[13184,128]{1,0:T(8,128)(2,1)S(1)}, bf16[13184,128]{1,0:T(8,128)(2,1)S(1)}) custom-call(bf16[2048,128]{1,0:T(8,128)(2,1)} %bitcast.15, s32[96,128]{1,0:T(8,128)} %bitcast.18, s32[96,128]{1,0:T(8,128)} %bitcast.20), custom_call_target="tpu_custom_call" | custom-call | tf_op jit(solution)/shard_map/pallas_call | solution.py:538
  13.6 32.8 %shard_map.181 = (bf16[12288,128]{1,0:T(8,128)(2,1)}, f32[2048,128]{1,0:T(8,128)S(1)}, f32[1024,128]{1,0:T(8,128)S(1)}, f32[18,256,384]{2,1,0:T(8,128)S(1)}) custom-call(s32[17]{0:T(128)S(1)} %get-tuple-element.23.bounds, bf16[1408,128]{1,0:T(8,128)(2,1)S(1)} %get-tuple-element.24.face_ref, bf16[13184,128]{1,0:T(8,128)(2,1)S(1)} %get-tuple-element.25.key_col, ...), custom_call_target="tpu_custom_call" | custom-call | flops 10000000000 | bytes 20000000 | tf_op jit(solution)/shard_map/pallas_call | solution.py:392
  46.3 28.0 %shard_map.182 = (bf16[2048,128]{1,0:T(8,128)(2,1)S(1)}, f32[128,8,128]{2,1,0:T(8,128)S(1)}) custom-call(f32[2048,128]{1,0:T(8,128)S(1)} %get-tuple-element.27.base_ref, f32[128,8,128]{2,1,0:T(8,128)S(1)} %bitcast.13, f32[18,256,384]{2,1,0:T(8,128)S(1)} %get-tuple-element.29.sums, bf16[1408,128]{1,0:T(8,128)(2,1)S(1)} %get-tuple-element.24.face_ref, ...), custom_call_target="tpu_custom_call" | custom-call | tf_op jit(solution)/shard_map/pallas_call | solution.py:793
  74.4 1.1 %shard_map.183 = (bf16[2048,128]{1,0:T(8,128)(2,1)}, f32[384,128]{1,0:T(8,128)}, f32[128,128]{1,0:T(8,128)}, f32[256,128]{1,0:T(8,128)}, f32[128,128]{1,0:T(8,128)}, /*index=5*/f32[4,128]{1,0:T(4,128)}) custom-call(bf16[2048,128]{1,0:T(8,128)(2,1)S(1)} %get-tuple-element.30.grad_ref, f32[1024,128]{1,0:T(8,128)S(1)} %bitcast.14), custom_call_target="tpu_custom_call" | custom-call | tf_op jit(solution)/shard_map/pallas_call | solution.py:778

commit v5 on v4

--- a/solution.py
+++ b/solution.py
@@ -16,6 +16,8 @@
 LOCAL_VMEM = 37 * 1024 * 1024
 PADDED = EDGES + TILE
 CHUNK = 512
+NODE_CHUNK = 1024
+PIECE = 1024
 RAW_ROWS = 1024
 X_LOW, X_HIGH, Y_LOW, Y_HIGH, Z_LOW, Z_HIGH, FACES = 0, 128, 256, 320, 384, 896, 1408
 SPANS = ((X_LOW, 128), (X_HIGH, 128), (Y_LOW, 64), (Y_HIGH, 64), (Z_LOW, 512), (Z_HIGH, 512))
@@ -143,8 +145,19 @@
     planes[0] = 0
     last = lax.fori_loop(0, PLANES, list_plane, 1)
     rounds = last // 2
-    starts[last] = EDGES
-    planes[last] = 0
+    for k in range(3):
+        starts[last + k] = EDGES
+        planes[last + k] = 0
+
+    def clear(i, carry):
+        sums[i] = jnp.zeros((256, 3 * H), F32)
+        return carry
+
+    lax.fori_loop(0, PLANES + 2, clear, 0)
+    gathered[...] = jnp.zeros((CELLS, 2 * H), F32)
+    degree[...] = jnp.zeros((CELLS, H), F32)
+    wide[...] = jnp.zeros((2 * ROWS, H), F32)
+    raw_ref[...] = jnp.zeros((RAW_ROWS, H), F32)
 
     for item in small_copies[:6]:
         item.wait()
@@ -163,7 +176,6 @@
     proj_face[...] = dot(face_ref[...], w1b)
     proj[0:ROWS, :] = proj_face[X_LOW : X_LOW + ROWS, :]
     proj[ROWS * (PLANES + 1) :, :] = proj_face[X_HIGH : X_HIGH + ROWS, :]
-    wide[...] = jnp.zeros((2 * ROWS, H), F32)
     w1bc = jnp.concatenate([w1b, w1c], axis=1)
 
     def project(k, carry):
@@ -171,8 +183,6 @@
         both = dot(node_ref[rows, :], w1bc)
         proj[pl.ds(pl.multiple_of(k * CHUNK + ROWS, ROWS), CHUNK), :] = both[:, :H]
         proj_own[rows, :] = both[:, H:] + b1e
-        gathered[rows, :] = jnp.zeros((CHUNK, 2 * H), F32)
-        degree[rows, :] = jnp.zeros((CHUNK, H), F32)
         return carry
 
     lax.fori_loop(0, CELLS // CHUNK, project, 0)
@@ -295,12 +305,11 @@
 
     for item in small_copies[6:]:
         item.wait()
-    raw_ref[...] = jnp.zeros((RAW_ROWS, H), F32)
     w2nt = w2n_ref[...].T
     w1nt = w1n_ref[...].T
 
     def nodes(k, carry):
-        rows = pl.ds(pl.multiple_of(k * CHUNK, CHUNK), CHUNK)
+        rows = pl.ds(pl.multiple_of(k * NODE_CHUNK, NODE_CHUNK), NODE_CHUNK)
         packed = gathered[rows, :]
         count = jnp.sum(degree[rows, :], axis=1, keepdims=True)
         aggregate = (
@@ -322,14 +331,9 @@
         raw_ref[899:900, :] += jnp.sum(cot_cells.astype(F32), axis=0, keepdims=True)
         return carry
 
-    lax.fori_loop(0, CELLS // CHUNK, nodes, 0)
+    lax.fori_loop(0, CELLS // NODE_CHUNK, nodes, 0)
     copies[1].wait()
 
-    def clear(i, carry):
-        sums[i] = jnp.zeros((256, 3 * H), F32)
-        return carry
-
-    lax.fori_loop(0, PLANES + 2, clear, 0)
     ones = jnp.ones((16, TILE), BF16)
 
     def backward_sums(j, d_buffer):
@@ -370,20 +374,33 @@
         new = d_wide + pair_dot(dz_edge, diag_w1t[...])
         grad[span, :] = keep_head(grad, start, new, head_inside(start, i)).astype(BF16)
 
+    def piece(c):
+        rows = pl.ds(pl.multiple_of(c * PIECE, PIECE), PIECE)
+        return pltpu.make_async_copy(grad.at[rows, :], grad_edge_hbm.at[rows, :], sems.at[2])
+
+    def send_pieces(done, final):
+        upto = final // PIECE
+
+        def send(c, carry):
+            piece(c).start()
+            return carry
+
+        lax.fori_loop(done, upto, send, 0)
+        return jnp.maximum(done, upto)
+
     def backward(m, carry):
         backward_values(2 * m + 1, d_a)
         backward_sums(2 * m, d_b)
         backward_values(2 * m + 2, d_b)
         backward_sums(2 * m + 1, d_a)
-        return carry
+        return send_pieces(carry, starts[2 * m + 3])
 
     d_b[...] = jnp.zeros((TILE, 2 * H), BF16)
-    lax.fori_loop(0, rounds, backward, 0)
+    sent = lax.fori_loop(0, rounds, backward, 0)
+    send_pieces(sent, EDGES)
     backward_sums(2 * rounds, d_b)
-    grad_copy = pltpu.make_async_copy(grad.at[pl.ds(0, EDGES), :], grad_edge_hbm, sems.at[2])
-    grad_copy.start()
-
-    grad_copy.wait()
+    whole = pltpu.make_async_copy(grad.at[pl.ds(0, EDGES), :], grad_edge_hbm, sems.at[2])
+    whole.wait()
 
 
 def local_terms(bounds, faces, columns, edge_rows, cot_rows, small):
@@ -598,21 +615,33 @@
     chip = (ga * nb + gb) * nz + chip_z
     partner = (ga, gb, 2 * chip_z + 1 - core)
 
+    spots = (
+        [lax.rem(ga + d, na) for d in range(na)],
+        [lax.rem(gb + d, nb) for d in range(nb)],
+        [lax.rem(chip_z + d, nz) for d in range(nz)],
+    )
+    rows_a = [spot * (nb * nz) for spot in spots[0]]
+    rows_b = [spot * nz for spot in spots[1]]
+    cores = [2 * spot + core for spot in spots[2]]
+
+    def hops(d):
+        da, db, dz = d
+        return min(da, na - da) + min(db, nb - db) // 2 + db % 2 + 2 * dz
+
+    offsets = sorted(
+        ((da, db, dz) for da in range(na) for db in range(nb) for dz in range(nz)),
+        key=lambda d: (-hops(d), d),
+    )[:-1]
+
     def peer(d):
-        da, rest = lax.div(d, nb * nz), lax.rem(d, nb * nz)
-        db, dz = lax.div(rest, nz), lax.rem(rest, nz)
-        pa, pb = lax.rem(ga + da, na), lax.rem(gb + db, nb)
-        pz = lax.rem(chip_z + dz, nz)
-        return (pa, pb, 2 * pz + core), (pa * nb + pb) * nz + pz
+        da, db, dz = d
+        where = (spots[0][da], spots[1][db], cores[dz])
+        return where, rows_a[da] + rows_b[db] + spots[2][dz]
 
     barrier = pltpu.get_barrier_semaphore()
-
-    def greet(d, carry):
+    for d in offsets:
         pl.semaphore_signal(barrier, inc=1, device_id=peer(d)[0], device_id_type=MESH)
-        return carry
-
     pl.semaphore_signal(barrier, inc=1, device_id=partner, device_id_type=MESH)
-    lax.fori_loop(1, chips, greet, 0)
     for side in (4, 5):
         pl.semaphore_signal(barrier, inc=1, device_id=across(side), device_id_type=MESH)
 
@@ -693,7 +722,7 @@
     first.wait()
     half[...] = raw_ref[pl.ds(core * chips, chips)] + partner_part[...]
 
-    def scatter(d, carry):
+    for d in offsets:
         where, other = peer(d)
         pltpu.make_async_remote_copy(
             src_ref=half.at[other],
@@ -703,11 +732,6 @@
             device_id=where,
             device_id_type=MESH,
         ).start()
-        return carry
-
-    lax.fori_loop(1, chips, scatter, 0)
-    for side in (4, 5):
-        halos[side].start()
     parts[chip] = half[chip]
 
     def settle(buffer, sem):
@@ -717,20 +741,23 @@
     settle(parts, all_recv.at[0])
     mine[...] = jnp.sum(parts[...], axis=0)
 
-    def gather(d, carry):
-        where, _ = peer(d)
+    slot = core * chips + chip
+    for d in offsets:
         pltpu.make_async_remote_copy(
             src_ref=mine,
-            dst_ref=full.at[core * chips + chip],
+            dst_ref=full.at[slot],
             send_sem=all_send.at[1],
             recv_sem=all_recv.at[1],
-            device_id=where,
+            device_id=peer(d)[0],
             device_id_type=MESH,
         ).start()
-        return carry
-
-    lax.fori_loop(1, chips, gather, 0)
-    full[core * chips + chip] = mine[...]
+    for side in (4, 5):
+        halos[side].start()
+    full[slot] = mine[...]
+    settle(full, all_recv.at[1])
+    held = pl.ds(core * chips, chips)
+    last = to_partner(full.at[held], full.at[held], 1)
+    last.start()
     for item in halos:
         item.wait()
     cells[0:ROWS, :] += faces[X_LOW : X_LOW + ROWS, :].astype(F32)
@@ -742,10 +769,6 @@
     cells[pl.ds(0, 512, stride=4), :] += faces[Z_LOW : Z_LOW + 512, :].astype(F32)
     cells[pl.ds(3, 512, stride=4), :] += faces[Z_HIGH : Z_HIGH + 512, :].astype(F32)
     grad_ref[...] = cells[...].astype(BF16)
-    settle(full, all_recv.at[1])
-    held = pl.ds(core * chips, chips)
-    last = to_partner(full.at[held], full.at[held], 1)
-    last.start()
     settle(half, all_send.at[0])
     settle(half, all_send.at[1])
     last.wait()

time: 75.6 us -> 70 us (0.926)
  Pallas kernels: 74.8 us -> 69.2 us
    pallas_call x1, Pallas kernels: 28 us -> 24.9 us  [finish(): pl.pallas_call(finish_kernel, out_shape=(jax.ShapeDtypeStruct((CELLS, H),...]
    pallas_call x1, Pallas kernels: 32.8 us -> 30.4 us  [local_terms(): pl.pallas_call(local_kernel, out_shape=(jax.ShapeDtypeStruct((EDGES, H),...]
where the time goes in v5:
time: 70 us; the launch traced here: 69.9 us
  Pallas kernels  69.2 us (99%)
    pallas_call x1, Pallas kernels, local_terms(): pl.pallas_call(local_kernel, out_shape=(jax.ShapeDtypeStruct((EDGES, H),...  30.4 us
    pallas_call x1, Pallas kernels, finish(): pl.pallas_call(finish_kernel, out_shape=(jax.ShapeDtypeStruct((CELLS, H),...  24.9 us
    pallas_call x1, Pallas kernels, halo(): pl.pallas_call(halo_kernel, out_shape=(pltpu.VMEM((FACES, H), BF16), jax....  12.9 us

profile of v5, /device:TPU:1, one launch (start us, length us, event | category | flops | bytes accessed | tf_op | source)
XLA Modules:
  0.0 69.9 jit_solution(8788739142795110835)
XLA Ops:
  0.6 12.9 %shard_map.180 = (bf16[1408,128]{1,0:T(8,128)(2,1)S(1)}, s32[17]{0:T(128)S(1)}, bf16[13184,128]{1,0:T(8,128)(2,1)S(1)}, bf16[13184,128]{1,0:T(8,128)(2,1)S(1)}) custom-call(bf16[2048,128]{1,0:T(8,128)(2,1)} %bitcast.15, s32[96,128]{1,0:T(8,128)} %bitcast.18, s32[96,128]{1,0:T(8,128)} %bitcast.20), custom_call_target="tpu_custom_call" | custom-call | tf_op jit(solution)/shard_map/pallas_call | solution.py:555
  13.6 30.4 %shard_map.181 = (bf16[12288,128]{1,0:T(8,128)(2,1)}, f32[2048,128]{1,0:T(8,128)S(1)}, f32[1024,128]{1,0:T(8,128)S(1)}, f32[18,256,384]{2,1,0:T(8,128)S(1)}) custom-call(s32[17]{0:T(128)S(1)} %get-tuple-element.23.bounds, bf16[1408,128]{1,0:T(8,128)(2,1)S(1)} %get-tuple-element.24.face_ref, bf16[13184,128]{1,0:T(8,128)(2,1)S(1)} %get-tuple-element.25.key_col, ...), custom_call_target="tpu_custom_call" | custom-call | flops 10000000000 | bytes 20000000 | tf_op jit(solution)/shard_map/pallas_call | solution.py:409
  43.9 24.9 %shard_map.182 = (bf16[2048,128]{1,0:T(8,128)(2,1)S(1)}, f32[128,8,128]{2,1,0:T(8,128)S(1)}) custom-call(f32[2048,128]{1,0:T(8,128)S(1)} %get-tuple-element.27.base_ref, f32[128,8,128]{2,1,0:T(8,128)S(1)} %bitcast.13, f32[18,256,384]{2,1,0:T(8,128)S(1)} %get-tuple-element.29.sums, bf16[1408,128]{1,0:T(8,128)(2,1)S(1)} %get-tuple-element.24.face_ref, ...), custom_call_target="tpu_custom_call" | custom-call | tf_op jit(solution)/shard_map/pallas_call | solution.py:816
  68.8 1.1 %shard_map.183 = (bf16[2048,128]{1,0:T(8,128)(2,1)}, f32[384,128]{1,0:T(8,128)}, f32[128,128]{1,0:T(8,128)}, f32[256,128]{1,0:T(8,128)}, f32[128,128]{1,0:T(8,128)}, /*index=5*/f32[4,128]{1,0:T(4,128)}) custom-call(bf16[2048,128]{1,0:T(8,128)(2,1)S(1)} %get-tuple-element.30.grad_ref, f32[1024,128]{1,0:T(8,128)S(1)} %bitcast.14), custom_call_target="tpu_custom_call" | custom-call | tf_op jit(solution)/shard_map/pallas_call | solution.py:801

commit v6 on v5

--- a/solution.py
+++ b/solution.py
@@ -13,11 +13,12 @@
 CELLS = PLANES * ROWS
 EDGES = 12288
 TILE = 896
-LOCAL_VMEM = 37 * 1024 * 1024
+LOCAL_VMEM = 26 * 1024 * 1024
 PADDED = EDGES + TILE
 CHUNK = 512
 NODE_CHUNK = 1024
 PIECE = 1024
+DENSE = 2048
 RAW_ROWS = 1024
 X_LOW, X_HIGH, Y_LOW, Y_HIGH, Z_LOW, Z_HIGH, FACES = 0, 128, 256, 320, 384, 896, 1408
 SPANS = ((X_LOW, 128), (X_HIGH, 128), (Y_LOW, 64), (Y_HIGH, 64), (Z_LOW, 512), (Z_HIGH, 512))
@@ -76,8 +77,9 @@
         raw_ref,
         sums,
         edge,
+        value,
+        dz_all,
         cot,
-        value,
         slope,
         grad,
         code_row,
@@ -99,8 +101,8 @@
         planes,
         sems,
         small_sems,
-    ) = refs[:28]
-    small = refs[28:]
+    ) = refs[:29]
+    small = refs[29:]
     (
         recv_ref,
         send_ref,
@@ -259,6 +261,12 @@
         old = ref[pl.ds(start, 16), :].astype(F32)
         return jnp.concatenate([jnp.where(inside, new[:16], old), new[16:]], axis=0)
 
+    def keep_rows(ref, start, new, inside):
+        head = pl.ds(start, 16)
+        old = ref[head, :].astype(F32)
+        ref[head, :] = jnp.where(inside, new[:16].astype(F32), old).astype(BF16)
+        ref[pl.ds(pl.multiple_of(start + 16, 16), TILE - 16), :] = new[16:]
+
     copies[0].wait()
 
     def forward_sums(j, z_buffer):
@@ -325,6 +333,8 @@
         dx_node = dot(dz_node, w1nt)
         base_ref[rows, :] = cot_cells.astype(F32) + dx_node[:, :H]
         gathered[rows, 0:H] = dx_node[:, H:]
+        raw_ref[384:512, :] += dot_tn(packed[:, H:].astype(BF16), dx_node[:, H:].astype(BF16))
+        raw_ref[897:898, :] += jnp.sum(count * dx_node[:, H:], axis=0, keepdims=True)
         raw_ref[512:768, :] += dot_tn(x_node, dz_node)
         raw_ref[768:896, :] += dot_tn(u_node.astype(BF16), cot_cells)
         raw_ref[898:899, :] += jnp.sum(dz_node.astype(F32), axis=0, keepdims=True)
@@ -334,17 +344,9 @@
     lax.fori_loop(0, CELLS // NODE_CHUNK, nodes, 0)
     copies[1].wait()
 
-    ones = jnp.ones((16, TILE), BF16)
-
     def backward_sums(j, d_buffer):
         start, span, i = tile_at(j)
-        dz_edge = d_buffer[:, :H]
-        both = dot(
-            jnp.concatenate([edge[span, :].T, value[span, :].T, ones], axis=0), d_buffer[...]
-        )
-        raw_ref[0:H, :] += both[:H, :H]
-        raw_ref[384:512, :] += both[H : 2 * H, H:]
-        raw_ref[897:898, :] += both[2 * H : 2 * H + 1, H:]
+        dz_edge = d_buffer[...]
         codes = row_codes(start)
         keys = (codes >> 3) - 128 * i + ((codes >> 2) & 1) * 128
         keys = jnp.where((codes >> 10) == i, keys, -1)
@@ -363,16 +365,17 @@
 
     def backward_values(j, d_buffer):
         start, span, i = tile_at(j)
-        keys, kind = key_col[span, :], kind_col[span, :]
+        keys = key_col[span, :]
         hot = jnp.where((keys == lane_low) | (keys == lane_high), one, zero)
         added = pair_dot(hot, block_diagonal(gathered[plane_rows(i), 0:H].astype(BF16)))
         d_wide = cot[span, :].astype(F32) + added
-        low, _, high = (number.astype(BF16) for number in kinds(i, 3))
-        d_edge = jnp.where((kind >= low) & (kind <= high), d_wide.astype(BF16), zero)
+        d_edge = d_wide.astype(BF16)
+        inside = head_inside(start, i)
         dz_edge = (pair_dot(d_edge, diag_w2t[...]) * slope[span, :].astype(F32)).astype(BF16)
-        d_buffer[...] = jnp.concatenate([dz_edge, d_edge], axis=1)
+        d_buffer[...] = dz_edge
+        keep_rows(dz_all, start, dz_edge, inside)
         new = d_wide + pair_dot(dz_edge, diag_w1t[...])
-        grad[span, :] = keep_head(grad, start, new, head_inside(start, i)).astype(BF16)
+        grad[span, :] = keep_head(grad, start, new, inside).astype(BF16)
 
     def piece(c):
         rows = pl.ds(pl.multiple_of(c * PIECE, PIECE), PIECE)
@@ -395,7 +398,7 @@
         backward_sums(2 * m + 1, d_a)
         return send_pieces(carry, starts[2 * m + 3])
 
-    d_b[...] = jnp.zeros((TILE, 2 * H), BF16)
+    d_b[...] = jnp.zeros((TILE, H), BF16)
     sent = lax.fori_loop(0, rounds, backward, 0)
     send_pieces(sent, EDGES)
     backward_sums(2 * rounds, d_b)
@@ -413,10 +416,11 @@
             pltpu.VMEM((CELLS, H), F32),
             pltpu.VMEM((RAW_ROWS, H), F32),
             pltpu.VMEM((PLANES + 2, 256, 3 * H), F32),
-        ),
+        )
+        + (pltpu.VMEM((PADDED, H), BF16),) * 4,
         in_specs=[pl.BlockSpec(memory_space=pltpu.SMEM)] + [vmem] * 3 + [hbm] * 13,
-        out_specs=(hbm, vmem, vmem, vmem),
-        scratch_shapes=[pltpu.VMEM((PADDED, H), BF16)] * 5
+        out_specs=(hbm,) + (vmem,) * 7,
+        scratch_shapes=[pltpu.VMEM((PADDED, H), BF16)] * 2
         + [
             pltpu.VMEM((112, 128), jnp.int32),
             pltpu.VMEM((CELLS + 2 * ROWS, H), F32),
@@ -431,8 +435,8 @@
             pltpu.VMEM((256, 256), BF16),
             pltpu.VMEM((TILE, H), F32),
             pltpu.VMEM((TILE, H), F32),
-            pltpu.VMEM((TILE, 2 * H), BF16),
-            pltpu.VMEM((TILE, 2 * H), BF16),
+            pltpu.VMEM((TILE, H), BF16),
+            pltpu.VMEM((TILE, H), BF16),
             pltpu.SMEM((48,), jnp.int32),
             pltpu.SMEM((48,), jnp.int32),
             pltpu.SemaphoreType.DMA((3,)),
@@ -582,6 +586,10 @@
     raw_in,
     sums,
     face_ref,
+    edge,
+    value,
+    dz_all,
+    cot,
     node_hbm,
     w1e_hbm,
     grad_ref,
@@ -590,6 +598,7 @@
     w1e_ref,
     raw_ref,
     edge_raw,
+    dense_raw,
     leaving,
     wide,
     out_ref,
@@ -702,6 +711,23 @@
     block = raw_ref.shape[1]
     raw_ref[H // block : 3 * H // block] = edge_raw[0 : 2 * H, :].reshape(2 * H // block, block, H)
     raw_ref[896 // block, 896 % block : 896 % block + 1, :] = edge_raw[2 * H : 2 * H + 1, :]
+
+    dense_raw[...] = jnp.zeros_like(dense_raw)
+    ones = jnp.ones((16, DENSE), BF16)
+
+    def dense(k, carry):
+        rows = pl.ds(pl.multiple_of(k * DENSE, DENSE), DENSE)
+        dense_raw[...] += dot(
+            jnp.concatenate([edge[rows, :].T, value[rows, :].T, ones], axis=0),
+            jnp.concatenate([dz_all[rows, :], cot[rows, :]], axis=1),
+        )
+        return carry
+
+    lax.fori_loop(0, EDGES // DENSE, dense, 0)
+    per = H // block
+    raw_ref[0:per] = dense_raw[0:H, :H].reshape(per, block, H)
+    raw_ref[3 * per : 4 * per] += dense_raw[H : 2 * H, H:].reshape(per, block, H)
+    raw_ref[897 // block, 897 % block : 897 % block + 1, :] += dense_raw[2 * H : 2 * H + 1, H:]
     pl.semaphore_wait(barrier, chips + 2)
 
     def to_partner(source, target, k):
@@ -809,7 +835,7 @@
     )(grad, total)
 
 
-def finish(base, raw, sums, faces, node, w1_edge):
+def finish(base, raw, sums, faces, slots, node, w1_edge):
     chips = lax.axis_size("gx") * lax.axis_size("gy") * lax.axis_size("gz") // 2
     block = RAW_ROWS // (2 * chips)
     vmem = pl.BlockSpec(memory_space=pltpu.VMEM)
@@ -819,13 +845,14 @@
             jax.ShapeDtypeStruct((CELLS, H), BF16),
             jax.ShapeDtypeStruct((2 * chips, block, H), F32),
         ),
-        in_specs=[vmem] * 4 + [pl.BlockSpec(memory_space=pltpu.MemorySpace.HBM)] * 2,
+        in_specs=[vmem] * 8 + [pl.BlockSpec(memory_space=pltpu.MemorySpace.HBM)] * 2,
         out_specs=(vmem,) * 2,
         scratch_shapes=[
             pltpu.VMEM((CELLS, H), BF16),
             pltpu.VMEM((3 * H, H), BF16),
             pltpu.VMEM((2 * chips, block, H), F32),
             pltpu.VMEM((2 * H + 8, H), F32),
+            pltpu.VMEM((2 * H + 16, 2 * H), F32),
             pltpu.VMEM((FACES, H), F32),
             pltpu.VMEM((2 * ROWS, H), F32),
             pltpu.VMEM((FACES, H), BF16),
@@ -847,7 +874,7 @@
         compiler_params=pltpu.CompilerParams(
             collective_id=1, has_side_effects=True, vmem_limit_bytes=24 * 1024 * 1024
         ),
-    )(base, raw.reshape(2 * chips, block, H), sums, faces, node, w1_edge)
+    )(base, raw.reshape(2 * chips, block, H), sums, faces, *slots, node, w1_edge)
     return write(grad, total.reshape(RAW_ROWS, H))
 
 
@@ -874,7 +901,7 @@
     receiver_ids = keep(receivers.reshape(96, 128))
     w1_edge = keep(w1_edge)
     faces, bounds, *columns = halo(cells, sender_ids, receiver_ids)
-    grad_edge, base, raw, sums = local_terms(
+    grad_edge, base, raw, sums, *slots = local_terms(
         bounds,
         faces,
         columns,
@@ -894,7 +921,7 @@
             keep(w2_node),
         ),
     )
-    grad_node, *grads = finish(base, raw, sums, faces, cells, w1_edge)
+    grad_node, *grads = finish(base, raw, sums, faces, slots, cells, w1_edge)
     return (grad_node.reshape(node_latent.shape), grad_edge.reshape(edge_latent.shape), *grads)
 
 

time: 70 us -> 71.1 us (1.016); the launches traced: 69.9 us -> 70.2 us
    pallas_call x1, Pallas kernels: 24.9 us -> 27.2 us  [finish(): pl.pallas_call(finish_kernel, out_shape=(jax.ShapeDtypeStruct((CELLS, H),...]
    pallas_call x1, Pallas kernels: 30.4 us -> 28.3 us  [local_terms(): pl.pallas_call(local_kernel, out_shape=(jax.ShapeDtypeStruct((EDGES, H),...]
where the time goes in v6:
time: 71.1 us; the launch traced here: 70.2 us
  Pallas kernels  69.5 us (98%)
    pallas_call x1, Pallas kernels, local_terms(): pl.pallas_call(local_kernel, out_shape=(jax.ShapeDtypeStruct((EDGES, H),...  28.3 us
    pallas_call x1, Pallas kernels, finish(): pl.pallas_call(finish_kernel, out_shape=(jax.ShapeDtypeStruct((CELLS, H),...  27.2 us
    pallas_call x1, Pallas kernels, halo(): pl.pallas_call(halo_kernel, out_shape=(pltpu.VMEM((FACES, H), BF16), jax....  12.9 us

profile of v6, /device:TPU:1, one launch (start us, length us, event | category | flops | bytes accessed | tf_op | source)
XLA Modules:
  0.0 70.2 jit_solution(2570986997329796754)
XLA Ops:
  0.6 12.9 %shard_map.180 = (bf16[1408,128]{1,0:T(8,128)(2,1)S(1)}, s32[17]{0:T(128)S(1)}, bf16[13184,128]{1,0:T(8,128)(2,1)S(1)}, bf16[13184,128]{1,0:T(8,128)(2,1)S(1)}) custom-call(bf16[2048,128]{1,0:T(8,128)(2,1)} %bitcast.15, s32[96,128]{1,0:T(8,128)} %bitcast.18, s32[96,128]{1,0:T(8,128)} %bitcast.20), custom_call_target="tpu_custom_call" | custom-call | tf_op jit(solution)/shard_map/pallas_call | solution.py:559
  13.6 28.3 %shard_map.181 = (bf16[12288,128]{1,0:T(8,128)(2,1)}, f32[2048,128]{1,0:T(8,128)S(1)}, f32[1024,128]{1,0:T(8,128)S(1)}, f32[18,256,384]{2,1,0:T(8,128)S(1)}, bf1...) custom-call(s32[17]{0:T(128)S(1)} %get-tuple-element.27.bounds, ...), custom_call_target="tpu_custom_call" | custom-call | flops 10000000000 | bytes 20000000 | tf_op jit(solution)/shard_map/pallas_call | solution.py:412
  41.8 27.2 %shard_map.182 = (bf16[2048,128]{1,0:T(8,128)(2,1)S(1)}, f32[128,8,128]{2,1,0:T(8,128)S(1)}) custom-call(f32[2048,128]{1,0:T(8,128)S(1)} %get-tuple-element.31.base_ref, f32[128,8,128]{2,1,0:T(8,128)S(1)} %bitcast.13, f32[18,256,384]{2,1,0:T(8,128)S(1)} %get-tuple-element.33.sums, bf16[1408,128]{1,0:T(8,128)(2,1)S(1)} %get-tuple-element.28.face_ref, ...), custom_call_target="tpu_custom_call" | custom-call | tf_op jit(solution)/shard_map/pallas_call | solution.py:842
  69.1 1.1 %shard_map.183 = (bf16[2048,128]{1,0:T(8,128)(2,1)}, f32[384,128]{1,0:T(8,128)}, f32[128,128]{1,0:T(8,128)}, f32[256,128]{1,0:T(8,128)}, f32[128,128]{1,0:T(8,128)}, /*index=5*/f32[4,128]{1,0:T(4,128)}) custom-call(bf16[2048,128]{1,0:T(8,128)(2,1)S(1)} %get-tuple-element.38.grad_ref, f32[1024,128]{1,0:T(8,128)S(1)} %bitcast.14), custom_call_target="tpu_custom_call" | custom-call | tf_op jit(solution)/shard_map/pallas_call | solution.py:827

commit v7 on v6

--- a/solution.py
+++ b/solution.py
@@ -16,9 +16,10 @@
 LOCAL_VMEM = 26 * 1024 * 1024
 PADDED = EDGES + TILE
 CHUNK = 512
-NODE_CHUNK = 1024
+NODE_CHUNK = 2048
 PIECE = 1024
-DENSE = 2048
+PROJECT = 2048
+DENSE = 4096
 RAW_ROWS = 1024
 X_LOW, X_HIGH, Y_LOW, Y_HIGH, Z_LOW, Z_HIGH, FACES = 0, 128, 256, 320, 384, 896, 1408
 SPANS = ((X_LOW, 128), (X_HIGH, 128), (Y_LOW, 64), (Y_HIGH, 64), (Z_LOW, 512), (Z_HIGH, 512))
@@ -181,13 +182,13 @@
     w1bc = jnp.concatenate([w1b, w1c], axis=1)
 
     def project(k, carry):
-        rows = pl.ds(pl.multiple_of(k * CHUNK, CHUNK), CHUNK)
+        rows = pl.ds(pl.multiple_of(k * PROJECT, PROJECT), PROJECT)
         both = dot(node_ref[rows, :], w1bc)
-        proj[pl.ds(pl.multiple_of(k * CHUNK + ROWS, ROWS), CHUNK), :] = both[:, :H]
+        proj[pl.ds(pl.multiple_of(k * PROJECT + ROWS, ROWS), PROJECT), :] = both[:, :H]
         proj_own[rows, :] = both[:, H:] + b1e
         return carry
 
-    lax.fori_loop(0, CELLS // CHUNK, project, 0)
+    lax.fori_loop(0, CELLS // PROJECT, project, 0)
 
     row_id = lax.broadcasted_iota(jnp.int32, (ROWS, H), 0)
     low_z = (row_id & 3) == 0
@@ -600,6 +601,7 @@
     edge_raw,
     dense_raw,
     leaving,
+    moved,
     wide,
     out_ref,
     faces,
@@ -688,15 +690,15 @@
             + jnp.where(low_z, 0.0, pltpu.roll(zp, 1, 0))
             + jnp.where(high_z, 0.0, pltpu.roll(zm, 127, 0))
         )
-        moved = jnp.concatenate([left, arrived], axis=1).astype(BF16)
+        both_ways = jnp.concatenate([left, arrived], axis=1).astype(BF16)
+        moved[rows, :] = both_ways
         leaving[pl.ds(Y_LOW + 4 * i, 4), :] = ym[:4]
         leaving[pl.ds(Y_HIGH + 4 * i, 4), :] = yp[124:]
         wide[0:ROWS, :] = zm
         wide[ROWS:, :] = zp
         leaving[pl.ds(Z_LOW + 32 * i, 32), :] = wide[pl.ds(0, 32, stride=4), :]
         leaving[pl.ds(Z_HIGH + 32 * i, 32), :] = wide[pl.ds(ROWS + 3, 32, stride=4), :]
-        cells[rows, :] = base_ref[rows, :] + dot(moved, w1bct)
-        both = dot_tn(node_ref[rows, :], moved)
+        both = dot_tn(node_ref[rows, :], both_ways)
         edge_raw[0:H, :] += both[:, :H]
         edge_raw[H : 2 * H, :] += both[:, H:]
         edge_raw[2 * H : 2 * H + 1, :] += jnp.sum(arrived, axis=0, keepdims=True)
@@ -705,9 +707,7 @@
     lax.fori_loop(0, PLANES, collect, 0)
     leaving[X_LOW : X_LOW + ROWS, :] = sums[1, ROWS : 2 * ROWS, 0:H]
     leaving[X_HIGH : X_HIGH + ROWS, :] = sums[PLANES, 0:ROWS, 0:H]
-    gone = leaving[...].astype(BF16)
-    out_ref[...] = dot(gone, w1bt).astype(BF16)
-    edge_raw[0:H, :] += dot_tn(face_ref[...], gone)
+    edge_raw[0:H, :] += dot_tn(face_ref[...], leaving[...].astype(BF16))
     block = raw_ref.shape[1]
     raw_ref[H // block : 3 * H // block] = edge_raw[0 : 2 * H, :].reshape(2 * H // block, block, H)
     raw_ref[896 // block, 896 % block : 896 % block + 1, :] = edge_raw[2 * H : 2 * H + 1, :]
@@ -742,9 +742,6 @@
 
     first = to_partner(raw_ref.at[pl.ds((1 - core) * chips, chips)], partner_part, 0)
     first.start()
-    halos = face_copies(out_ref, faces, send_sems, recv_sems)
-    for side in (0, 1, 2, 3):
-        halos[side].start()
     first.wait()
     half[...] = raw_ref[pl.ds(core * chips, chips)] + partner_part[...]
 
@@ -759,6 +756,18 @@
             device_id_type=MESH,
         ).start()
     parts[chip] = half[chip]
+
+    out_ref[...] = dot(leaving[...].astype(BF16), w1bt).astype(BF16)
+    halos = face_copies(out_ref, faces, send_sems, recv_sems)
+    for side in (0, 1, 2, 3):
+        halos[side].start()
+
+    def combine(k, carry):
+        rows = pl.ds(pl.multiple_of(k * CHUNK, CHUNK), CHUNK)
+        cells[rows, :] = base_ref[rows, :] + dot(moved[rows, :], w1bct)
+        return carry
+
+    lax.fori_loop(0, CELLS // CHUNK, combine, 0)
 
     def settle(buffer, sem):
         span = buffer.at[pl.ds(0, chips - 1)]
@@ -854,6 +863,7 @@
             pltpu.VMEM((2 * H + 8, H), F32),
             pltpu.VMEM((2 * H + 16, 2 * H), F32),
             pltpu.VMEM((FACES, H), F32),
+            pltpu.VMEM((CELLS, 2 * H), BF16),
             pltpu.VMEM((2 * ROWS, H), F32),
             pltpu.VMEM((FACES, H), BF16),
             pltpu.VMEM((FACES, H), BF16),

time: 71.1 us -> 68.5 us (0.963); the launches traced: 70.2 us -> 68.3 us
  Pallas kernels: 69.5 us -> 67.7 us
    pallas_call x1, Pallas kernels: 28.3 us -> 27.3 us  [local_terms(): pl.pallas_call(local_kernel, out_shape=(jax.ShapeDtypeStruct((EDGES, H),...]
    pallas_call x1, Pallas kernels: 27.2 us -> 26.4 us  [finish(): pl.pallas_call(finish_kernel, out_shape=(jax.ShapeDtypeStruct((CELLS, H),...]
where the time goes in v7:
time: 68.5 us; the launch traced here: 68.3 us
  Pallas kernels  67.7 us (99%)
    pallas_call x1, Pallas kernels, local_terms(): pl.pallas_call(local_kernel, out_shape=(jax.ShapeDtypeStruct((EDGES, H),...  27.3 us
    pallas_call x1, Pallas kernels, finish(): pl.pallas_call(finish_kernel, out_shape=(jax.ShapeDtypeStruct((CELLS, H),...  26.4 us
    pallas_call x1, Pallas kernels, halo(): pl.pallas_call(halo_kernel, out_shape=(pltpu.VMEM((FACES, H), BF16), jax....  12.9 us

profile of v7, /device:TPU:1, one launch (start us, length us, event | category | flops | bytes accessed | tf_op | source)
XLA Modules:
  0.0 68.3 jit_solution(6178838238905848019)
XLA Ops:
  0.6 12.9 %shard_map.180 = (bf16[1408,128]{1,0:T(8,128)(2,1)S(1)}, s32[17]{0:T(128)S(1)}, bf16[13184,128]{1,0:T(8,128)(2,1)S(1)}, bf16[13184,128]{1,0:T(8,128)(2,1)S(1)}) custom-call(bf16[2048,128]{1,0:T(8,128)(2,1)} %bitcast.15, s32[96,128]{1,0:T(8,128)} %bitcast.18, s32[96,128]{1,0:T(8,128)} %bitcast.20), custom_call_target="tpu_custom_call" | custom-call | tf_op jit(solution)/shard_map/pallas_call | solution.py:560
  13.6 27.3 %shard_map.181 = (bf16[12288,128]{1,0:T(8,128)(2,1)}, f32[2048,128]{1,0:T(8,128)S(1)}, f32[1024,128]{1,0:T(8,128)S(1)}, f32[18,256,384]{2,1,0:T(8,128)S(1)}, bf1...) custom-call(s32[17]{0:T(128)S(1)} %get-tuple-element.27.bounds, ...), custom_call_target="tpu_custom_call" | custom-call | flops 10000000000 | bytes 20000000 | tf_op jit(solution)/shard_map/pallas_call | solution.py:413
  40.9 26.4 %shard_map.182 = (bf16[2048,128]{1,0:T(8,128)(2,1)S(1)}, f32[128,8,128]{2,1,0:T(8,128)S(1)}) custom-call(f32[2048,128]{1,0:T(8,128)S(1)} %get-tuple-element.31.base_ref, f32[128,8,128]{2,1,0:T(8,128)S(1)} %bitcast.13, f32[18,256,384]{2,1,0:T(8,128)S(1)} %get-tuple-element.33.sums, bf16[1408,128]{1,0:T(8,128)(2,1)S(1)} %get-tuple-element.28.face_ref, ...), custom_call_target="tpu_custom_call" | custom-call | tf_op jit(solution)/shard_map/pallas_call | solution.py:851
  67.2 1.1 %shard_map.183 = (bf16[2048,128]{1,0:T(8,128)(2,1)}, f32[384,128]{1,0:T(8,128)}, f32[128,128]{1,0:T(8,128)}, f32[256,128]{1,0:T(8,128)}, f32[128,128]{1,0:T(8,128)}, /*index=5*/f32[4,128]{1,0:T(4,128)}) custom-call(bf16[2048,128]{1,0:T(8,128)(2,1)S(1)} %get-tuple-element.38.grad_ref, f32[1024,128]{1,0:T(8,128)S(1)} %bitcast.14), custom_call_target="tpu_custom_call" | custom-call | tf_op jit(solution)/shard_map/pallas_call | solution.py:836

commit v8 on v7

--- a/solution.py
+++ b/solution.py
@@ -704,7 +704,12 @@
         edge_raw[2 * H : 2 * H + 1, :] += jnp.sum(arrived, axis=0, keepdims=True)
         return carry
 
-    lax.fori_loop(0, PLANES, collect, 0)
+    def collect_four(k, carry):
+        for step in range(4):
+            carry = collect(4 * k + step, carry)
+        return carry
+
+    lax.fori_loop(0, PLANES // 4, collect_four, 0)
     leaving[X_LOW : X_LOW + ROWS, :] = sums[1, ROWS : 2 * ROWS, 0:H]
     leaving[X_HIGH : X_HIGH + ROWS, :] = sums[PLANES, 0:ROWS, 0:H]
     edge_raw[0:H, :] += dot_tn(face_ref[...], leaving[...].astype(BF16))

time: 68.5 us -> 67 us (0.978)
  Pallas kernels: 67.7 us -> 66.2 us
    pallas_call x1, Pallas kernels: 26.4 us -> 24.9 us  [finish(): pl.pallas_call(finish_kernel, out_shape=(jax.ShapeDtypeStruct((CELLS, H),...]
where the time goes in v8:
time: 67 us; the launch traced here: 66.8 us
  Pallas kernels  66.2 us (99%)
    pallas_call x1, Pallas kernels, local_terms(): pl.pallas_call(local_kernel, out_shape=(jax.ShapeDtypeStruct((EDGES, H),...  27.3 us
    pallas_call x1, Pallas kernels, finish(): pl.pallas_call(finish_kernel, out_shape=(jax.ShapeDtypeStruct((CELLS, H),...  24.9 us
    pallas_call x1, Pallas kernels, halo(): pl.pallas_call(halo_kernel, out_shape=(pltpu.VMEM((FACES, H), BF16), jax....  12.9 us

profile of v8, /device:TPU:1, one launch (start us, length us, event | category | flops | bytes accessed | tf_op | source)
XLA Modules:
  0.0 66.8 jit_solution(13867934874042445561)
XLA Ops:
  0.6 12.9 %shard_map.180 = (bf16[1408,128]{1,0:T(8,128)(2,1)S(1)}, s32[17]{0:T(128)S(1)}, bf16[13184,128]{1,0:T(8,128)(2,1)S(1)}, bf16[13184,128]{1,0:T(8,128)(2,1)S(1)}) custom-call(bf16[2048,128]{1,0:T(8,128)(2,1)} %bitcast.15, s32[96,128]{1,0:T(8,128)} %bitcast.18, s32[96,128]{1,0:T(8,128)} %bitcast.20), custom_call_target="tpu_custom_call" | custom-call | tf_op jit(solution)/shard_map/pallas_call | solution.py:560
  13.6 27.3 %shard_map.181 = (bf16[12288,128]{1,0:T(8,128)(2,1)}, f32[2048,128]{1,0:T(8,128)S(1)}, f32[1024,128]{1,0:T(8,128)S(1)}, f32[18,256,384]{2,1,0:T(8,128)S(1)}, bf1...) custom-call(s32[17]{0:T(128)S(1)} %get-tuple-element.27.bounds, ...), custom_call_target="tpu_custom_call" | custom-call | flops 10000000000 | bytes 20000000 | tf_op jit(solution)/shard_map/pallas_call | solution.py:413
  40.9 24.9 %shard_map.182 = (bf16[2048,128]{1,0:T(8,128)(2,1)S(1)}, f32[128,8,128]{2,1,0:T(8,128)S(1)}) custom-call(f32[2048,128]{1,0:T(8,128)S(1)} %get-tuple-element.31.base_ref, f32[128,8,128]{2,1,0:T(8,128)S(1)} %bitcast.13, f32[18,256,384]{2,1,0:T(8,128)S(1)} %get-tuple-element.33.sums, bf16[1408,128]{1,0:T(8,128)(2,1)S(1)} %get-tuple-element.28.face_ref, ...), custom_call_target="tpu_custom_call" | custom-call | tf_op jit(solution)/shard_map/pallas_call | solution.py:856
  65.8 1.1 %shard_map.183 = (bf16[2048,128]{1,0:T(8,128)(2,1)}, f32[384,128]{1,0:T(8,128)}, f32[128,128]{1,0:T(8,128)}, f32[256,128]{1,0:T(8,128)}, f32[128,128]{1,0:T(8,128)}, /*index=5*/f32[4,128]{1,0:T(4,128)}) custom-call(bf16[2048,128]{1,0:T(8,128)(2,1)S(1)} %get-tuple-element.38.grad_ref, f32[1024,128]{1,0:T(8,128)S(1)} %bitcast.14), custom_call_target="tpu_custom_call" | custom-call | tf_op jit(solution)/shard_map/pallas_call | solution.py:841
